TPU v7x, 32 devices: a whole 2x2x4 slice. The times are simulated.
32 devices in a mesh: owner: 4 (over x, core), rows: 8 (over z, y).
Axes of the slice: x: 2, y: 2, z: 4, core: 2. Of those that a mesh axis runs over, the one named last changes fastest.
Arguments:
- master_gate: float32 [64, 2048, 1408], P('owner', 'rows'), may hold values from -0.1875 to 0.1875
- master_up: float32 [64, 2048, 1408], P('owner', 'rows'), may hold values from -0.1875 to 0.1875
- router_weight: float32 [2048, 64], P('rows', 'owner'), may hold values from -0.125 to 0.125
- router_gain: float32 [2048], P('rows'), may hold values from 0.25 to 1.75
Outputs:
- final_gate: bfloat16 [64, 2048, 1408], P('owner', None, 'rows')
- final_up: bfloat16 [64, 2048, 1408], P('owner', None, 'rows')
- scale_gate: float32 [64, 1408], P('owner', 'rows')
- scale_up: float32 [64, 1408], P('owner', 'rows')
- serve_router: bfloat16 [2048, 64], replicated
All inputs are finite; a program needn't handle non-finite values. Where the computation divides by a largest or mean magnitude, that divisor is 1e-20 or more.
Results may differ from a plain program's by a relative error of at most 0.001.
Values may be sent and summed in bfloat16 or wider, within the bound.
No kernel may reach another device: no remote copies, remote signals or barrier semaphores. Data moves between devices by JAX's collectives and lax.ppermute only.
A program may use at most 192 MiB of HBM per device.

v0:
```python
import jax
import jax.numpy as jnp
from jax import lax
from jax.sharding import PartitionSpec as P


def shards(master_gate, master_up, router_weight, router_gain):
    scale_gate, scale_up = lax.pmax(
        (jnp.max(jnp.abs(master_gate), axis=1), jnp.max(jnp.abs(master_up), axis=1)), "rows"
    )
    narrow_gate, narrow_up = (
        (master_gate / jnp.expand_dims(scale_gate, 1)).astype(jnp.bfloat16),
        (master_up / jnp.expand_dims(scale_up, 1)).astype(jnp.bfloat16),
    )
    final_gate, final_up = (
        lax.all_to_all(narrow_gate, "rows", split_axis=2, concat_axis=1, tiled=True),
        lax.all_to_all(narrow_up, "rows", split_axis=2, concat_axis=1, tiled=True),
    )
    scale_gate = lax.dynamic_slice_in_dim(
        scale_gate, lax.axis_index("rows") * final_gate.shape[2], final_gate.shape[2], axis=1
    )
    scale_up = lax.dynamic_slice_in_dim(
        scale_up, lax.axis_index("rows") * final_up.shape[2], final_up.shape[2], axis=1
    )
    part_router = (router_weight * router_gain[:, None]).astype(jnp.bfloat16)
    row_router = lax.all_gather(part_router, "rows", axis=0, tiled=True)
    serve_router = lax.all_gather(row_router, "owner", axis=1, tiled=True)
    return (final_gate, final_up, scale_gate, scale_up, serve_router)


def solution(mesh):
    return jax.shard_map(
        shards,
        mesh=mesh,
        in_specs=(
            P("owner", "rows", None),
            P("owner", "rows", None),
            P("rows", "owner"),
            P("rows"),
        ),
        out_specs=(
            P("owner", None, "rows"),
            P("owner", None, "rows"),
            P("owner", "rows"),
            P("owner", "rows"),
            P(),
        ),
        check_vma=False,
    )
```

profile of v0, /device:TPU:0, one launch (start us, length us, event | category | flops | bytes accessed | tf_op | source)
XLA Modules:
  0.0 714.9 jit_solution(11512561346431727942)
XLA Ops:
  7.2 0.0 all-reduce.3.cloned.1.call-start
  7.2 0.0 copy-start
  7.2 9.7 %abs_reduce_fusion = f32[16,1408]{1,0:T(8,128)} fusion(f32[16,256,1408]{2,1,0:T(8,128)} %param.5), kind=kLoop, calls=%fused_computation.1 | loop fusion | flops 11511808 | bytes 23158784 | tf_op jit(solution)/shard_map/reduce_max | solution.py:9
  16.9 4.5 copy-done
  21.4 2.4 abs_reduce_fusion.1
  23.8 0.0 all-reduce.3.cloned.1.call-update
  23.8 23.7 %copy.18 = f32[16,256,1408]{1,0,2:T(8,128)} copy(f32[16,256,1408]{2,1,0:T(8,128)} %param.4) | data formatting | bytes 46137344 | tf_op args[0]
  47.5 50.1 %all-reduce.3.cloned.1.call-done = (f32[16,1408]{1,0:T(8,128)}, f32[16,1408]{1,0:T(8,128)}) async-done(((f32[16,1408]{1,0:T(8,128)}, f32[16,1408]{1,0:T(8,128)}), (f32[16,1408]{1,0:T(8,128)}, f32[16,1408]{1,0:T(8,128)})) %all-reduce.3.cloned.1.call-update) | async-done | bytes 180240 | tf_op jit(solution)/shard_map/pmax | solution.py:8
  97.6 1.1 copy.17
  98.8 14.2 %divide_convert_fusion.1 = bf16[16,256,1408]{1,0,2:T(8,128)(2,1)} fusion(f32[16,256,1408]{1,0,2:T(8,128)} %copy.18, f32[16,1408]{0,1:T(8,128)S(1)} %copy.17), kind=kLoop, calls=%fused_computation.2 | loop fusion | flops 11534336 | bytes 34693120 | tf_op jit(solution)/shard_map/convert_element_type | solution.py:12
  113.0 5.2 all-to-all-start
  118.3 0.0 copy-start.1
  118.3 23.7 %copy.22 = f32[16,256,1408]{1,0,2:T(8,128)} copy(f32[16,256,1408]{2,1,0:T(8,128)} %param.5) | data formatting | bytes 46137344 | tf_op args[1]
  142.0 0.0 copy-done.1
  142.0 0.3 copy.21
  142.3 0.0 copy-start.2
  142.3 0.0 copy-start.3
  142.3 14.2 %divide_convert_fusion = bf16[16,256,1408]{1,0,2:T(8,128)(2,1)} fusion(f32[16,256,1408]{1,0,2:T(8,128)} %copy.22, f32[16,1408]{0,1:T(8,128)S(1)} %copy.21), kind=kLoop, calls=%fused_computation | loop fusion | flops 11534336 | bytes 34693120 | tf_op jit(solution)/shard_map/convert_element_type | solution.py:13
  156.5 210.6 %all-to-all-done = bf16[16,256,1408]{1,0,2:T(8,128)(2,1)} async-done(((bf16[16,256,1408]{1,0,2:T(8,128)(2,1)}), bf16[16,256,1408]{1,0,2:T(8,128)(2,1)}, u32[]{:S(2)}, u32[]{:S(2)}) %all-to-all-start) | async-done | bytes 11534368 | tf_op jit(solution)/shard_map/all_to_all | solution.py:16
  367.1 5.3 all-to-all-start.1
  372.3 0.0 copy-done.2
  372.3 0.0 copy-done.3
  372.4 269.1 %all_gather.6 = bf16[2048,16]{0,1:T(8,128)(2,1)S(1)} all-gather(bf16[256,16]{0,1:T(8,128)(2,1)S(1)} %multiply_convert_fusion), channel_id=1, replica_groups=mesh['owner'=4,'rows'=8] {'rows'}, dimensions={0}, use_global_device_ids=true | all-gather | bytes 73728 | tf_op jit(solution)/shard_map/all_gather | solution.py:26
  641.5 5.8 all_gather.7
  647.3 1.4 constant_dynamic-slice_fusion
  648.7 11.3 %copy.20 = bf16[16,8,256,176]{2,1,3,0:T(8,128)(2,1)} copy(bf16[16,8,256,176]{2,0,3,1:T(8,128)(2,1)} %bitcast.2) | data formatting | bytes 23068672 | tf_op jit(solution)/shard_map/all_to_all | solution.py:16
  660.0 18.0 %all_to_all.29 = bf16[16,2048,176]{1,2,0:T(8,128)(2,1)} reshape(bf16[16,8,256,176]{2,1,3,0:T(8,128)(2,1)} %copy.20) | data formatting | bytes 23068672 | tf_op jit(solution)/shard_map/all_to_all | solution.py:16
  678.0 0.0 all-to-all-done.1
  678.0 11.4 %copy.24 = bf16[16,8,256,176]{2,1,3,0:T(8,128)(2,1)} copy(bf16[16,8,256,176]{2,0,3,1:T(8,128)(2,1)} %bitcast.5) | data formatting | bytes 23068672 | tf_op jit(solution)/shard_map/all_to_all | solution.py:17
  689.4 18.0 %all_to_all.33 = bf16[16,2048,176]{1,2,0:T(8,128)(2,1)} reshape(bf16[16,8,256,176]{2,1,3,0:T(8,128)(2,1)} %copy.24) | data formatting | bytes 23068672 | tf_op jit(solution)/shard_map/all_to_all | solution.py:17
  707.3 0.7 copy.30
  (1 shorter events, 0.0 us)
Async XLA Ops:
  7.2 90.5 %all-reduce.3.cloned.1.call-start = ((), (), s32[]{:S(2)}) async-start(), calls=%async_computation.2 | async-start | bytes 360448 | tf_op jit(solution)/shard_map/pmax | solution.py:8
  7.2 14.2 %copy-start = (f32[16,256,1408]{2,1,0:T(8,128)S(1)}, f32[16,256,1408]{2,1,0:T(8,128)}, u32[]{:S(2)}) copy-start(f32[16,256,1408]{2,1,0:T(8,128)} %param.4) | copy-start | bytes 69206016
  113.0 254.0 %all-to-all-start = ((bf16[16,256,1408]{1,0,2:T(8,128)(2,1)}), bf16[16,256,1408]{1,0,2:T(8,128)(2,1)}, u32[]{:S(2)}, u32[]{:S(2)}) async-start(bf16[16,256,1408]{1,0,2:T(8,128)(2,1)} %divide_convert_fusion.1), calls=%async_computation | async-start | bytes 23068672 | tf_op jit(solution)/shard_map/all_to_all | solution.py:16
  118.3 23.7 %copy-start.1 = (f32[16,1408]{1,0:T(8,128)S(1)}, f32[16,1408]{1,0:T(8,128)}, u32[]{:S(2)}) copy-start(f32[16,1408]{1,0:T(8,128)} %get-tuple-element.6) | copy-start | bytes 270340
  142.3 230.1 %copy-start.2 = (f32[256,16]{0,1:T(8,128)S(1)}, f32[256,16]{0,1:T(8,128)}, u32[]{:S(2)}) copy-start(f32[256,16]{0,1:T(8,128)} %param.6) | copy-start | bytes 49156
  142.3 230.1 %copy-start.3 = (f32[256]{0:T(256)S(1)}, f32[256]{0:T(256)}, u32[]{:S(2)}) copy-start(f32[256]{0:T(256)} %param.7) | copy-start | bytes 3076
  367.1 310.9 %all-to-all-start.1 = ((bf16[16,256,1408]{1,0,2:T(8,128)(2,1)}), bf16[16,256,1408]{1,0,2:T(8,128)(2,1)}, u32[]{:S(2)}, u32[]{:S(2)}) async-start(bf16[16,256,1408]{1,0,2:T(8,128)(2,1)} %divide_convert_fusion), calls=%async_computation.1 | async-start | bytes 23068672 | tf_op jit(solution)/shard_map/all_to_all | solution.py:17
Sparse Core Ops, SparseCore 0:
  24.0 73.6 all-reduce.2
where the time goes:
time: 717 us; the launch traced here: 715 us
  blocking collectives  275 us (38%)
  waiting for transfers between devices  261 us (36%)
  local copies, waits for them, and re-layouts  114 us (16%)
  other arithmetic  40.5 us (6%)
  between operations  14.1 us (2%)
  starting transfers between devices  10.5 us (1%)
    all_gather x1, blocking collectives, shards(): row_router = lax.all_gather(part_router, 'rows', axis=0, tiled=True)  269 us
    all_to_all x1, waiting for transfers between devices, shards(): lax.all_to_all(narrow_gate, 'rows', split_axis=2, concat_axis=1, tiled=True)  211 us
    unnamed x11, local copies, waits for them, and re-layouts  52.6 us
    pmax x1, waiting for transfers between devices, shards(): lax.pmax((jnp.max(jnp.abs(master_gate), axis=1), jnp.max(jnp.abs(master_u...  50.1 us
    all_to_all x2, local copies, waits for them, and re-layouts, shards(): lax.all_to_all(narrow_up, 'rows', split_axis=2, concat_axis=1, tiled=True)  29.3 us
    all_to_all x2, local copies, waits for them, and re-layouts, shards(): lax.all_to_all(narrow_gate, 'rows', split_axis=2, concat_axis=1, tiled=True)  29.3 us
  transfers between devices with their start and end apart: 3, of which 2 were waited for; matrix products, arithmetic and copies ran while one was open for 10% of the time, Pallas kernels for 0%

commit v1 on v0

v1 whole, which is shorter than its diff:
```python
import functools

import jax
import jax.numpy as jnp
from jax import lax
from jax.experimental import pallas as pl
from jax.experimental.pallas import tpu as pltpu
from jax.sharding import PartitionSpec as P


SPAN = 252.0
LN2 = 0.6931471805599453
TINY = 1e-30


def plain_shards(master_gate, master_up, router_weight, router_gain):
    scale_gate, scale_up = lax.pmax(
        (jnp.max(jnp.abs(master_gate), axis=1), jnp.max(jnp.abs(master_up), axis=1)), "rows"
    )
    finals, scales = [], []
    for master, scale in ((master_gate, scale_gate), (master_up, scale_up)):
        narrow = (master / jnp.expand_dims(scale, 1)).astype(jnp.bfloat16)
        final = lax.all_to_all(narrow, "rows", split_axis=2, concat_axis=1, tiled=True)
        width = final.shape[2]
        finals.append(final)
        scales.append(lax.dynamic_slice_in_dim(scale, lax.axis_index("rows") * width, width, axis=1))
    part_router = (router_weight * router_gain[:, None]).astype(jnp.bfloat16)
    row_router = lax.all_gather(part_router, "rows", axis=0, tiled=True)
    serve_router = lax.all_gather(row_router, "owner", axis=1, tiled=True)
    return (*finals, *scales, serve_router)


def pack_body(n, me_ref, x_ref, *refs):
    pieces, top_ref, turned = refs[:n], refs[n], refs[n + 1]
    depth = turned.shape[0]
    width = depth // n
    for c in range(depth // 128):
        cols = slice(128 * c, 128 * (c + 1))
        x = x_ref[0, :, cols]
        size = jnp.abs(x)
        top = jnp.max(size, axis=0, keepdims=True)
        top_ref[0, :, cols] = top
        root = jnp.sqrt(size * (1.0 / jnp.maximum(top, TINY)))
        code = jnp.exp((SPAN * LN2) * root - (SPAN * LN2 / 2))
        code = jnp.where(x < 0, -code, code)
        turned[cols, :] = code.T.astype(jnp.bfloat16)
    for k in range(n):
        to = lax.rem(me_ref[0] + k, n)
        pieces[k][0] = turned[pl.ds(pl.multiple_of(to * width, width), width), :]


def pack(me, master, first, count, n):
    _, rows, depth = master.shape
    width = depth // n
    return pl.pallas_call(
        functools.partial(pack_body, n),
        grid_spec=pltpu.PrefetchScalarGridSpec(
            num_scalar_prefetch=1,
            grid=(count,),
            in_specs=[pl.BlockSpec((1, rows, depth), lambda e, me: (first + e, 0, 0))],
            out_specs=[pl.BlockSpec((1, width, rows), lambda e, me: (e, 0, 0))] * n
            + [pl.BlockSpec((1, 1, depth), lambda e, me: (e, 0, 0))],
            scratch_shapes=[pltpu.VMEM((depth, rows), jnp.bfloat16)],
        ),
        out_shape=[jax.ShapeDtypeStruct((count, width, rows), jnp.bfloat16)] * n
        + [jax.ShapeDtypeStruct((count, 1, depth), jnp.float32)],
        cost_estimate=pl.CostEstimate(
            flops=count * rows * depth * 40, bytes_accessed=count * rows * depth * 6, transcendentals=0
        ),
    )(me, master)


def unpack_body(n, me_ref, ratio_ref, *refs):
    pieces, out = refs[:n], refs[-1]
    width, rows = pieces[0].shape[1:]
    step = 16

    def some_rows(i, _):
        part = pl.ds(pl.multiple_of(i * step, step), step)
        ratio = ratio_ref[0, part, :]
        for k in range(n):
            code = pieces[k][0, part, :].astype(jnp.float32)
            root = jnp.log(jnp.abs(code)) * (1.0 / (SPAN * LN2)) + 0.5
            value = root * root * ratio[:, k : k + 1]
            value = jnp.where(code < 0, -value, value).astype(jnp.bfloat16)
            source = lax.rem(me_ref[0] + (n - k), n)
            out[0, part, pl.ds(pl.multiple_of(source * rows, rows), rows)] = value
        return 0

    lax.fori_loop(0, width // step, some_rows, 0)


def unpack(me, ratio, pieces, whole, first, shape):
    n = len(pieces)
    count, width, rows = pieces[0].shape
    operands = [ratio, *pieces] + ([] if whole is None else [whole])
    return pl.pallas_call(
        functools.partial(unpack_body, n),
        grid_spec=pltpu.PrefetchScalarGridSpec(
            num_scalar_prefetch=1,
            grid=(count,),
            in_specs=[pl.BlockSpec((1, width, n), lambda e, me: (first + e, 0, 0))]
            + [pl.BlockSpec((1, width, rows), lambda e, me: (e, 0, 0))] * n
            + ([] if whole is None else [pl.BlockSpec(memory_space=pl.ANY)]),
            out_specs=pl.BlockSpec((1, width, n * rows), lambda e, me: (first + e, 0, 0)),
        ),
        out_shape=jax.ShapeDtypeStruct(shape, jnp.bfloat16),
        input_output_aliases={} if whole is None else {n + 2: 0},
        cost_estimate=pl.CostEstimate(
            flops=count * rows * width * n * 30, bytes_accessed=count * rows * width * n * 4, transcendentals=0
        ),
    )(me, *operands)


def plan(experts):
    small = max(1, experts // 8)
    return (
        (0, 0, small),
        (0, small, experts - small),
        (1, 0, experts - small),
        (1, experts - small, small),
    )


def join_body(n, me_ref, *refs):
    out, rows = refs[n], refs[0].shape[1]
    for k in range(n):
        source = lax.rem(me_ref[0] + (n - k), n)
        out[:, pl.ds(pl.multiple_of(source * rows, rows), rows)] = refs[k][...]


def join(me, pieces):
    n = len(pieces)
    columns, rows = pieces[0].shape
    return pl.pallas_call(
        functools.partial(join_body, n),
        in_specs=[pl.BlockSpec(memory_space=pltpu.SMEM)] + [pl.BlockSpec(memory_space=pltpu.VMEM)] * n,
        out_specs=pl.BlockSpec(memory_space=pltpu.VMEM),
        out_shape=jax.ShapeDtypeStruct((columns, n * rows), jnp.bfloat16),
        name="join",
    )(me, *pieces)


def send_order(n):
    return sorted(range(1, n), key=lambda k: abs(2 * k - n))


def fast_shards(n, masters, router_weight, router_gain):
    me = lax.axis_index("rows")
    here = jnp.reshape(me, (1,)).astype(jnp.int32)
    experts, rows, depth = masters[0].shape
    width = depth // n
    turns = [[(r, (r + k) % n) for r in range(n)] for k in range(n)]

    def send(pieces):
        came = list(pieces)
        for k in send_order(n):
            came[k] = lax.ppermute(pieces[k], "rows", turns[k])
        return came

    chunks = plan(experts)
    packed, tops = [], [[], []]
    for a, first, count in chunks:
        *pieces, top = pack(here, masters[a], first, count, n)
        packed.append(pieces)
        tops[a].append(top[:, 0, :])
    came = [send(pieces) for pieces in packed]

    top = jnp.concatenate(tops[0] + tops[1], axis=0)
    top = lax.dynamic_slice_in_dim(jnp.concatenate([top, top], axis=1), me * width, depth, axis=1)
    all_tops = send([top[:, k * width : (k + 1) * width] for k in range(n)])
    scale = functools.reduce(jnp.maximum, all_tops)
    ratio = jnp.stack(all_tops, axis=-1) / scale[:, :, None]
    ratios = (ratio[:experts], ratio[experts:])

    wholes = [None, None]
    for c, (a, first, count) in enumerate(chunks):
        wholes[a] = unpack(here, ratios[a], came[c], wholes[a], first, (experts, width, n * rows))
    finals = [jnp.swapaxes(whole, 1, 2) for whole in wholes]

    part_router = (router_weight * router_gain[:, None]).astype(jnp.bfloat16).T
    routers = join(here, send([part_router] * n))
    serve_router = lax.all_gather(routers, "owner", axis=0, tiled=True).T
    return (*finals, scale[:experts], scale[experts:], serve_router)


def shards(n, master_gate, master_up, router_weight, router_gain):
    experts, rows, depth = master_gate.shape
    if fits(n, experts, rows, depth):
        return fast_shards(n, (master_gate, master_up), router_weight, router_gain)
    return plain_shards(master_gate, master_up, router_weight, router_gain)


def fits(n, experts, rows, depth):
    return n > 1 and experts > 1 and rows % 128 == 0 and depth % (16 * n) == 0 and depth % 128 == 0


def solution(mesh):
    n = mesh.shape["rows"]
    step = placed(mesh, n)

    return step


def placed(mesh, n):
    return jax.shard_map(
        functools.partial(shards, n),
        mesh=mesh,
        in_specs=(
            P("owner", "rows", None),
            P("owner", "rows", None),
            P("rows", "owner"),
            P("rows"),
        ),
        out_specs=(
            P("owner", None, "rows"),
            P("owner", None, "rows"),
            P("owner", "rows"),
            P("owner", "rows"),
            P(),
        ),
        check_vma=False,
    )
```

time: 717 us -> 687 us (0.958)
  the two profiles are of different devices: /device:TPU:0 before, /device:TPU:17 now
where the time goes in v1:
time: 687 us; the launch traced here: 684 us
  starting transfers between devices  396 us (58%)
  waiting for transfers between devices  134 us (20%)
  Pallas kernels  99.4 us (14%)
  local copies, waits for them, and re-layouts  41.3 us (6%)
    ppermute x42, starting transfers between devices, send(): came[k] = lax.ppermute(pieces[k], 'rows', turns[k])  396 us
    ppermute x42, waiting for transfers between devices, send(): came[k] = lax.ppermute(pieces[k], 'rows', turns[k])  134 us
    pallas_call x4, Pallas kernels, pack(): pl.pallas_call(functools.partial(pack_body, n), grid_spec=pltpu.PrefetchS...  50.6 us
    pallas_call x4, Pallas kernels, unpack(): pl.pallas_call(functools.partial(unpack_body, n), grid_spec=pltpu.Prefetc...  47.3 us
    another operation x9, local copies, waits for them, and re-layouts, fast_shards(): ratio = jnp.stack(all_tops, axis=-1) / scale[:, :, None]  34.8 us
  transfers between devices with their start and end apart: 42, of which 14 were waited for; matrix products, arithmetic and copies ran while one was open for 6% of the time, Pallas kernels for 12%

profile of v1, /device:TPU:17, one launch (start us, length us, event | category | flops | bytes accessed | tf_op | source)
XLA Modules:
  0.0 683.6 jit_solution(7750004092456281143)
XLA Ops:
  1.4 1.2 collective-permute-start.35
  2.6 1.3 collective-permute-start.36
  3.9 0.9 collective-permute-start.37
  4.8 4.4 shard_map.86
  9.5 1.3 collective-permute-start.22
  10.8 20.9 %shard_map.85 = (bf16[14,176,256]{2,1,0:T(8,128)(2,1)}, bf16[14,176,256]{2,1,0:T(8,128)(2,1)}, bf16[14,176,256]{2,1,0:T(8,128)(2,1)}, bf16[14,176,256]{2,1,0:T(8...) custom-call(s32[1]{0:T(128)} %bitcast.me_ref, ...), custom_call_target="tpu_custom_call" | custom-call | flops 201850880 | bytes 30277632 | tf_op jit(solution)/shard_map/pallas_call | solution.py:55
  31.7 20.9 %shard_map.84 = (bf16[14,176,256]{2,1,0:T(8,128)(2,1)}, bf16[14,176,256]{2,1,0:T(8,128)(2,1)}, bf16[14,176,256]{2,1,0:T(8,128)(2,1)}, bf16[14,176,256]{2,1,0:T(8...) custom-call(s32[1]{0:T(128)} %bitcast.me_ref, ...), custom_call_target="tpu_custom_call" | custom-call | flops 201850880 | bytes 30277632 | tf_op jit(solution)/shard_map/pallas_call | solution.py:55
  52.7 4.5 shard_map.83
  57.3 0.8 copy.103
  58.5 2.2 collective-permute-start
  60.8 3.3 collective-permute-start.39
  64.9 2.3 collective-permute-start.41
  67.8 1.4 collective-permute-start.1
  69.8 2.6 collective-permute-start.2
  72.4 1.9 collective-permute-start.4
  74.4 1.2 collective-permute-start.5
  76.2 2.0 collective-permute-start.6
  78.9 1.0 collective-permute-start.23
  81.3 2.6 collective-permute-start.25
  83.9 1.0 collective-permute-start.26
  85.5 2.7 collective-permute-start.14
  88.2 4.7 collective-permute-done.24.refs_4_
  92.8 12.3 %collective-permute-start.28 = (bf16[14,176,256]{2,1,0:T(8,128)(2,1)}, bf16[14,176,256]{2,1,0:T(8,128)(2,1)}, u32[]{:S(2)}, u32[]{:S(2)}) collective-permute-start(bf16[14,176,256]{2,1,0:T(8,128)(2,1)} %get-tuple-element.70), channel_id=1, source_target_pairs={{0,1},{1,2},{2,3},{3,4},{4,5},{5,6},{6,7},{7,0},{8,9},{9,10},{10,1... | collective-permute-start | bytes 3784712 | tf_op jit(solution)/shard_map/ppermute | solution.py:158
  105.1 3.0 collective-permute-start.29
  108.8 1.6 collective-permute-start.31
  110.5 1.0 collective-permute-start.15
  111.5 68.4 %collective-permute-done.15.refs_2_ = bf16[2,176,256]{2,1,0:T(8,128)(2,1)S(1)} collective-permute-done((bf16[2,176,256]{2,1,0:T(8,128)(2,1)}, bf16[2,176,256]{2,1,0:T(8,128)(2,1)S(1)}, u32[]{:S(2)}, u32[]{:S(2)}) %collective-permute-start.15) | collective-permute-done | bytes 180256 | tf_op jit(solution)/shard_map/ppermute | solution.py:158
  179.9 25.3 %collective-permute-start.16 = (bf16[2,176,256]{2,1,0:T(8,128)(2,1)}, bf16[2,176,256]{2,1,0:T(8,128)(2,1)S(1)}, u32[]{:S(2)}, u32[]{:S(2)}) collective-permute-start(bf16[2,176,256]{2,1,0:T(8,128)(2,1)} %get-tuple-element.56), channel_id=1, source_target_pairs={{0,3},{1,4},{2,5},{3,6},{4,7},{5,0},{6,1},{7,2},{8,11},{9,12},{10,... | collective-permute-start | bytes 540680 | tf_op jit(solution)/shard_map/ppermute | solution.py:158
  205.2 5.7 collective-permute-done.16.refs_3_
  210.9 72.9 %collective-permute-start.17 = (bf16[2,176,256]{2,1,0:T(8,128)(2,1)}, bf16[2,176,256]{2,1,0:T(8,128)(2,1)S(1)}, u32[]{:S(2)}, u32[]{:S(2)}) collective-permute-start(bf16[2,176,256]{2,1,0:T(8,128)(2,1)} %get-tuple-element.57), channel_id=1, source_target_pairs={{0,4},{1,5},{2,6},{3,7},{4,0},{5,1},{6,2},{7,3},{8,12},{9,13},{10,... | collective-permute-start | bytes 540680 | tf_op jit(solution)/shard_map/ppermute | solution.py:158
  283.8 3.8 collective-permute-done.17.refs_4_
  287.6 1.6 collective-permute-start.18
  289.2 4.2 collective-permute-done.18.refs_5_
  293.4 1.8 collective-permute-start.19
  295.2 3.6 collective-permute-done.19.refs_6_
  298.8 1.9 collective-permute-start.20
  300.8 4.7 collective-permute-done.20.refs_7_
  305.5 4.4 collective-permute-start.32
  309.9 2.9 collective-permute-start.33
  312.7 1.0 collective-permute-start.10
  313.8 2.6 collective-permute-start.11
  316.4 1.4 join.1
  317.9 37.6 %collective-permute-done.32.refs_5_ = bf16[14,176,256]{2,1,0:T(8,128)(2,1)} collective-permute-done((bf16[14,176,256]{2,1,0:T(8,128)(2,1)}, bf16[14,176,256]{2,1,0:T(8,128)(2,1)}, u32[]{:S(2)}, u32[]{:S(2)}) %collective-permute-start.32) | collective-permute-done | bytes 1261600 | tf_op jit(solution)/shard_map/ppermute | solution.py:158
  355.5 148.3 %collective-permute-start.12 = (bf16[14,176,256]{2,1,0:T(8,128)(2,1)}, bf16[14,176,256]{2,1,0:T(8,128)(2,1)}, u32[]{:S(2)}, u32[]{:S(2)}) collective-permute-start(bf16[14,176,256]{2,1,0:T(8,128)(2,1)} %get-tuple-element.51), channel_id=1, source_target_pairs={{0,6},{1,7},{2,0},{3,1},{4,2},{5,3},{6,4},{7,5},{8,14},{9,15},{10,... | collective-permute-start | bytes 3784712 | tf_op jit(solution)/shard_map/ppermute | solution.py:158
  503.8 1.5 collective-permute-start.7
  505.3 54.5 %collective-permute-start.8 = (bf16[14,176,256]{2,1,0:T(8,128)(2,1)}, bf16[14,176,256]{2,1,0:T(8,128)(2,1)}, u32[]{:S(2)}, u32[]{:S(2)}) collective-permute-start(bf16[14,176,256]{2,1,0:T(8,128)(2,1)} %get-tuple-element.47), channel_id=1, source_target_pairs={{0,2},{1,3},{2,4},{3,5},{4,6},{5,7},{6,0},{7,1},{8,10},{9,11},{10,... | collective-permute-start | bytes 3784712 | tf_op jit(solution)/shard_map/ppermute | solution.py:158
  559.8 28.0 %collective-permute-start.9 = (bf16[14,176,256]{2,1,0:T(8,128)(2,1)}, bf16[14,176,256]{2,1,0:T(8,128)(2,1)}, u32[]{:S(2)}, u32[]{:S(2)}) collective-permute-start(bf16[14,176,256]{2,1,0:T(8,128)(2,1)} %get-tuple-element.48), channel_id=1, source_target_pairs={{0,3},{1,4},{2,5},{3,6},{4,7},{5,0},{6,1},{7,2},{8,11},{9,12},{10,... | collective-permute-start | bytes 3784712 | tf_op jit(solution)/shard_map/ppermute | solution.py:158
  587.7 6.9 %all_gather.3 = bf16[64,2048]{1,0:T(8,128)(2,1)S(1)} all-gather(bf16[16,2048]{1,0:T(8,128)(2,1)} %join.1), channel_id=1, replica_groups=mesh['owner'=4,'rows'=8] {'owner'}, dimensions={0}, use_global_device_ids=true | all-gather | bytes 327680 | tf_op jit(solution)/shard_map/all_gather | solution.py:183
  594.6 1.5 maximum_maximum_fusion
  596.1 1.7 copy.84
  597.8 3.3 copy.85
  601.1 2.5 copy.86
  603.6 2.5 copy.87
  606.1 2.5 copy.88
  608.7 2.6 copy.89
  611.2 2.5 copy.90
  613.8 2.5 copy.91
  616.2 14.7 %stack.35 = f32[32,176,8]{2,1,0:T(8,128)} concatenate(f32[32,176,1]{2,1,0:T(8,128)S(1)} %copy.84, f32[32,176,1]{2,1,0:T(8,128)} %copy.85, f32[32,176,1]{2,1,0:T(8,128)} %copy.86, f32[32,176,1]{2,1,0:T(8,128)} %copy.87, f32[32,176,1]{2,1,0:T(8,128)} %copy.88, f32[32,176,1]{2,1,0:T(8,128)} %copy.89, f32[32,176,1]{2,1,0:T(8,128)} %copy.90, f32[32,176,1]{2,1,0:T(8,128)} %copy.91), dimensions={2} | concatenate | bytes 360448 | tf_op jit(solution)/shard_map/stack | solution.py:173
  631.5 2.3 broadcast_divide_fusion
  633.8 1.7 fusion.8
  635.6 4.2 shard_map.87.refs_8_
  639.8 19.4 %shard_map.89.refs_8_ = bf16[16,176,2048]{2,1,0:T(8,128)(2,1)} custom-call(s32[1]{0:T(128)} %bitcast.me_ref, f32[16,176,8]{2,1,0:T(8,128)} %get-tuple-element.77.ratio_ref, bf16[14,176,256]{2,1,0:T(8,128)(2,1)} %get-tuple-element.69.refs_0_, bf16[14,176,256]{2,1,0:T(8,128)(2,1)} %collective-permute-done.28.refs_1_, ...), custom_call_target="tpu_custom_call" | custom-call | flops 151388160 | bytes 20185088 | tf_op jit(solution)/shard_map/pallas_call | solution.py:97
  659.2 4.2 shard_map.90
  663.5 19.4 %shard_map.88 = bf16[16,176,2048]{2,1,0:T(8,128)(2,1)} custom-call(s32[1]{0:T(128)} %bitcast.me_ref, f32[16,176,8]{2,1,0:T(8,128)} %get-tuple-element.78.ratio_ref, bf16[14,176,256]{2,1,0:T(8,128)(2,1)} %get-tuple-element.45.refs_0_, bf16[14,176,256]{2,1,0:T(8,128)(2,1)} %collective-permute-done.7.refs_1_, ...), custom_call_target="tpu_custom_call", output_to_operand_aliasing={{}: (10, {})} | custom-call | flops 151388160 | bytes 20185088 | tf_op jit(solution)/shard_map/pallas_call | solution.py:97
  (143 shorter events, 9.1 us)
Async XLA Ops:
  1.4 63.5 %copy-start.31 = (bf16[16,256]{1,0:T(8,128)(2,1)}, bf16[16,256]{1,0:T(8,128)(2,1)S(1)}, u32[]{:S(2)}) copy-start(bf16[16,256]{1,0:T(8,128)(2,1)S(1)} %fusion.7.refs_0_) | copy-start | bytes 24580
  1.4 57.1 %collective-permute-start.35 = (bf16[16,256]{1,0:T(8,128)(2,1)S(1)}, bf16[16,256]{1,0:T(8,128)(2,1)S(1)}, u32[]{:S(2)}, u32[]{:S(2)}) collective-permute-start(bf16[16,256]{1,0:T(8,128)(2,1)S(1)} %fusion.7.refs_0_), channel_id=1, source_target_pairs={{0,1},{1,2},{2,3},{3,4},{4,5},{5,6},{6,7},{7,0},{8,9},{9,10},{10,1... | collective-permute-start | bytes 24584 | tf_op jit(solution)/shard_map/ppermute | solution.py:158
  2.6 58.1 %collective-permute-start.36 = (bf16[16,256]{1,0:T(8,128)(2,1)S(1)}, bf16[16,256]{1,0:T(8,128)(2,1)S(1)}, u32[]{:S(2)}, u32[]{:S(2)}) collective-permute-start(bf16[16,256]{1,0:T(8,128)(2,1)S(1)} %fusion.7.refs_0_), channel_id=1, source_target_pairs={{0,2},{1,3},{2,4},{3,5},{4,6},{5,7},{6,0},{7,1},{8,10},{9,11},{10,... | collective-permute-start | bytes 24584 | tf_op jit(solution)/shard_map/ppermute | solution.py:158
  3.9 56.9 %collective-permute-start.37 = (bf16[16,256]{1,0:T(8,128)(2,1)S(1)}, bf16[16,256]{1,0:T(8,128)(2,1)S(1)}, u32[]{:S(2)}, u32[]{:S(2)}) collective-permute-start(bf16[16,256]{1,0:T(8,128)(2,1)S(1)} %fusion.7.refs_0_), channel_id=1, source_target_pairs={{0,3},{1,4},{2,5},{3,6},{4,7},{5,0},{6,1},{7,2},{8,11},{9,12},{10,... | collective-permute-start | bytes 24584 | tf_op jit(solution)/shard_map/ppermute | solution.py:158
  9.1 74.8 %collective-permute-start.21 = (bf16[2,176,256]{2,1,0:T(8,128)(2,1)}, bf16[2,176,256]{2,1,0:T(8,128)(2,1)S(1)}, u32[]{:S(2)}, u32[]{:S(2)}) collective-permute-start(bf16[2,176,256]{2,1,0:T(8,128)(2,1)} %get-tuple-element.62), channel_id=1, source_target_pairs={{0,1},{1,2},{2,3},{3,4},{4,5},{5,6},{6,7},{7,0},{8,9},{9,10},{10,1... | collective-permute-start | bytes 540680 | tf_op jit(solution)/shard_map/ppermute | solution.py:158
  9.5 75.4 %collective-permute-start.22 = (bf16[2,176,256]{2,1,0:T(8,128)(2,1)}, bf16[2,176,256]{2,1,0:T(8,128)(2,1)S(1)}, u32[]{:S(2)}, u32[]{:S(2)}) collective-permute-start(bf16[2,176,256]{2,1,0:T(8,128)(2,1)} %get-tuple-element.63), channel_id=1, source_target_pairs={{0,2},{1,3},{2,4},{3,5},{4,6},{5,7},{6,0},{7,1},{8,10},{9,11},{10,... | collective-permute-start | bytes 540680 | tf_op jit(solution)/shard_map/ppermute | solution.py:158
  52.6 27.9 %copy-start.44 = (bf16[2,176,256]{2,1,0:T(8,128)(2,1)S(1)}, bf16[2,176,256]{2,1,0:T(8,128)(2,1)}, u32[]{:S(2)}) copy-start(bf16[2,176,256]{2,1,0:T(8,128)(2,1)} %get-tuple-element.65) | copy-start | bytes 540676
  52.6 28.6 %copy-start.43 = (bf16[2,176,256]{2,1,0:T(8,128)(2,1)S(1)}, bf16[2,176,256]{2,1,0:T(8,128)(2,1)}, u32[]{:S(2)}) copy-start(bf16[2,176,256]{2,1,0:T(8,128)(2,1)} %get-tuple-element.66) | copy-start | bytes 540676
  52.6 31.3 %copy-start.42 = (bf16[2,176,256]{2,1,0:T(8,128)(2,1)S(1)}, bf16[2,176,256]{2,1,0:T(8,128)(2,1)}, u32[]{:S(2)}) copy-start(bf16[2,176,256]{2,1,0:T(8,128)(2,1)} %get-tuple-element.67) | copy-start | bytes 540676
  52.7 32.3 %copy-start.41 = (bf16[2,176,256]{2,1,0:T(8,128)(2,1)S(1)}, bf16[2,176,256]{2,1,0:T(8,128)(2,1)}, u32[]{:S(2)}) copy-start(bf16[2,176,256]{2,1,0:T(8,128)(2,1)} %get-tuple-element.68) | copy-start | bytes 540676
  57.2 51.6 %copy-start.40 = (bf16[14,176,256]{2,1,0:T(8,128)(2,1)S(1)}, bf16[14,176,256]{2,1,0:T(8,128)(2,1)}, u32[]{:S(2)}) copy-start(bf16[14,176,256]{2,1,0:T(8,128)(2,1)} %get-tuple-element.73) | copy-start | bytes 3784708
  58.5 257.9 %copy-start.33 = (bf16[16,256]{1,0:T(8,128)(2,1)}, bf16[16,256]{1,0:T(8,128)(2,1)S(1)}, u32[]{:S(2)}) copy-start(bf16[16,256]{1,0:T(8,128)(2,1)S(1)} %collective-permute-done.35.refs_1_) | copy-start | bytes 24580
  58.5 13.9 %collective-permute-start = (f32[32,176]{1,0:T(8,128)S(1)}, f32[32,176]{1,0:T(8,128)S(1)}, u32[]{:S(2)}, u32[]{:S(2)}) collective-permute-start(f32[32,176]{1,0:T(8,128)S(1)} %get-tuple-element.87), channel_id=1, source_target_pairs={{0,1},{1,2},{2,3},{3,4},{4,5},{5,6},{6,7},{7,0},{8,9},{9,10},{10,1... | collective-permute-start | bytes 67592 | tf_op jit(solution)/shard_map/ppermute | solution.py:158
  60.7 255.7 %copy-start.34 = (bf16[16,256]{1,0:T(8,128)(2,1)}, bf16[16,256]{1,0:T(8,128)(2,1)S(1)}, u32[]{:S(2)}) copy-start(bf16[16,256]{1,0:T(8,128)(2,1)S(1)} %collective-permute-done.36.refs_2_) | copy-start | bytes 24580
  60.7 3.4 collective-permute-start.38
  60.8 255.6 %copy-start.35 = (bf16[16,256]{1,0:T(8,128)(2,1)}, bf16[16,256]{1,0:T(8,128)(2,1)S(1)}, u32[]{:S(2)}) copy-start(bf16[16,256]{1,0:T(8,128)(2,1)S(1)} %collective-permute-done.37.refs_3_) | copy-start | bytes 24580
  60.8 4.1 collective-permute-start.39
  64.1 3.1 collective-permute-start.40
  64.9 4.3 collective-permute-start.41
  67.8 4.7 collective-permute-start.1
  69.8 4.6 collective-permute-start.2
  72.4 3.8 collective-permute-start.3
  72.4 5.8 collective-permute-start.4
  74.4 5.5 collective-permute-start.5
  76.2 5.1 collective-permute-start.6
  78.9 6.6 collective-permute-start.23
  80.5 12.4 %collective-permute-start.24 = (bf16[2,176,256]{2,1,0:T(8,128)(2,1)S(1)}, bf16[2,176,256]{2,1,0:T(8,128)(2,1)S(1)}, u32[]{:S(2)}, u32[]{:S(2)}) collective-permute-start(bf16[2,176,256]{2,1,0:T(8,128)(2,1)S(1)} %copy-done.44), channel_id=1, source_target_pairs={{0,4},{1,5},{2,6},{3,7},{4,0},{5,1},{6,2},{7,3},{8,12},{9,13},{10,... | collective-permute-start | bytes 540680 | tf_op jit(solution)/shard_map/ppermute | solution.py:158
  81.3 478.5 %copy-start.27 = (f32[32,176]{1,0:T(8,128)}, f32[32,176]{1,0:T(8,128)S(1)}, u32[]{:S(2)}) copy-start(f32[32,176]{1,0:T(8,128)S(1)} %collective-permute-done.6) | copy-start | bytes 67588
  81.3 23.9 %collective-permute-start.25 = (bf16[2,176,256]{2,1,0:T(8,128)(2,1)S(1)}, bf16[2,176,256]{2,1,0:T(8,128)(2,1)S(1)}, u32[]{:S(2)}, u32[]{:S(2)}) collective-permute-start(bf16[2,176,256]{2,1,0:T(8,128)(2,1)S(1)} %copy-done.43), channel_id=1, source_target_pairs={{0,5},{1,6},{2,7},{3,0},{4,1},{5,2},{6,3},{7,4},{8,13},{9,14},{10,... | collective-permute-start | bytes 540680 | tf_op jit(solution)/shard_map/ppermute | solution.py:158
  83.9 513.9 %copy-start.2 = (bf16[2,176,256]{2,1,0:T(8,128)(2,1)}, bf16[2,176,256]{2,1,0:T(8,128)(2,1)S(1)}, u32[]{:S(2)}) copy-start(bf16[2,176,256]{2,1,0:T(8,128)(2,1)S(1)} %collective-permute-done.21.refs_1_) | copy-start | bytes 540676
  83.9 24.2 %collective-permute-start.26 = (bf16[2,176,256]{2,1,0:T(8,128)(2,1)S(1)}, bf16[2,176,256]{2,1,0:T(8,128)(2,1)S(1)}, u32[]{:S(2)}, u32[]{:S(2)}) collective-permute-start(bf16[2,176,256]{2,1,0:T(8,128)(2,1)S(1)} %copy-done.42), channel_id=1, source_target_pairs={{0,6},{1,7},{2,0},{3,1},{4,2},{5,3},{6,4},{7,5},{8,14},{9,15},{10,... | collective-permute-start | bytes 540680 | tf_op jit(solution)/shard_map/ppermute | solution.py:158
  85.0 512.8 %copy-start.3 = (bf16[2,176,256]{2,1,0:T(8,128)(2,1)}, bf16[2,176,256]{2,1,0:T(8,128)(2,1)S(1)}, u32[]{:S(2)}) copy-start(bf16[2,176,256]{2,1,0:T(8,128)(2,1)S(1)} %collective-permute-done.22.refs_2_) | copy-start | bytes 540676
  85.0 23.8 %collective-permute-start.27 = (bf16[2,176,256]{2,1,0:T(8,128)(2,1)S(1)}, bf16[2,176,256]{2,1,0:T(8,128)(2,1)S(1)}, u32[]{:S(2)}, u32[]{:S(2)}) collective-permute-start(bf16[2,176,256]{2,1,0:T(8,128)(2,1)S(1)} %copy-done.41), channel_id=1, source_target_pairs={{0,7},{1,0},{2,1},{3,2},{4,3},{5,4},{6,5},{7,6},{8,15},{9,8},{10,9... | collective-permute-start | bytes 540680 | tf_op jit(solution)/shard_map/ppermute | solution.py:158
  85.5 510.6 %copy-start.4 = (bf16[2,176,256]{2,1,0:T(8,128)(2,1)}, bf16[2,176,256]{2,1,0:T(8,128)(2,1)S(1)}, u32[]{:S(2)}) copy-start(bf16[2,176,256]{2,1,0:T(8,128)(2,1)S(1)} %collective-permute-done.23.refs_3_) | copy-start | bytes 540676
  85.5 25.0 %collective-permute-start.14 = (bf16[2,176,256]{2,1,0:T(8,128)(2,1)}, bf16[2,176,256]{2,1,0:T(8,128)(2,1)S(1)}, u32[]{:S(2)}, u32[]{:S(2)}) collective-permute-start(bf16[2,176,256]{2,1,0:T(8,128)(2,1)} %get-tuple-element.54), channel_id=1, source_target_pairs={{0,1},{1,2},{2,3},{3,4},{4,5},{5,6},{6,7},{7,0},{8,9},{9,10},{10,1... | collective-permute-start | bytes 540680 | tf_op jit(solution)/shard_map/ppermute | solution.py:158
  92.8 466.9 %copy-start.5 = (bf16[2,176,256]{2,1,0:T(8,128)(2,1)}, bf16[2,176,256]{2,1,0:T(8,128)(2,1)S(1)}, u32[]{:S(2)}) copy-start(bf16[2,176,256]{2,1,0:T(8,128)(2,1)S(1)} %collective-permute-done.24.refs_4_) | copy-start | bytes 540676
  92.8 217.0 %collective-permute-start.28 = (bf16[14,176,256]{2,1,0:T(8,128)(2,1)}, bf16[14,176,256]{2,1,0:T(8,128)(2,1)}, u32[]{:S(2)}, u32[]{:S(2)}) collective-permute-start(bf16[14,176,256]{2,1,0:T(8,128)(2,1)} %get-tuple-element.70), channel_id=1, source_target_pairs={{0,1},{1,2},{2,3},{3,4},{4,5},{5,6},{6,7},{7,0},{8,9},{9,10},{10,1... | collective-permute-start | bytes 3784712 | tf_op jit(solution)/shard_map/ppermute | solution.py:158
  105.1 208.6 %copy-start.6 = (bf16[2,176,256]{2,1,0:T(8,128)(2,1)}, bf16[2,176,256]{2,1,0:T(8,128)(2,1)S(1)}, u32[]{:S(2)}) copy-start(bf16[2,176,256]{2,1,0:T(8,128)(2,1)S(1)} %collective-permute-done.25.refs_5_) | copy-start | bytes 540676
  105.1 207.6 %collective-permute-start.29 = (bf16[14,176,256]{2,1,0:T(8,128)(2,1)}, bf16[14,176,256]{2,1,0:T(8,128)(2,1)}, u32[]{:S(2)}, u32[]{:S(2)}) collective-permute-start(bf16[14,176,256]{2,1,0:T(8,128)(2,1)} %get-tuple-element.71), channel_id=1, source_target_pairs={{0,2},{1,3},{2,4},{3,5},{4,6},{5,7},{6,0},{7,1},{8,10},{9,11},{10,... | collective-permute-start | bytes 3784712 | tf_op jit(solution)/shard_map/ppermute | solution.py:158
  108.1 205.7 %copy-start.7 = (bf16[2,176,256]{2,1,0:T(8,128)(2,1)}, bf16[2,176,256]{2,1,0:T(8,128)(2,1)S(1)}, u32[]{:S(2)}) copy-start(bf16[2,176,256]{2,1,0:T(8,128)(2,1)S(1)} %collective-permute-done.26.refs_6_) | copy-start | bytes 540676
  108.1 204.6 %collective-permute-start.30 = (bf16[14,176,256]{2,1,0:T(8,128)(2,1)}, bf16[14,176,256]{2,1,0:T(8,128)(2,1)}, u32[]{:S(2)}, u32[]{:S(2)}) collective-permute-start(bf16[14,176,256]{2,1,0:T(8,128)(2,1)} %get-tuple-element.72), channel_id=1, source_target_pairs={{0,3},{1,4},{2,5},{3,6},{4,7},{5,0},{6,1},{7,2},{8,11},{9,12},{10,... | collective-permute-start | bytes 3784712 | tf_op jit(solution)/shard_map/ppermute | solution.py:158
  108.8 205.0 %copy-start.8 = (bf16[2,176,256]{2,1,0:T(8,128)(2,1)}, bf16[2,176,256]{2,1,0:T(8,128)(2,1)S(1)}, u32[]{:S(2)}) copy-start(bf16[2,176,256]{2,1,0:T(8,128)(2,1)S(1)} %collective-permute-done.27.refs_7_) | copy-start | bytes 540676
  108.8 205.0 %collective-permute-start.31 = (bf16[14,176,256]{2,1,0:T(8,128)(2,1)S(1)}, bf16[14,176,256]{2,1,0:T(8,128)(2,1)}, u32[]{:S(2)}, u32[]{:S(2)}) collective-permute-start(bf16[14,176,256]{2,1,0:T(8,128)(2,1)S(1)} %copy-done.40), channel_id=1, source_target_pairs={{0,4},{1,5},{2,6},{3,7},{4,0},{5,1},{6,2},{7,3},{8,12},{9,13},{10,... | collective-permute-start | bytes 3784712 | tf_op jit(solution)/shard_map/ppermute | solution.py:158
  110.5 203.3 %copy-start.9 = (bf16[2,176,256]{2,1,0:T(8,128)(2,1)}, bf16[2,176,256]{2,1,0:T(8,128)(2,1)S(1)}, u32[]{:S(2)}) copy-start(bf16[2,176,256]{2,1,0:T(8,128)(2,1)S(1)} %collective-permute-done.14.refs_1_) | copy-start | bytes 540676
  110.5 69.4 %collective-permute-start.15 = (bf16[2,176,256]{2,1,0:T(8,128)(2,1)}, bf16[2,176,256]{2,1,0:T(8,128)(2,1)S(1)}, u32[]{:S(2)}, u32[]{:S(2)}) collective-permute-start(bf16[2,176,256]{2,1,0:T(8,128)(2,1)} %get-tuple-element.55), channel_id=1, source_target_pairs={{0,2},{1,3},{2,4},{3,5},{4,6},{5,7},{6,0},{7,1},{8,10},{9,11},{10,... | collective-permute-start | bytes 540680 | tf_op jit(solution)/shard_map/ppermute | solution.py:158
  179.9 133.9 %copy-start.10 = (bf16[2,176,256]{2,1,0:T(8,128)(2,1)}, bf16[2,176,256]{2,1,0:T(8,128)(2,1)S(1)}, u32[]{:S(2)}) copy-start(bf16[2,176,256]{2,1,0:T(8,128)(2,1)S(1)} %collective-permute-done.15.refs_2_) | copy-start | bytes 540676
  179.9 31.0 %collective-permute-start.16 = (bf16[2,176,256]{2,1,0:T(8,128)(2,1)}, bf16[2,176,256]{2,1,0:T(8,128)(2,1)S(1)}, u32[]{:S(2)}, u32[]{:S(2)}) collective-permute-start(bf16[2,176,256]{2,1,0:T(8,128)(2,1)} %get-tuple-element.56), channel_id=1, source_target_pairs={{0,3},{1,4},{2,5},{3,6},{4,7},{5,0},{6,1},{7,2},{8,11},{9,12},{10,... | collective-permute-start | bytes 540680 | tf_op jit(solution)/shard_map/ppermute | solution.py:158
  210.9 102.9 %copy-start.11 = (bf16[2,176,256]{2,1,0:T(8,128)(2,1)}, bf16[2,176,256]{2,1,0:T(8,128)(2,1)S(1)}, u32[]{:S(2)}) copy-start(bf16[2,176,256]{2,1,0:T(8,128)(2,1)S(1)} %collective-permute-done.16.refs_3_) | copy-start | bytes 540676
  210.9 76.7 %collective-permute-start.17 = (bf16[2,176,256]{2,1,0:T(8,128)(2,1)}, bf16[2,176,256]{2,1,0:T(8,128)(2,1)S(1)}, u32[]{:S(2)}, u32[]{:S(2)}) collective-permute-start(bf16[2,176,256]{2,1,0:T(8,128)(2,1)} %get-tuple-element.57), channel_id=1, source_target_pairs={{0,4},{1,5},{2,6},{3,7},{4,0},{5,1},{6,2},{7,3},{8,12},{9,13},{10,... | collective-permute-start | bytes 540680 | tf_op jit(solution)/shard_map/ppermute | solution.py:158
  287.6 5.7 collective-permute-start.18
  293.4 5.4 collective-permute-start.19
  298.8 6.7 collective-permute-start.20
  305.5 50.0 %collective-permute-start.32 = (bf16[14,176,256]{2,1,0:T(8,128)(2,1)}, bf16[14,176,256]{2,1,0:T(8,128)(2,1)}, u32[]{:S(2)}, u32[]{:S(2)}) collective-permute-start(bf16[14,176,256]{2,1,0:T(8,128)(2,1)} %get-tuple-element.74), channel_id=1, source_target_pairs={{0,5},{1,6},{2,7},{3,0},{4,1},{5,2},{6,3},{7,4},{8,13},{9,14},{10,... | collective-permute-start | bytes 3784712 | tf_op jit(solution)/shard_map/ppermute | solution.py:158
  309.9 193.9 %collective-permute-start.33 = (bf16[14,176,256]{2,1,0:T(8,128)(2,1)}, bf16[14,176,256]{2,1,0:T(8,128)(2,1)}, u32[]{:S(2)}, u32[]{:S(2)}) collective-permute-start(bf16[14,176,256]{2,1,0:T(8,128)(2,1)} %get-tuple-element.75), channel_id=1, source_target_pairs={{0,6},{1,7},{2,0},{3,1},{4,2},{5,3},{6,4},{7,5},{8,14},{9,15},{10,... | collective-permute-start | bytes 3784712 | tf_op jit(solution)/shard_map/ppermute | solution.py:158
  312.7 191.1 %collective-permute-start.34 = (bf16[14,176,256]{2,1,0:T(8,128)(2,1)}, bf16[14,176,256]{2,1,0:T(8,128)(2,1)}, u32[]{:S(2)}, u32[]{:S(2)}) collective-permute-start(bf16[14,176,256]{2,1,0:T(8,128)(2,1)} %get-tuple-element.76), channel_id=1, source_target_pairs={{0,7},{1,0},{2,1},{3,2},{4,3},{5,4},{6,5},{7,6},{8,15},{9,8},{10,9... | collective-permute-start | bytes 3784712 | tf_op jit(solution)/shard_map/ppermute | solution.py:158
  312.7 192.5 %collective-permute-start.10 = (bf16[14,176,256]{2,1,0:T(8,128)(2,1)}, bf16[14,176,256]{2,1,0:T(8,128)(2,1)S(1)}, u32[]{:S(2)}, u32[]{:S(2)}) collective-permute-start(bf16[14,176,256]{2,1,0:T(8,128)(2,1)} %get-tuple-element.49), channel_id=1, source_target_pairs={{0,4},{1,5},{2,6},{3,7},{4,0},{5,1},{6,2},{7,3},{8,12},{9,13},{10,... | collective-permute-start | bytes 3784712 | tf_op jit(solution)/shard_map/ppermute | solution.py:158
  313.8 245.9 %collective-permute-start.11 = (bf16[14,176,256]{2,1,0:T(8,128)(2,1)}, bf16[14,176,256]{2,1,0:T(8,128)(2,1)S(1)}, u32[]{:S(2)}, u32[]{:S(2)}) collective-permute-start(bf16[14,176,256]{2,1,0:T(8,128)(2,1)} %get-tuple-element.50), channel_id=1, source_target_pairs={{0,5},{1,6},{2,7},{3,0},{4,1},{5,2},{6,3},{7,4},{8,13},{9,14},{10,... | collective-permute-start | bytes 3784712 | tf_op jit(solution)/shard_map/ppermute | solution.py:158
  355.5 307.9 %collective-permute-start.12 = (bf16[14,176,256]{2,1,0:T(8,128)(2,1)}, bf16[14,176,256]{2,1,0:T(8,128)(2,1)}, u32[]{:S(2)}, u32[]{:S(2)}) collective-permute-start(bf16[14,176,256]{2,1,0:T(8,128)(2,1)} %get-tuple-element.51), channel_id=1, source_target_pairs={{0,6},{1,7},{2,0},{3,1},{4,2},{5,3},{6,4},{7,5},{8,14},{9,15},{10,... | collective-permute-start | bytes 3784712 | tf_op jit(solution)/shard_map/ppermute | solution.py:158
  503.8 159.7 %collective-permute-start.13 = (bf16[14,176,256]{2,1,0:T(8,128)(2,1)}, bf16[14,176,256]{2,1,0:T(8,128)(2,1)}, u32[]{:S(2)}, u32[]{:S(2)}) collective-permute-start(bf16[14,176,256]{2,1,0:T(8,128)(2,1)} %get-tuple-element.52), channel_id=1, source_target_pairs={{0,7},{1,0},{2,1},{3,2},{4,3},{5,4},{6,5},{7,6},{8,15},{9,8},{10,9... | collective-permute-start | bytes 3784712 | tf_op jit(solution)/shard_map/ppermute | solution.py:158
  503.8 159.7 %collective-permute-start.7 = (bf16[14,176,256]{2,1,0:T(8,128)(2,1)}, bf16[14,176,256]{2,1,0:T(8,128)(2,1)}, u32[]{:S(2)}, u32[]{:S(2)}) collective-permute-start(bf16[14,176,256]{2,1,0:T(8,128)(2,1)} %get-tuple-element.46), channel_id=1, source_target_pairs={{0,1},{1,2},{2,3},{3,4},{4,5},{5,6},{6,7},{7,0},{8,9},{9,10},{10,1... | collective-permute-start | bytes 3784712 | tf_op jit(solution)/shard_map/ppermute | solution.py:158
  505.3 90.8 %copy-start = (bf16[14,176,256]{2,1,0:T(8,128)(2,1)}, bf16[14,176,256]{2,1,0:T(8,128)(2,1)S(1)}, u32[]{:S(2)}) copy-start(bf16[14,176,256]{2,1,0:T(8,128)(2,1)S(1)} %collective-permute-done.10.refs_4_) | copy-start | bytes 3784708
  505.3 158.2 %collective-permute-start.8 = (bf16[14,176,256]{2,1,0:T(8,128)(2,1)}, bf16[14,176,256]{2,1,0:T(8,128)(2,1)}, u32[]{:S(2)}, u32[]{:S(2)}) collective-permute-start(bf16[14,176,256]{2,1,0:T(8,128)(2,1)} %get-tuple-element.47), channel_id=1, source_target_pairs={{0,2},{1,3},{2,4},{3,5},{4,6},{5,7},{6,0},{7,1},{8,10},{9,11},{10,... | collective-permute-start | bytes 3784712 | tf_op jit(solution)/shard_map/ppermute | solution.py:158
  559.8 36.3 %copy-start.1 = (bf16[14,176,256]{2,1,0:T(8,128)(2,1)}, bf16[14,176,256]{2,1,0:T(8,128)(2,1)S(1)}, u32[]{:S(2)}) copy-start(bf16[14,176,256]{2,1,0:T(8,128)(2,1)S(1)} %collective-permute-done.11.refs_5_) | copy-start | bytes 3784708
  559.8 103.7 %collective-permute-start.9 = (bf16[14,176,256]{2,1,0:T(8,128)(2,1)}, bf16[14,176,256]{2,1,0:T(8,128)(2,1)}, u32[]{:S(2)}, u32[]{:S(2)}) collective-permute-start(bf16[14,176,256]{2,1,0:T(8,128)(2,1)} %get-tuple-element.48), channel_id=1, source_target_pairs={{0,3},{1,4},{2,5},{3,6},{4,7},{5,0},{6,1},{7,2},{8,11},{9,12},{10,... | collective-permute-start | bytes 3784712 | tf_op jit(solution)/shard_map/ppermute | solution.py:158
  (24 other events, 165.8 us)

commit v2 on v1

--- a/solution.py
+++ b/solution.py
@@ -70,14 +70,17 @@
     )(me, master)
 
 
-def unpack_body(n, me_ref, ratio_ref, *refs):
-    pieces, out = refs[:n], refs[-1]
+def unpack_body(n, first, start, me_ref, *refs):
+    tops, pieces, out, ratios = refs[:n], refs[n : 2 * n], refs[-2], refs[-1]
     width, rows = pieces[0].shape[1:]
     step = 16
+    expert = first + pl.program_id(0)
+    top = jnp.concatenate([t[pl.ds(expert, 1), start : start + width] for t in tops], axis=0)
+    ratios[...] = (top / jnp.max(top, axis=0, keepdims=True)).T
 
     def some_rows(i, _):
         part = pl.ds(pl.multiple_of(i * step, step), step)
-        ratio = ratio_ref[0, part, :]
+        ratio = ratios[part, :]
         for k in range(n):
             code = pieces[k][0, part, :].astype(jnp.float32)
             root = jnp.log(jnp.abs(code)) * (1.0 / (SPAN * LN2)) + 0.5
@@ -90,55 +93,56 @@
     lax.fori_loop(0, width // step, some_rows, 0)
 
 
-def unpack(me, ratio, pieces, whole, first, shape):
+def unpack(me, tops, start, pieces, whole, first, shape):
     n = len(pieces)
     count, width, rows = pieces[0].shape
-    operands = [ratio, *pieces] + ([] if whole is None else [whole])
+    operands = [*tops, *pieces] + ([] if whole is None else [whole])
     return pl.pallas_call(
-        functools.partial(unpack_body, n),
+        functools.partial(unpack_body, n, first, start),
         grid_spec=pltpu.PrefetchScalarGridSpec(
             num_scalar_prefetch=1,
             grid=(count,),
-            in_specs=[pl.BlockSpec((1, width, n), lambda e, me: (first + e, 0, 0))]
+            in_specs=[pl.BlockSpec(tops[0].shape, lambda e, me: (0, 0))] * n
             + [pl.BlockSpec((1, width, rows), lambda e, me: (e, 0, 0))] * n
             + ([] if whole is None else [pl.BlockSpec(memory_space=pl.ANY)]),
             out_specs=pl.BlockSpec((1, width, n * rows), lambda e, me: (first + e, 0, 0)),
+            scratch_shapes=[pltpu.VMEM((width, n), jnp.float32)],
         ),
         out_shape=jax.ShapeDtypeStruct(shape, jnp.bfloat16),
-        input_output_aliases={} if whole is None else {n + 2: 0},
+        input_output_aliases={} if whole is None else {2 * n + 1: 0},
         cost_estimate=pl.CostEstimate(
             flops=count * rows * width * n * 30, bytes_accessed=count * rows * width * n * 4, transcendentals=0
         ),
     )(me, *operands)
 
 
-def plan(experts):
-    small = max(1, experts // 8)
-    return (
-        (0, 0, small),
-        (0, small, experts - small),
-        (1, 0, experts - small),
-        (1, experts - small, small),
-    )
-
-
 def join_body(n, me_ref, *refs):
-    out, rows = refs[n], refs[0].shape[1]
-    for k in range(n):
-        source = lax.rem(me_ref[0] + (n - k), n)
-        out[:, pl.ds(pl.multiple_of(source * rows, rows), rows)] = refs[k][...]
-
-
-def join(me, pieces):
-    n = len(pieces)
-    columns, rows = pieces[0].shape
+    out, half = refs[-1], n // 2
+    columns, rows = refs[0].shape[0] // 2, refs[0].shape[1]
+    place = lax.rem(me_ref[0], half)
+    for k in range(half):
+        source = me_ref[0] - place + lax.rem(place + (half - k), half)
+        for part in range(2):
+            at = lax.rem(source + part * half, n) * rows
+            out[:, pl.ds(pl.multiple_of(at, rows), rows)] = refs[k][columns * part : columns * (part + 1), :]
+
+
+def join(n, me, pairs):
+    columns, rows = pairs[0].shape[0] // 2, pairs[0].shape[1]
     return pl.pallas_call(
         functools.partial(join_body, n),
-        in_specs=[pl.BlockSpec(memory_space=pltpu.SMEM)] + [pl.BlockSpec(memory_space=pltpu.VMEM)] * n,
+        in_specs=[pl.BlockSpec(memory_space=pltpu.SMEM)] + [pl.BlockSpec(memory_space=pltpu.VMEM)] * len(pairs),
         out_specs=pl.BlockSpec(memory_space=pltpu.VMEM),
         out_shape=jax.ShapeDtypeStruct((columns, n * rows), jnp.bfloat16),
         name="join",
-    )(me, *pieces)
+    )(me, *pairs)
+
+
+def plan(experts):
+    first = [c for c in (experts // 8, experts // 3) if c]
+    last = [c for c in (experts // 4, experts // 8, experts // 16) if c]
+    counts = ((*first, experts - sum(first)), (experts - sum(last), *last))
+    return [(a, sum(counts[a][:c]), count) for a in range(2) for c, count in enumerate(counts[a])]
 
 
 def send_order(n):
@@ -166,22 +170,25 @@
         tops[a].append(top[:, 0, :])
     came = [send(pieces) for pieces in packed]
 
-    top = jnp.concatenate(tops[0] + tops[1], axis=0)
-    top = lax.dynamic_slice_in_dim(jnp.concatenate([top, top], axis=1), me * width, depth, axis=1)
-    all_tops = send([top[:, k * width : (k + 1) * width] for k in range(n)])
-    scale = functools.reduce(jnp.maximum, all_tops)
-    ratio = jnp.stack(all_tops, axis=-1) / scale[:, :, None]
-    ratios = (ratio[:experts], ratio[experts:])
+    tops = [jnp.concatenate(some, axis=0) for some in tops]
+    tops = [lax.dynamic_slice_in_dim(jnp.concatenate([t, t], axis=1), me * width, depth, axis=1) for t in tops]
+    tops = send([jnp.concatenate([t[:, k * width : (k + 1) * width] for t in tops], axis=1) for k in range(n)])
+    scale = functools.reduce(jnp.maximum, tops)
 
     wholes = [None, None]
     for c, (a, first, count) in enumerate(chunks):
-        wholes[a] = unpack(here, ratios[a], came[c], wholes[a], first, (experts, width, n * rows))
+        wholes[a] = unpack(here, tops, a * width, came[c], wholes[a], first, (experts, width, n * rows))
     finals = [jnp.swapaxes(whole, 1, 2) for whole in wholes]
 
-    part_router = (router_weight * router_gain[:, None]).astype(jnp.bfloat16).T
-    routers = join(here, send([part_router] * n))
-    serve_router = lax.all_gather(routers, "owner", axis=0, tiled=True).T
-    return (*finals, scale[:experts], scale[experts:], serve_router)
+    half = n // 2
+    router = (router_weight * router_gain[:, None]).astype(jnp.bfloat16).T
+    pair = [router, lax.ppermute(router, "rows", turns[half])]
+    pairs = [jnp.concatenate(pair, axis=0)]
+    for k in range(1, half):
+        inside = [(r, r // half * half + (r + k) % half) for r in range(n)]
+        pairs.append(lax.ppermute(pairs[0], "rows", inside))
+    serve_router = lax.all_gather(join(n, here, pairs), "owner", axis=0, tiled=True).T
+    return (*finals, scale[:, :width], scale[:, width:], serve_router)
 
 
 def shards(n, master_gate, master_up, router_weight, router_gain):
@@ -192,7 +199,7 @@
 
 
 def fits(n, experts, rows, depth):
-    return n > 1 and experts > 1 and rows % 128 == 0 and depth % (16 * n) == 0 and depth % 128 == 0
+    return n % 2 == 0 and experts >= 8 and rows % 128 == 0 and depth % (16 * n) == 0 and depth % 128 == 0
 
 
 def solution(mesh):

time: 687 us -> 635 us (0.924)
  starting transfers between devices: 396 us -> 289 us
  waiting for transfers between devices: 134 us -> 199 us
  local copies, waits for them, and re-layouts: 41.3 us -> 8.79 us
  Pallas kernels: 99.4 us -> 115 us
  blocking collectives: 6.86 us -> 16.5 us
    ppermute x42 -> x56, starting transfers between devices: 396 us -> 286 us  [send(): came[k] = lax.ppermute(pieces[k], 'rows', turns[k])]
    ppermute x42 -> x56, waiting for transfers between devices: 134 us -> 188 us  [send(): came[k] = lax.ppermute(pieces[k], 'rows', turns[k])]
    another operation x9 -> x0, local copies, waits for them, and re-layouts: 34.8 us -> none  [fast_shards(): ratio = jnp.stack(all_tops, axis=-1) / scale[:, :, None]]
    ppermute x0 -> x4, waiting for transfers between devices: none -> 10.6 us  [the longest x3 7.99 us: fast_shards(): pairs.append(lax.ppermute(pairs[0], 'rows', inside))]
    pallas_call x4 -> x7, Pallas kernels: 47.3 us -> 57.1 us  [unpack(): pl.pallas_call(functools.partial(unpack_body, n, first, start), grid_spec...]
    all_gather x1, blocking collectives: 6.86 us -> 16.5 us  [fast_shards(): lax.all_gather(join(n, here, pairs), 'owner', axis=0, tiled=True)]
    pallas_call x4 -> x7, Pallas kernels: 50.6 us -> 56.1 us  [pack(): pl.pallas_call(functools.partial(pack_body, n), grid_spec=pltpu.PrefetchS...]
  transfers between devices with their start and end apart: 42 -> 60, of which waited for: 14 -> 15; matrix products, arithmetic and copies ran while one was open for 6% -> 0% of each run, Pallas kernels for 12% -> 7%
where the time goes in v2:
time: 635 us; the launch traced here: 632 us
  starting transfers between devices  289 us (46%)
  waiting for transfers between devices  199 us (31%)
  Pallas kernels  115 us (18%)
  blocking collectives  16.5 us (3%)
  local copies, waits for them, and re-layouts  8.79 us (1%)
    ppermute x56, starting transfers between devices, send(): came[k] = lax.ppermute(pieces[k], 'rows', turns[k])  286 us
    ppermute x56, waiting for transfers between devices, send(): came[k] = lax.ppermute(pieces[k], 'rows', turns[k])  188 us
    pallas_call x7, Pallas kernels, unpack(): pl.pallas_call(functools.partial(unpack_body, n, first, start), grid_spec...  57.1 us
    pallas_call x7, Pallas kernels, pack(): pl.pallas_call(functools.partial(pack_body, n), grid_spec=pltpu.PrefetchS...  56.1 us
    all_gather x1, blocking collectives, fast_shards(): lax.all_gather(join(n, here, pairs), 'owner', axis=0, tiled=True)  16.5 us
  transfers between devices with their start and end apart: 60, of which 15 were waited for; matrix products, arithmetic and copies ran while one was open for 0% of the time, Pallas kernels for 7%

profile of v2, /device:TPU:17, one launch (start us, length us, event | category | flops | bytes accessed | tf_op | source)
XLA Modules:
  0.0 632.0 jit_solution(15640839300501128617)
XLA Ops:
  0.6 14.1 %shard_map.85 = (bf16[9,176,256]{2,1,0:T(8,128)(2,1)}, bf16[9,176,256]{2,1,0:T(8,128)(2,1)}, bf16[9,176,256]{2,1,0:T(8,128)(2,1)}, bf16[9,176,256]{2,1,0:T(8,128...) custom-call(s32[1]{0:T(128)} %bitcast.me_ref, ...), custom_call_target="tpu_custom_call" | custom-call | flops 129761280 | bytes 19464192 | tf_op jit(solution)/shard_map/pallas_call | solution.py:55
  14.7 8.7 %shard_map.84 = (bf16[5,176,256]{2,1,0:T(8,128)(2,1)}, bf16[5,176,256]{2,1,0:T(8,128)(2,1)}, bf16[5,176,256]{2,1,0:T(8,128)(2,1)}, bf16[5,176,256]{2,1,0:T(8,128...) custom-call(s32[1]{0:T(128)} %bitcast.me_ref, ...), custom_call_target="tpu_custom_call" | custom-call | flops 72089600 | bytes 10813440 | tf_op jit(solution)/shard_map/pallas_call | solution.py:55
  23.4 14.0 %shard_map.86 = (bf16[9,176,256]{2,1,0:T(8,128)(2,1)}, bf16[9,176,256]{2,1,0:T(8,128)(2,1)}, bf16[9,176,256]{2,1,0:T(8,128)(2,1)}, bf16[9,176,256]{2,1,0:T(8,128...) custom-call(s32[1]{0:T(128)} %bitcast.me_ref, ...), custom_call_target="tpu_custom_call" | custom-call | flops 129761280 | bytes 19464192 | tf_op jit(solution)/shard_map/pallas_call | solution.py:55
  37.4 7.2 %shard_map.87 = (bf16[4,176,256]{2,1,0:T(8,128)(2,1)}, bf16[4,176,256]{2,1,0:T(8,128)(2,1)}, bf16[4,176,256]{2,1,0:T(8,128)(2,1)}, bf16[4,176,256]{2,1,0:T(8,128...) custom-call(s32[1]{0:T(128)} %bitcast.me_ref, ...), custom_call_target="tpu_custom_call" | custom-call | flops 57671680 | bytes 8650752 | tf_op jit(solution)/shard_map/pallas_call | solution.py:55
  44.6 4.4 shard_map.88
  49.0 4.4 shard_map.83
  53.5 3.4 shard_map.89
  57.0 1.1 fusion.3
  58.4 1.2 collective-permute-start
  59.8 1.3 collective-permute-start.1
  62.1 1.4 collective-permute-start.3
  64.7 2.6 collective-permute-done.56
  69.2 1.7 collective-permute-start.6
  71.2 4.2 collective-permute-start.30
  76.1 4.3 collective-permute-done.57.refs_1_
  80.4 1.8 collective-permute-start.58
  82.2 1.4 collective-permute-done.58.refs_2_
  84.2 2.3 collective-permute-done.59.refs_3_
  86.5 3.5 collective-permute-start.32
  91.3 1.5 collective-permute-start.35
  93.5 3.6 collective-permute-start.37
  97.7 1.2 collective-permute-start.34
  98.9 14.0 %collective-permute-done.34.refs_15_ = bf16[1,176,256]{2,1,0:T(8,128)(2,1)S(1)} collective-permute-done((bf16[1,176,256]{2,1,0:T(8,128)(2,1)}, bf16[1,176,256]{2,1,0:T(8,128)(2,1)S(1)}, u32[]{:S(2)}, u32[]{:S(2)}) %collective-permute-start.34) | collective-permute-done | bytes 90144 | tf_op jit(solution)/shard_map/ppermute | solution.py:162
  113.7 3.0 collective-permute-start.41
  117.0 2.4 collective-permute-start.22
  119.4 4.5 collective-permute-start.23
  123.9 1.0 collective-permute-done.40.refs_14_
  125.5 9.3 %collective-permute-start.42 = (bf16[4,176,256]{2,1,0:T(8,128)(2,1)}, bf16[4,176,256]{2,1,0:T(8,128)(2,1)S(1)}, u32[]{:S(2)}, u32[]{:S(2)}) collective-permute-start(bf16[4,176,256]{2,1,0:T(8,128)(2,1)} %get-tuple-element.116), channel_id=1, source_target_pairs={{0,1},{1,2},{2,3},{3,4},{4,5},{5,6},{6,7},{7,0},{8,9},{9,10},{10,1... | collective-permute-start | bytes 1081352 | tf_op jit(solution)/shard_map/ppermute | solution.py:162
  135.1 3.8 collective-permute-start.26
  138.9 2.4 collective-permute-start.27
  141.3 11.0 %collective-permute-done.25.refs_13_ = bf16[2,176,256]{2,1,0:T(8,128)(2,1)S(1)} collective-permute-done((bf16[2,176,256]{2,1,0:T(8,128)(2,1)}, bf16[2,176,256]{2,1,0:T(8,128)(2,1)S(1)}, u32[]{:S(2)}, u32[]{:S(2)}) %collective-permute-start.25) | collective-permute-done | bytes 180256 | tf_op jit(solution)/shard_map/ppermute | solution.py:162
  152.3 1.8 collective-permute-start.44
  154.1 1.1 collective-permute-done.26.refs_14_
  155.3 1.3 collective-permute-start.45
  156.6 14.0 %collective-permute-done.27.refs_15_ = bf16[2,176,256]{2,1,0:T(8,128)(2,1)S(1)} collective-permute-done((bf16[2,176,256]{2,1,0:T(8,128)(2,1)S(1)}, bf16[2,176,256]{2,1,0:T(8,128)(2,1)S(1)}, u32[]{:S(2)}, u32[]{:S(2)}) %collective-permute-start.27) | collective-permute-done | bytes 180256 | tf_op jit(solution)/shard_map/ppermute | solution.py:162
  170.6 4.0 collective-permute-start.46
  174.6 1.9 collective-permute-start.47
  176.6 34.7 %collective-permute-start.14 = (bf16[5,176,256]{2,1,0:T(8,128)(2,1)}, bf16[5,176,256]{2,1,0:T(8,128)(2,1)S(1)}, u32[]{:S(2)}, u32[]{:S(2)}) collective-permute-start(bf16[5,176,256]{2,1,0:T(8,128)(2,1)} %get-tuple-element.84), channel_id=1, source_target_pairs={{0,1},{1,2},{2,3},{3,4},{4,5},{5,6},{6,7},{7,0},{8,9},{9,10},{10,1... | collective-permute-start | bytes 1351688 | tf_op jit(solution)/shard_map/ppermute | solution.py:162
  212.1 7.6 %collective-permute-start.15 = (bf16[5,176,256]{2,1,0:T(8,128)(2,1)S(1)}, bf16[5,176,256]{2,1,0:T(8,128)(2,1)S(1)}, u32[]{:S(2)}, u32[]{:S(2)}) collective-permute-start(bf16[5,176,256]{2,1,0:T(8,128)(2,1)S(1)} %copy-done.61), channel_id=1, source_target_pairs={{0,2},{1,3},{2,4},{3,5},{4,6},{5,7},{6,0},{7,1},{8,10},{9,11},{10,... | collective-permute-start | bytes 1351688 | tf_op jit(solution)/shard_map/ppermute | solution.py:162
  220.5 7.9 %collective-permute-start.16 = (bf16[5,176,256]{2,1,0:T(8,128)(2,1)}, bf16[5,176,256]{2,1,0:T(8,128)(2,1)S(1)}, u32[]{:S(2)}, u32[]{:S(2)}) collective-permute-start(bf16[5,176,256]{2,1,0:T(8,128)(2,1)} %get-tuple-element.86), channel_id=1, source_target_pairs={{0,3},{1,4},{2,5},{3,6},{4,7},{5,0},{6,1},{7,2},{8,11},{9,12},{10,... | collective-permute-start | bytes 1351688 | tf_op jit(solution)/shard_map/ppermute | solution.py:162
  228.5 16.4 %collective-permute-done.48.refs_15_ = bf16[4,176,256]{2,1,0:T(8,128)(2,1)S(1)} collective-permute-done((bf16[4,176,256]{2,1,0:T(8,128)(2,1)S(1)}, bf16[4,176,256]{2,1,0:T(8,128)(2,1)S(1)}, u32[]{:S(2)}, u32[]{:S(2)}) %collective-permute-start.48) | collective-permute-done | bytes 360480 | tf_op jit(solution)/shard_map/ppermute | solution.py:162
  245.2 2.1 collective-permute-start.19
  249.0 21.3 %collective-permute-start.50 = (bf16[9,176,256]{2,1,0:T(8,128)(2,1)}, bf16[9,176,256]{2,1,0:T(8,128)(2,1)S(1)}, u32[]{:S(2)}, u32[]{:S(2)}) collective-permute-start(bf16[9,176,256]{2,1,0:T(8,128)(2,1)} %get-tuple-element.125), channel_id=1, source_target_pairs={{0,2},{1,3},{2,4},{3,5},{4,6},{5,7},{6,0},{7,1},{8,10},{9,11},{10,... | collective-permute-start | bytes 2433032 | tf_op jit(solution)/shard_map/ppermute | solution.py:162
  270.4 18.9 %collective-permute-start.51 = (bf16[9,176,256]{2,1,0:T(8,128)(2,1)S(1)}, bf16[9,176,256]{2,1,0:T(8,128)(2,1)S(1)}, u32[]{:S(2)}, u32[]{:S(2)}) collective-permute-start(bf16[9,176,256]{2,1,0:T(8,128)(2,1)S(1)} %copy-done.60), channel_id=1, source_target_pairs={{0,3},{1,4},{2,5},{3,6},{4,7},{5,0},{6,1},{7,2},{8,11},{9,12},{10,... | collective-permute-start | bytes 2433032 | tf_op jit(solution)/shard_map/ppermute | solution.py:162
  290.0 24.7 %collective-permute-done.19.refs_14_ = bf16[5,176,256]{2,1,0:T(8,128)(2,1)S(1)} collective-permute-done((bf16[5,176,256]{2,1,0:T(8,128)(2,1)}, bf16[5,176,256]{2,1,0:T(8,128)(2,1)S(1)}, u32[]{:S(2)}, u32[]{:S(2)}) %collective-permute-start.19) | collective-permute-done | bytes 450592 | tf_op jit(solution)/shard_map/ppermute | solution.py:162
  314.7 52.8 %collective-permute-start.20 = (bf16[5,176,256]{2,1,0:T(8,128)(2,1)}, bf16[5,176,256]{2,1,0:T(8,128)(2,1)S(1)}, u32[]{:S(2)}, u32[]{:S(2)}) collective-permute-start(bf16[5,176,256]{2,1,0:T(8,128)(2,1)} %get-tuple-element.90), channel_id=1, source_target_pairs={{0,7},{1,0},{2,1},{3,2},{4,3},{5,4},{6,5},{7,6},{8,15},{9,8},{10,9... | collective-permute-start | bytes 1351688 | tf_op jit(solution)/shard_map/ppermute | solution.py:162
  367.5 27.6 %collective-permute-done.20.refs_15_ = bf16[5,176,256]{2,1,0:T(8,128)(2,1)S(1)} collective-permute-done((bf16[5,176,256]{2,1,0:T(8,128)(2,1)}, bf16[5,176,256]{2,1,0:T(8,128)(2,1)S(1)}, u32[]{:S(2)}, u32[]{:S(2)}) %collective-permute-start.20) | collective-permute-done | bytes 450592 | tf_op jit(solution)/shard_map/ppermute | solution.py:162
  395.9 3.0 collective-permute-start.55
  399.0 4.0 collective-permute-start.10
  403.5 27.4 %collective-permute-done.53.refs_13_ = bf16[9,176,256]{2,1,0:T(8,128)(2,1)S(1)} collective-permute-done((bf16[9,176,256]{2,1,0:T(8,128)(2,1)}, bf16[9,176,256]{2,1,0:T(8,128)(2,1)S(1)}, u32[]{:S(2)}, u32[]{:S(2)}) %collective-permute-start.53) | collective-permute-done | bytes 811040 | tf_op jit(solution)/shard_map/ppermute | solution.py:162
  430.9 36.3 %collective-permute-start.12 = (bf16[9,176,256]{2,1,0:T(8,128)(2,1)}, bf16[9,176,256]{2,1,0:T(8,128)(2,1)}, u32[]{:S(2)}, u32[]{:S(2)}) collective-permute-start(bf16[9,176,256]{2,1,0:T(8,128)(2,1)} %get-tuple-element.81), channel_id=1, source_target_pairs={{0,6},{1,7},{2,0},{3,1},{4,2},{5,3},{6,4},{7,5},{8,14},{9,15},{10,... | collective-permute-start | bytes 2433032 | tf_op jit(solution)/shard_map/ppermute | solution.py:162
  467.2 25.3 %collective-permute-done.55.refs_15_ = bf16[9,176,256]{2,1,0:T(8,128)(2,1)S(1)} collective-permute-done((bf16[9,176,256]{2,1,0:T(8,128)(2,1)}, bf16[9,176,256]{2,1,0:T(8,128)(2,1)S(1)}, u32[]{:S(2)}, u32[]{:S(2)}) %collective-permute-start.55) | collective-permute-done | bytes 811040 | tf_op jit(solution)/shard_map/ppermute | solution.py:162
  492.5 25.2 %collective-permute-done.10.refs_12_ = bf16[9,176,256]{2,1,0:T(8,128)(2,1)S(1)} collective-permute-done((bf16[9,176,256]{2,1,0:T(8,128)(2,1)}, bf16[9,176,256]{2,1,0:T(8,128)(2,1)S(1)}, u32[]{:S(2)}, u32[]{:S(2)}) %collective-permute-start.10) | collective-permute-done | bytes 811040 | tf_op jit(solution)/shard_map/ppermute | solution.py:162
  517.8 18.6 %collective-permute-start.8 = (bf16[9,176,256]{2,1,0:T(8,128)(2,1)}, bf16[9,176,256]{2,1,0:T(8,128)(2,1)}, u32[]{:S(2)}, u32[]{:S(2)}) collective-permute-start(bf16[9,176,256]{2,1,0:T(8,128)(2,1)} %get-tuple-element.77), channel_id=1, source_target_pairs={{0,2},{1,3},{2,4},{3,5},{4,6},{5,7},{6,0},{7,1},{8,10},{9,11},{10,... | collective-permute-start | bytes 2433032 | tf_op jit(solution)/shard_map/ppermute | solution.py:162
  536.4 18.3 %collective-permute-start.9 = (bf16[9,176,256]{2,1,0:T(8,128)(2,1)}, bf16[9,176,256]{2,1,0:T(8,128)(2,1)}, u32[]{:S(2)}, u32[]{:S(2)}) collective-permute-start(bf16[9,176,256]{2,1,0:T(8,128)(2,1)} %get-tuple-element.78), channel_id=1, source_target_pairs={{0,3},{1,4},{2,5},{3,6},{4,7},{5,0},{6,1},{7,2},{8,11},{9,12},{10,... | collective-permute-start | bytes 2433032 | tf_op jit(solution)/shard_map/ppermute | solution.py:162
  556.1 1.4 join.1
  557.5 16.5 %all_gather.3 = bf16[64,2048]{1,0:T(8,128)(2,1)S(1)} all-gather(bf16[16,2048]{1,0:T(8,128)(2,1)} %join.1), channel_id=1, replica_groups=mesh['owner'=4,'rows'=8] {'owner'}, dimensions={0}, use_global_device_ids=true | all-gather | bytes 327680 | tf_op jit(solution)/shard_map/all_gather | solution.py:190
  574.1 4.6 shard_map.90.refs_16_
  578.7 8.6 %shard_map.91.refs_16_ = bf16[16,176,2048]{2,1,0:T(8,128)(2,1)} custom-call(s32[1]{0:T(128)} %bitcast.me_ref, f32[16,352]{1,0:T(8,128)} %get-tuple-element.132.refs_0_, f32[16,352]{1,0:T(8,128)} %copy-done, f32[16,352]{1,0:T(8,128)} %copy-done.1, f32[16,352]{1,0:T(8,128)} %copy-done.2, f32[16,352]{1,0:T(8,128)} %copy-done.3, ...), custom_call_target="tpu_custom_call", output_to_operand_aliasing={{}: (17, {})} | custom-call | flops 54067200 | bytes 7208960 | tf_op jit(solution)/shard_map/pallas_call | solution.py:100
  587.4 14.3 %shard_map.93.refs_16_ = bf16[16,176,2048]{2,1,0:T(8,128)(2,1)} custom-call(s32[1]{0:T(128)} %bitcast.me_ref, f32[16,352]{1,0:T(8,128)} %get-tuple-element.132.refs_0_, f32[16,352]{1,0:T(8,128)} %copy-done, f32[16,352]{1,0:T(8,128)} %copy-done.1, f32[16,352]{1,0:T(8,128)} %copy-done.2, f32[16,352]{1,0:T(8,128)} %copy-done.3, f32[16,352]{1,0:T(8,128)} %copy-done.4, ...), custom_call_target="tpu_custom_call" | custom-call | flops 97320960 | bytes 12976128 | tf_op jit(solution)/shard_map/pallas_call | solution.py:100
  601.7 7.5 %shard_map.94.refs_16_ = bf16[16,176,2048]{2,1,0:T(8,128)(2,1)} custom-call(s32[1]{0:T(128)} %bitcast.me_ref, f32[16,352]{1,0:T(8,128)} %get-tuple-element.132.refs_0_, f32[16,352]{1,0:T(8,128)} %copy-done, f32[16,352]{1,0:T(8,128)} %copy-done.1, f32[16,352]{1,0:T(8,128)} %copy-done.2, f32[16,352]{1,0:T(8,128)} %copy-done.3, ...), custom_call_target="tpu_custom_call", output_to_operand_aliasing={{}: (17, {})} | custom-call | flops 43253760 | bytes 5767168 | tf_op jit(solution)/shard_map/pallas_call | solution.py:100
  609.1 4.7 shard_map.95.refs_16_
  613.9 3.4 shard_map.96
  617.3 14.0 %shard_map.92 = bf16[16,176,2048]{2,1,0:T(8,128)(2,1)} custom-call(s32[1]{0:T(128)} %bitcast.me_ref, f32[16,352]{1,0:T(8,128)} %get-tuple-element.132.refs_0_, f32[16,352]{1,0:T(8,128)} %copy-done, f32[16,352]{1,0:T(8,128)} %copy-done.1, f32[16,352]{1,0:T(8,128)} %copy-done.2, f32[16,352]{1,0:T(8,128)} %copy-done.3, ...), custom_call_target="tpu_custom_call", output_to_operand_aliasing={{}: (17, {})} | custom-call | flops 97320960 | bytes 12976128 | tf_op jit(solution)/shard_map/pallas_call | solution.py:100
  (221 shorter events, 18.4 us)
Async XLA Ops:
  58.4 9.7 %collective-permute-start = (f32[16,352]{1,0:T(8,128)S(1)}, f32[16,352]{1,0:T(8,128)S(1)}, u32[]{:S(2)}, u32[]{:S(2)}) collective-permute-start(f32[16,352]{1,0:T(8,128)S(1)} %pad_maximum_fusion.1), channel_id=1, source_target_pairs={{0,1},{1,2},{2,3},{3,4},{4,5},{5,6},{6,7},{7,0},{8,9},{9,10},{10,1... | collective-permute-start | bytes 67592 | tf_op jit(solution)/shard_map/ppermute | solution.py:162
  59.8 9.5 %collective-permute-start.1 = (f32[16,352]{1,0:T(8,128)S(1)}, f32[16,352]{1,0:T(8,128)S(1)}, u32[]{:S(2)}, u32[]{:S(2)}) collective-permute-start(f32[16,352]{1,0:T(8,128)S(1)} %pad_maximum_fusion.2), channel_id=1, source_target_pairs={{0,2},{1,3},{2,4},{3,5},{4,6},{5,7},{6,0},{7,1},{8,10},{9,11},{10,... | collective-permute-start | bytes 67592 | tf_op jit(solution)/shard_map/ppermute | solution.py:162
  61.1 9.8 %collective-permute-start.2 = (f32[16,352]{1,0:T(8,128)S(1)}, f32[16,352]{1,0:T(8,128)S(1)}, u32[]{:S(2)}, u32[]{:S(2)}) collective-permute-start(f32[16,352]{1,0:T(8,128)S(1)} %pad_maximum_fusion.3), channel_id=1, source_target_pairs={{0,3},{1,4},{2,5},{3,6},{4,7},{5,0},{6,1},{7,2},{8,11},{9,12},{10,... | collective-permute-start | bytes 67592 | tf_op jit(solution)/shard_map/ppermute | solution.py:162
  62.1 8.8 %collective-permute-start.3 = (f32[16,352]{1,0:T(8,128)S(1)}, f32[16,352]{1,0:T(8,128)S(1)}, u32[]{:S(2)}, u32[]{:S(2)}) collective-permute-start(f32[16,352]{1,0:T(8,128)S(1)} %pad_maximum_fusion.4), channel_id=1, source_target_pairs={{0,4},{1,5},{2,6},{3,7},{4,0},{5,1},{6,2},{7,3},{8,12},{9,13},{10,... | collective-permute-start | bytes 67592 | tf_op jit(solution)/shard_map/ppermute | solution.py:162
  63.6 3.8 collective-permute-start.56
  67.3 3.9 collective-permute-start.4
  68.2 505.9 %copy-start = (f32[16,352]{1,0:T(8,128)}, f32[16,352]{1,0:T(8,128)S(1)}, u32[]{:S(2)}) copy-start(f32[16,352]{1,0:T(8,128)S(1)} %collective-permute-done.refs_1_) | copy-start | bytes 67588
  68.2 7.3 %collective-permute-start.5 = (f32[16,352]{1,0:T(8,128)S(1)}, f32[16,352]{1,0:T(8,128)S(1)}, u32[]{:S(2)}, u32[]{:S(2)}) collective-permute-start(f32[16,352]{1,0:T(8,128)S(1)} %pad_maximum_fusion.6), channel_id=1, source_target_pairs={{0,6},{1,7},{2,0},{3,1},{4,2},{5,3},{6,4},{7,5},{8,14},{9,15},{10,... | collective-permute-start | bytes 67592 | tf_op jit(solution)/shard_map/ppermute | solution.py:162
  69.2 504.8 %copy-start.1 = (f32[16,352]{1,0:T(8,128)}, f32[16,352]{1,0:T(8,128)S(1)}, u32[]{:S(2)}) copy-start(f32[16,352]{1,0:T(8,128)S(1)} %collective-permute-done.1.refs_2_) | copy-start | bytes 67588
  69.2 6.8 %collective-permute-start.6 = (f32[16,352]{1,0:T(8,128)S(1)}, f32[16,352]{1,0:T(8,128)S(1)}, u32[]{:S(2)}, u32[]{:S(2)}) collective-permute-start(f32[16,352]{1,0:T(8,128)S(1)} %pad_maximum_fusion.7), channel_id=1, source_target_pairs={{0,7},{1,0},{2,1},{3,2},{4,3},{5,4},{6,5},{7,6},{8,15},{9,8},{10,9... | collective-permute-start | bytes 67592 | tf_op jit(solution)/shard_map/ppermute | solution.py:162
  70.9 503.1 %copy-start.2 = (f32[16,352]{1,0:T(8,128)}, f32[16,352]{1,0:T(8,128)S(1)}, u32[]{:S(2)}) copy-start(f32[16,352]{1,0:T(8,128)S(1)} %collective-permute-done.2.refs_3_) | copy-start | bytes 67588
  70.9 19.1 %collective-permute-start.28 = (bf16[1,176,256]{2,1,0:T(8,128)(2,1)}, bf16[1,176,256]{2,1,0:T(8,128)(2,1)S(1)}, u32[]{:S(2)}, u32[]{:S(2)}) collective-permute-start(bf16[1,176,256]{2,1,0:T(8,128)(2,1)} %get-tuple-element.100), channel_id=1, source_target_pairs={{0,1},{1,2},{2,3},{3,4},{4,5},{5,6},{6,7},{7,0},{8,9},{9,10},{10,1... | collective-permute-start | bytes 270344 | tf_op jit(solution)/shard_map/ppermute | solution.py:162
  70.9 503.1 %copy-start.3 = (f32[16,352]{1,0:T(8,128)}, f32[16,352]{1,0:T(8,128)S(1)}, u32[]{:S(2)}) copy-start(f32[16,352]{1,0:T(8,128)S(1)} %collective-permute-done.3.refs_4_) | copy-start | bytes 67588
  70.9 19.1 %collective-permute-start.29 = (bf16[1,176,256]{2,1,0:T(8,128)(2,1)}, bf16[1,176,256]{2,1,0:T(8,128)(2,1)S(1)}, u32[]{:S(2)}, u32[]{:S(2)}) collective-permute-start(bf16[1,176,256]{2,1,0:T(8,128)(2,1)} %get-tuple-element.101), channel_id=1, source_target_pairs={{0,2},{1,3},{2,4},{3,5},{4,6},{5,7},{6,0},{7,1},{8,10},{9,11},{10,... | collective-permute-start | bytes 270344 | tf_op jit(solution)/shard_map/ppermute | solution.py:162
  71.2 21.5 %collective-permute-start.30 = (bf16[1,176,256]{2,1,0:T(8,128)(2,1)}, bf16[1,176,256]{2,1,0:T(8,128)(2,1)S(1)}, u32[]{:S(2)}, u32[]{:S(2)}) collective-permute-start(bf16[1,176,256]{2,1,0:T(8,128)(2,1)} %get-tuple-element.102), channel_id=1, source_target_pairs={{0,3},{1,4},{2,5},{3,6},{4,7},{5,0},{6,1},{7,2},{8,11},{9,12},{10,... | collective-permute-start | bytes 270344 | tf_op jit(solution)/shard_map/ppermute | solution.py:162
  75.5 18.0 %collective-permute-start.31 = (bf16[1,176,256]{2,1,0:T(8,128)(2,1)}, bf16[1,176,256]{2,1,0:T(8,128)(2,1)S(1)}, u32[]{:S(2)}, u32[]{:S(2)}) collective-permute-start(bf16[1,176,256]{2,1,0:T(8,128)(2,1)} %get-tuple-element.103), channel_id=1, source_target_pairs={{0,4},{1,5},{2,6},{3,7},{4,0},{5,1},{6,2},{7,3},{8,12},{9,13},{10,... | collective-permute-start | bytes 270344 | tf_op jit(solution)/shard_map/ppermute | solution.py:162
  76.1 4.3 collective-permute-start.57
  80.4 3.2 collective-permute-start.58
  83.6 2.9 collective-permute-start.59
  86.5 10.5 %collective-permute-start.32 = (bf16[1,176,256]{2,1,0:T(8,128)(2,1)}, bf16[1,176,256]{2,1,0:T(8,128)(2,1)S(1)}, u32[]{:S(2)}, u32[]{:S(2)}) collective-permute-start(bf16[1,176,256]{2,1,0:T(8,128)(2,1)} %get-tuple-element.104), channel_id=1, source_target_pairs={{0,5},{1,6},{2,7},{3,0},{4,1},{5,2},{6,3},{7,4},{8,13},{9,14},{10,... | collective-permute-start | bytes 270344 | tf_op jit(solution)/shard_map/ppermute | solution.py:162
  90.0 7.7 %collective-permute-start.33 = (bf16[1,176,256]{2,1,0:T(8,128)(2,1)}, bf16[1,176,256]{2,1,0:T(8,128)(2,1)S(1)}, u32[]{:S(2)}, u32[]{:S(2)}) collective-permute-start(bf16[1,176,256]{2,1,0:T(8,128)(2,1)} %get-tuple-element.105), channel_id=1, source_target_pairs={{0,6},{1,7},{2,0},{3,1},{4,2},{5,3},{6,4},{7,5},{8,14},{9,15},{10,... | collective-permute-start | bytes 270344 | tf_op jit(solution)/shard_map/ppermute | solution.py:162
  91.3 22.3 %collective-permute-start.35 = (bf16[2,176,256]{2,1,0:T(8,128)(2,1)}, bf16[2,176,256]{2,1,0:T(8,128)(2,1)S(1)}, u32[]{:S(2)}, u32[]{:S(2)}) collective-permute-start(bf16[2,176,256]{2,1,0:T(8,128)(2,1)} %get-tuple-element.108), channel_id=1, source_target_pairs={{0,1},{1,2},{2,3},{3,4},{4,5},{5,6},{6,7},{7,0},{8,9},{9,10},{10,1... | collective-permute-start | bytes 540680 | tf_op jit(solution)/shard_map/ppermute | solution.py:162
  93.4 20.3 %collective-permute-start.36 = (bf16[2,176,256]{2,1,0:T(8,128)(2,1)}, bf16[2,176,256]{2,1,0:T(8,128)(2,1)S(1)}, u32[]{:S(2)}, u32[]{:S(2)}) collective-permute-start(bf16[2,176,256]{2,1,0:T(8,128)(2,1)} %get-tuple-element.109), channel_id=1, source_target_pairs={{0,2},{1,3},{2,4},{3,5},{4,6},{5,7},{6,0},{7,1},{8,10},{9,11},{10,... | collective-permute-start | bytes 540680 | tf_op jit(solution)/shard_map/ppermute | solution.py:162
  93.5 23.3 %collective-permute-start.37 = (bf16[2,176,256]{2,1,0:T(8,128)(2,1)}, bf16[2,176,256]{2,1,0:T(8,128)(2,1)S(1)}, u32[]{:S(2)}, u32[]{:S(2)}) collective-permute-start(bf16[2,176,256]{2,1,0:T(8,128)(2,1)} %get-tuple-element.110), channel_id=1, source_target_pairs={{0,3},{1,4},{2,5},{3,6},{4,7},{5,0},{6,1},{7,2},{8,11},{9,12},{10,... | collective-permute-start | bytes 540680 | tf_op jit(solution)/shard_map/ppermute | solution.py:162
  97.7 19.3 %collective-permute-start.38 = (bf16[2,176,256]{2,1,0:T(8,128)(2,1)}, bf16[2,176,256]{2,1,0:T(8,128)(2,1)S(1)}, u32[]{:S(2)}, u32[]{:S(2)}) collective-permute-start(bf16[2,176,256]{2,1,0:T(8,128)(2,1)} %get-tuple-element.111), channel_id=1, source_target_pairs={{0,4},{1,5},{2,6},{3,7},{4,0},{5,1},{6,2},{7,3},{8,12},{9,13},{10,... | collective-permute-start | bytes 540680 | tf_op jit(solution)/shard_map/ppermute | solution.py:162
  97.7 15.2 %collective-permute-start.34 = (bf16[1,176,256]{2,1,0:T(8,128)(2,1)}, bf16[1,176,256]{2,1,0:T(8,128)(2,1)S(1)}, u32[]{:S(2)}, u32[]{:S(2)}) collective-permute-start(bf16[1,176,256]{2,1,0:T(8,128)(2,1)} %get-tuple-element.106), channel_id=1, source_target_pairs={{0,7},{1,0},{2,1},{3,2},{4,3},{5,4},{6,5},{7,6},{8,15},{9,8},{10,9... | collective-permute-start | bytes 270344 | tf_op jit(solution)/shard_map/ppermute | solution.py:162
  113.6 5.8 collective-permute-start.39
  113.6 11.3 %collective-permute-start.40 = (bf16[2,176,256]{2,1,0:T(8,128)(2,1)}, bf16[2,176,256]{2,1,0:T(8,128)(2,1)S(1)}, u32[]{:S(2)}, u32[]{:S(2)}) collective-permute-start(bf16[2,176,256]{2,1,0:T(8,128)(2,1)} %get-tuple-element.113), channel_id=1, source_target_pairs={{0,6},{1,7},{2,0},{3,1},{4,2},{5,3},{6,4},{7,5},{8,14},{9,15},{10,... | collective-permute-start | bytes 540680 | tf_op jit(solution)/shard_map/ppermute | solution.py:162
  113.7 11.7 %collective-permute-start.41 = (bf16[2,176,256]{2,1,0:T(8,128)(2,1)}, bf16[2,176,256]{2,1,0:T(8,128)(2,1)S(1)}, u32[]{:S(2)}, u32[]{:S(2)}) collective-permute-start(bf16[2,176,256]{2,1,0:T(8,128)(2,1)} %get-tuple-element.114), channel_id=1, source_target_pairs={{0,7},{1,0},{2,1},{3,2},{4,3},{5,4},{6,5},{7,6},{8,15},{9,8},{10,9... | collective-permute-start | bytes 540680 | tf_op jit(solution)/shard_map/ppermute | solution.py:162
  116.8 18.0 %collective-permute-start.21 = (bf16[2,176,256]{2,1,0:T(8,128)(2,1)}, bf16[2,176,256]{2,1,0:T(8,128)(2,1)S(1)}, u32[]{:S(2)}, u32[]{:S(2)}) collective-permute-start(bf16[2,176,256]{2,1,0:T(8,128)(2,1)} %get-tuple-element.92), channel_id=1, source_target_pairs={{0,1},{1,2},{2,3},{3,4},{4,5},{5,6},{6,7},{7,0},{8,9},{9,10},{10,1... | collective-permute-start | bytes 540680 | tf_op jit(solution)/shard_map/ppermute | solution.py:162
  117.0 17.8 %collective-permute-start.22 = (bf16[2,176,256]{2,1,0:T(8,128)(2,1)}, bf16[2,176,256]{2,1,0:T(8,128)(2,1)S(1)}, u32[]{:S(2)}, u32[]{:S(2)}) collective-permute-start(bf16[2,176,256]{2,1,0:T(8,128)(2,1)} %get-tuple-element.93), channel_id=1, source_target_pairs={{0,2},{1,3},{2,4},{3,5},{4,6},{5,7},{6,0},{7,1},{8,10},{9,11},{10,... | collective-permute-start | bytes 540680 | tf_op jit(solution)/shard_map/ppermute | solution.py:162
  119.4 15.7 %collective-permute-start.23 = (bf16[2,176,256]{2,1,0:T(8,128)(2,1)}, bf16[2,176,256]{2,1,0:T(8,128)(2,1)S(1)}, u32[]{:S(2)}, u32[]{:S(2)}) collective-permute-start(bf16[2,176,256]{2,1,0:T(8,128)(2,1)} %get-tuple-element.94), channel_id=1, source_target_pairs={{0,3},{1,4},{2,5},{3,6},{4,7},{5,0},{6,1},{7,2},{8,11},{9,12},{10,... | collective-permute-start | bytes 540680 | tf_op jit(solution)/shard_map/ppermute | solution.py:162
  124.9 14.0 %collective-permute-start.24 = (bf16[2,176,256]{2,1,0:T(8,128)(2,1)}, bf16[2,176,256]{2,1,0:T(8,128)(2,1)S(1)}, u32[]{:S(2)}, u32[]{:S(2)}) collective-permute-start(bf16[2,176,256]{2,1,0:T(8,128)(2,1)} %get-tuple-element.95), channel_id=1, source_target_pairs={{0,4},{1,5},{2,6},{3,7},{4,0},{5,1},{6,2},{7,3},{8,12},{9,13},{10,... | collective-permute-start | bytes 540680 | tf_op jit(solution)/shard_map/ppermute | solution.py:162
  125.5 49.2 %collective-permute-start.42 = (bf16[4,176,256]{2,1,0:T(8,128)(2,1)}, bf16[4,176,256]{2,1,0:T(8,128)(2,1)S(1)}, u32[]{:S(2)}, u32[]{:S(2)}) collective-permute-start(bf16[4,176,256]{2,1,0:T(8,128)(2,1)} %get-tuple-element.116), channel_id=1, source_target_pairs={{0,1},{1,2},{2,3},{3,4},{4,5},{5,6},{6,7},{7,0},{8,9},{9,10},{10,1... | collective-permute-start | bytes 1081352 | tf_op jit(solution)/shard_map/ppermute | solution.py:162
  134.8 41.7 %collective-permute-start.43 = (bf16[4,176,256]{2,1,0:T(8,128)(2,1)}, bf16[4,176,256]{2,1,0:T(8,128)(2,1)S(1)}, u32[]{:S(2)}, u32[]{:S(2)}) collective-permute-start(bf16[4,176,256]{2,1,0:T(8,128)(2,1)} %get-tuple-element.117), channel_id=1, source_target_pairs={{0,2},{1,3},{2,4},{3,5},{4,6},{5,7},{6,0},{7,1},{8,10},{9,11},{10,... | collective-permute-start | bytes 1081352 | tf_op jit(solution)/shard_map/ppermute | solution.py:162
  134.8 17.5 %collective-permute-start.25 = (bf16[2,176,256]{2,1,0:T(8,128)(2,1)}, bf16[2,176,256]{2,1,0:T(8,128)(2,1)S(1)}, u32[]{:S(2)}, u32[]{:S(2)}) collective-permute-start(bf16[2,176,256]{2,1,0:T(8,128)(2,1)} %get-tuple-element.96), channel_id=1, source_target_pairs={{0,5},{1,6},{2,7},{3,0},{4,1},{5,2},{6,3},{7,4},{8,13},{9,14},{10,... | collective-permute-start | bytes 540680 | tf_op jit(solution)/shard_map/ppermute | solution.py:162
  135.1 20.1 %collective-permute-start.26 = (bf16[2,176,256]{2,1,0:T(8,128)(2,1)}, bf16[2,176,256]{2,1,0:T(8,128)(2,1)S(1)}, u32[]{:S(2)}, u32[]{:S(2)}) collective-permute-start(bf16[2,176,256]{2,1,0:T(8,128)(2,1)} %get-tuple-element.97), channel_id=1, source_target_pairs={{0,6},{1,7},{2,0},{3,1},{4,2},{5,3},{6,4},{7,5},{8,14},{9,15},{10,... | collective-permute-start | bytes 540680 | tf_op jit(solution)/shard_map/ppermute | solution.py:162
  138.9 31.7 %collective-permute-start.27 = (bf16[2,176,256]{2,1,0:T(8,128)(2,1)S(1)}, bf16[2,176,256]{2,1,0:T(8,128)(2,1)S(1)}, u32[]{:S(2)}, u32[]{:S(2)}) collective-permute-start(bf16[2,176,256]{2,1,0:T(8,128)(2,1)S(1)} %copy-done.63), channel_id=1, source_target_pairs={{0,7},{1,0},{2,1},{3,2},{4,3},{5,4},{6,5},{7,6},{8,15},{9,8},{10,9... | collective-permute-start | bytes 540680 | tf_op jit(solution)/shard_map/ppermute | solution.py:162
  152.3 24.3 %collective-permute-start.44 = (bf16[4,176,256]{2,1,0:T(8,128)(2,1)}, bf16[4,176,256]{2,1,0:T(8,128)(2,1)S(1)}, u32[]{:S(2)}, u32[]{:S(2)}) collective-permute-start(bf16[4,176,256]{2,1,0:T(8,128)(2,1)} %get-tuple-element.118), channel_id=1, source_target_pairs={{0,3},{1,4},{2,5},{3,6},{4,7},{5,0},{6,1},{7,2},{8,11},{9,12},{10,... | collective-permute-start | bytes 1081352 | tf_op jit(solution)/shard_map/ppermute | solution.py:162
  155.3 56.1 %collective-permute-start.45 = (bf16[4,176,256]{2,1,0:T(8,128)(2,1)}, bf16[4,176,256]{2,1,0:T(8,128)(2,1)S(1)}, u32[]{:S(2)}, u32[]{:S(2)}) collective-permute-start(bf16[4,176,256]{2,1,0:T(8,128)(2,1)} %get-tuple-element.119), channel_id=1, source_target_pairs={{0,4},{1,5},{2,6},{3,7},{4,0},{5,1},{6,2},{7,3},{8,12},{9,13},{10,... | collective-permute-start | bytes 1081352 | tf_op jit(solution)/shard_map/ppermute | solution.py:162
  170.6 49.1 %collective-permute-start.46 = (bf16[4,176,256]{2,1,0:T(8,128)(2,1)}, bf16[4,176,256]{2,1,0:T(8,128)(2,1)S(1)}, u32[]{:S(2)}, u32[]{:S(2)}) collective-permute-start(bf16[4,176,256]{2,1,0:T(8,128)(2,1)} %get-tuple-element.120), channel_id=1, source_target_pairs={{0,5},{1,6},{2,7},{3,0},{4,1},{5,2},{6,3},{7,4},{8,13},{9,14},{10,... | collective-permute-start | bytes 1081352 | tf_op jit(solution)/shard_map/ppermute | solution.py:162
  174.6 53.8 %collective-permute-start.47 = (bf16[4,176,256]{2,1,0:T(8,128)(2,1)}, bf16[4,176,256]{2,1,0:T(8,128)(2,1)S(1)}, u32[]{:S(2)}, u32[]{:S(2)}) collective-permute-start(bf16[4,176,256]{2,1,0:T(8,128)(2,1)} %get-tuple-element.121), channel_id=1, source_target_pairs={{0,6},{1,7},{2,0},{3,1},{4,2},{5,3},{6,4},{7,5},{8,14},{9,15},{10,... | collective-permute-start | bytes 1081352 | tf_op jit(solution)/shard_map/ppermute | solution.py:162
  176.5 68.3 %collective-permute-start.48 = (bf16[4,176,256]{2,1,0:T(8,128)(2,1)S(1)}, bf16[4,176,256]{2,1,0:T(8,128)(2,1)S(1)}, u32[]{:S(2)}, u32[]{:S(2)}) collective-permute-start(bf16[4,176,256]{2,1,0:T(8,128)(2,1)S(1)} %copy-done.62), channel_id=1, source_target_pairs={{0,7},{1,0},{2,1},{3,2},{4,3},{5,4},{6,5},{7,6},{8,15},{9,8},{10,9... | collective-permute-start | bytes 1081352 | tf_op jit(solution)/shard_map/ppermute | solution.py:162
  176.6 68.5 %collective-permute-start.14 = (bf16[5,176,256]{2,1,0:T(8,128)(2,1)}, bf16[5,176,256]{2,1,0:T(8,128)(2,1)S(1)}, u32[]{:S(2)}, u32[]{:S(2)}) collective-permute-start(bf16[5,176,256]{2,1,0:T(8,128)(2,1)} %get-tuple-element.84), channel_id=1, source_target_pairs={{0,1},{1,2},{2,3},{3,4},{4,5},{5,6},{6,7},{7,0},{8,9},{9,10},{10,1... | collective-permute-start | bytes 1351688 | tf_op jit(solution)/shard_map/ppermute | solution.py:162
  212.1 35.1 %collective-permute-start.15 = (bf16[5,176,256]{2,1,0:T(8,128)(2,1)S(1)}, bf16[5,176,256]{2,1,0:T(8,128)(2,1)S(1)}, u32[]{:S(2)}, u32[]{:S(2)}) collective-permute-start(bf16[5,176,256]{2,1,0:T(8,128)(2,1)S(1)} %copy-done.61), channel_id=1, source_target_pairs={{0,2},{1,3},{2,4},{3,5},{4,6},{5,7},{6,0},{7,1},{8,10},{9,11},{10,... | collective-permute-start | bytes 1351688 | tf_op jit(solution)/shard_map/ppermute | solution.py:162
  220.5 27.7 %collective-permute-start.16 = (bf16[5,176,256]{2,1,0:T(8,128)(2,1)}, bf16[5,176,256]{2,1,0:T(8,128)(2,1)S(1)}, u32[]{:S(2)}, u32[]{:S(2)}) collective-permute-start(bf16[5,176,256]{2,1,0:T(8,128)(2,1)} %get-tuple-element.86), channel_id=1, source_target_pairs={{0,3},{1,4},{2,5},{3,6},{4,7},{5,0},{6,1},{7,2},{8,11},{9,12},{10,... | collective-permute-start | bytes 1351688 | tf_op jit(solution)/shard_map/ppermute | solution.py:162
  228.5 41.9 %collective-permute-start.17 = (bf16[5,176,256]{2,1,0:T(8,128)(2,1)}, bf16[5,176,256]{2,1,0:T(8,128)(2,1)S(1)}, u32[]{:S(2)}, u32[]{:S(2)}) collective-permute-start(bf16[5,176,256]{2,1,0:T(8,128)(2,1)} %get-tuple-element.87), channel_id=1, source_target_pairs={{0,4},{1,5},{2,6},{3,7},{4,0},{5,1},{6,2},{7,3},{8,12},{9,13},{10,... | collective-permute-start | bytes 1351688 | tf_op jit(solution)/shard_map/ppermute | solution.py:162
  244.9 44.4 %collective-permute-start.18 = (bf16[5,176,256]{2,1,0:T(8,128)(2,1)}, bf16[5,176,256]{2,1,0:T(8,128)(2,1)S(1)}, u32[]{:S(2)}, u32[]{:S(2)}) collective-permute-start(bf16[5,176,256]{2,1,0:T(8,128)(2,1)} %get-tuple-element.88), channel_id=1, source_target_pairs={{0,5},{1,6},{2,7},{3,0},{4,1},{5,2},{6,3},{7,4},{8,13},{9,14},{10,... | collective-permute-start | bytes 1351688 | tf_op jit(solution)/shard_map/ppermute | solution.py:162
  245.2 69.5 %collective-permute-start.19 = (bf16[5,176,256]{2,1,0:T(8,128)(2,1)}, bf16[5,176,256]{2,1,0:T(8,128)(2,1)S(1)}, u32[]{:S(2)}, u32[]{:S(2)}) collective-permute-start(bf16[5,176,256]{2,1,0:T(8,128)(2,1)} %get-tuple-element.89), channel_id=1, source_target_pairs={{0,6},{1,7},{2,0},{3,1},{4,2},{5,3},{6,4},{7,5},{8,14},{9,15},{10,... | collective-permute-start | bytes 1351688 | tf_op jit(solution)/shard_map/ppermute | solution.py:162
  247.3 148.6 %collective-permute-start.49 = (bf16[9,176,256]{2,1,0:T(8,128)(2,1)}, bf16[9,176,256]{2,1,0:T(8,128)(2,1)S(1)}, u32[]{:S(2)}, u32[]{:S(2)}) collective-permute-start(bf16[9,176,256]{2,1,0:T(8,128)(2,1)} %get-tuple-element.124), channel_id=1, source_target_pairs={{0,1},{1,2},{2,3},{3,4},{4,5},{5,6},{6,7},{7,0},{8,9},{9,10},{10,1... | collective-permute-start | bytes 2433032 | tf_op jit(solution)/shard_map/ppermute | solution.py:162
  249.0 146.9 %collective-permute-start.50 = (bf16[9,176,256]{2,1,0:T(8,128)(2,1)}, bf16[9,176,256]{2,1,0:T(8,128)(2,1)S(1)}, u32[]{:S(2)}, u32[]{:S(2)}) collective-permute-start(bf16[9,176,256]{2,1,0:T(8,128)(2,1)} %get-tuple-element.125), channel_id=1, source_target_pairs={{0,2},{1,3},{2,4},{3,5},{4,6},{5,7},{6,0},{7,1},{8,10},{9,11},{10,... | collective-permute-start | bytes 2433032 | tf_op jit(solution)/shard_map/ppermute | solution.py:162
  270.4 128.6 %collective-permute-start.51 = (bf16[9,176,256]{2,1,0:T(8,128)(2,1)S(1)}, bf16[9,176,256]{2,1,0:T(8,128)(2,1)S(1)}, u32[]{:S(2)}, u32[]{:S(2)}) collective-permute-start(bf16[9,176,256]{2,1,0:T(8,128)(2,1)S(1)} %copy-done.60), channel_id=1, source_target_pairs={{0,3},{1,4},{2,5},{3,6},{4,7},{5,0},{6,1},{7,2},{8,11},{9,12},{10,... | collective-permute-start | bytes 2433032 | tf_op jit(solution)/shard_map/ppermute | solution.py:162
  290.0 113.0 %collective-permute-start.52 = (bf16[9,176,256]{2,1,0:T(8,128)(2,1)S(1)}, bf16[9,176,256]{2,1,0:T(8,128)(2,1)S(1)}, u32[]{:S(2)}, u32[]{:S(2)}) collective-permute-start(bf16[9,176,256]{2,1,0:T(8,128)(2,1)S(1)} %copy-done.59), channel_id=1, source_target_pairs={{0,4},{1,5},{2,6},{3,7},{4,0},{5,1},{6,2},{7,3},{8,12},{9,13},{10,... | collective-permute-start | bytes 2433032 | tf_op jit(solution)/shard_map/ppermute | solution.py:162
  314.7 80.4 %collective-permute-start.20 = (bf16[5,176,256]{2,1,0:T(8,128)(2,1)}, bf16[5,176,256]{2,1,0:T(8,128)(2,1)S(1)}, u32[]{:S(2)}, u32[]{:S(2)}) collective-permute-start(bf16[5,176,256]{2,1,0:T(8,128)(2,1)} %get-tuple-element.90), channel_id=1, source_target_pairs={{0,7},{1,0},{2,1},{3,2},{4,3},{5,4},{6,5},{7,6},{8,15},{9,8},{10,9... | collective-permute-start | bytes 1351688 | tf_op jit(solution)/shard_map/ppermute | solution.py:162
  395.9 35.0 %collective-permute-start.53 = (bf16[9,176,256]{2,1,0:T(8,128)(2,1)}, bf16[9,176,256]{2,1,0:T(8,128)(2,1)S(1)}, u32[]{:S(2)}, u32[]{:S(2)}) collective-permute-start(bf16[9,176,256]{2,1,0:T(8,128)(2,1)} %get-tuple-element.128), channel_id=1, source_target_pairs={{0,5},{1,6},{2,7},{3,0},{4,1},{5,2},{6,3},{7,4},{8,13},{9,14},{10,... | collective-permute-start | bytes 2433032 | tf_op jit(solution)/shard_map/ppermute | solution.py:162
  395.9 71.3 %collective-permute-start.54 = (bf16[9,176,256]{2,1,0:T(8,128)(2,1)}, bf16[9,176,256]{2,1,0:T(8,128)(2,1)S(1)}, u32[]{:S(2)}, u32[]{:S(2)}) collective-permute-start(bf16[9,176,256]{2,1,0:T(8,128)(2,1)} %get-tuple-element.129), channel_id=1, source_target_pairs={{0,6},{1,7},{2,0},{3,1},{4,2},{5,3},{6,4},{7,5},{8,14},{9,15},{10,... | collective-permute-start | bytes 2433032 | tf_op jit(solution)/shard_map/ppermute | solution.py:162
  395.9 96.6 %collective-permute-start.55 = (bf16[9,176,256]{2,1,0:T(8,128)(2,1)}, bf16[9,176,256]{2,1,0:T(8,128)(2,1)S(1)}, u32[]{:S(2)}, u32[]{:S(2)}) collective-permute-start(bf16[9,176,256]{2,1,0:T(8,128)(2,1)} %get-tuple-element.130), channel_id=1, source_target_pairs={{0,7},{1,0},{2,1},{3,2},{4,3},{5,4},{6,5},{7,6},{8,15},{9,8},{10,9... | collective-permute-start | bytes 2433032 | tf_op jit(solution)/shard_map/ppermute | solution.py:162
  399.0 118.7 %collective-permute-start.10 = (bf16[9,176,256]{2,1,0:T(8,128)(2,1)}, bf16[9,176,256]{2,1,0:T(8,128)(2,1)S(1)}, u32[]{:S(2)}, u32[]{:S(2)}) collective-permute-start(bf16[9,176,256]{2,1,0:T(8,128)(2,1)} %get-tuple-element.79), channel_id=1, source_target_pairs={{0,4},{1,5},{2,6},{3,7},{4,0},{5,1},{6,2},{7,3},{8,12},{9,13},{10,... | collective-permute-start | bytes 2433032 | tf_op jit(solution)/shard_map/ppermute | solution.py:162
  403.1 133.3 %collective-permute-start.11 = (bf16[9,176,256]{2,1,0:T(8,128)(2,1)}, bf16[9,176,256]{2,1,0:T(8,128)(2,1)S(1)}, u32[]{:S(2)}, u32[]{:S(2)}) collective-permute-start(bf16[9,176,256]{2,1,0:T(8,128)(2,1)} %get-tuple-element.80), channel_id=1, source_target_pairs={{0,5},{1,6},{2,7},{3,0},{4,1},{5,2},{6,3},{7,4},{8,13},{9,14},{10,... | collective-permute-start | bytes 2433032 | tf_op jit(solution)/shard_map/ppermute | solution.py:162
  430.9 186.4 %collective-permute-start.12 = (bf16[9,176,256]{2,1,0:T(8,128)(2,1)}, bf16[9,176,256]{2,1,0:T(8,128)(2,1)}, u32[]{:S(2)}, u32[]{:S(2)}) collective-permute-start(bf16[9,176,256]{2,1,0:T(8,128)(2,1)} %get-tuple-element.81), channel_id=1, source_target_pairs={{0,6},{1,7},{2,0},{3,1},{4,2},{5,3},{6,4},{7,5},{8,14},{9,15},{10,... | collective-permute-start | bytes 2433032 | tf_op jit(solution)/shard_map/ppermute | solution.py:162
  467.2 150.1 %collective-permute-start.13 = (bf16[9,176,256]{2,1,0:T(8,128)(2,1)}, bf16[9,176,256]{2,1,0:T(8,128)(2,1)}, u32[]{:S(2)}, u32[]{:S(2)}) collective-permute-start(bf16[9,176,256]{2,1,0:T(8,128)(2,1)} %get-tuple-element.82), channel_id=1, source_target_pairs={{0,7},{1,0},{2,1},{3,2},{4,3},{5,4},{6,5},{7,6},{8,15},{9,8},{10,9... | collective-permute-start | bytes 2433032 | tf_op jit(solution)/shard_map/ppermute | solution.py:162
  492.5 124.8 %collective-permute-start.7 = (bf16[9,176,256]{2,1,0:T(8,128)(2,1)}, bf16[9,176,256]{2,1,0:T(8,128)(2,1)}, u32[]{:S(2)}, u32[]{:S(2)}) collective-permute-start(bf16[9,176,256]{2,1,0:T(8,128)(2,1)} %get-tuple-element.76), channel_id=1, source_target_pairs={{0,1},{1,2},{2,3},{3,4},{4,5},{5,6},{6,7},{7,0},{8,9},{9,10},{10,1... | collective-permute-start | bytes 2433032 | tf_op jit(solution)/shard_map/ppermute | solution.py:162
  517.8 99.6 %collective-permute-start.8 = (bf16[9,176,256]{2,1,0:T(8,128)(2,1)}, bf16[9,176,256]{2,1,0:T(8,128)(2,1)}, u32[]{:S(2)}, u32[]{:S(2)}) collective-permute-start(bf16[9,176,256]{2,1,0:T(8,128)(2,1)} %get-tuple-element.77), channel_id=1, source_target_pairs={{0,2},{1,3},{2,4},{3,5},{4,6},{5,7},{6,0},{7,1},{8,10},{9,11},{10,... | collective-permute-start | bytes 2433032 | tf_op jit(solution)/shard_map/ppermute | solution.py:162
  536.4 80.9 %collective-permute-start.9 = (bf16[9,176,256]{2,1,0:T(8,128)(2,1)}, bf16[9,176,256]{2,1,0:T(8,128)(2,1)}, u32[]{:S(2)}, u32[]{:S(2)}) collective-permute-start(bf16[9,176,256]{2,1,0:T(8,128)(2,1)} %get-tuple-element.78), channel_id=1, source_target_pairs={{0,3},{1,4},{2,5},{3,6},{4,7},{5,0},{6,1},{7,2},{8,11},{9,12},{10,... | collective-permute-start | bytes 2433032 | tf_op jit(solution)/shard_map/ppermute | solution.py:162
  (60 other events, 4977.6 us)

commit v3 on v2

--- a/solution.py
+++ b/solution.py
@@ -40,13 +40,13 @@
         size = jnp.abs(x)
         top = jnp.max(size, axis=0, keepdims=True)
         top_ref[0, :, cols] = top
-        root = jnp.sqrt(size * (1.0 / jnp.maximum(top, TINY)))
-        code = jnp.exp((SPAN * LN2) * root - (SPAN * LN2 / 2))
-        code = jnp.where(x < 0, -code, code)
-        turned[cols, :] = code.T.astype(jnp.bfloat16)
+        square = size * (SPAN * SPAN / jnp.maximum(top, TINY))
+        root = square * lax.rsqrt(jnp.maximum(square, TINY))
+        code = jnp.exp2(root - SPAN / 2)
+        turned[cols, :] = jnp.where(x < 0, -code, code).T
     for k in range(n):
         to = lax.rem(me_ref[0] + k, n)
-        pieces[k][0] = turned[pl.ds(pl.multiple_of(to * width, width), width), :]
+        pieces[k][0] = turned[pl.ds(pl.multiple_of(to * width, width), width), :].astype(jnp.bfloat16)
 
 
 def pack(me, master, first, count, n):
@@ -60,7 +60,7 @@
             in_specs=[pl.BlockSpec((1, rows, depth), lambda e, me: (first + e, 0, 0))],
             out_specs=[pl.BlockSpec((1, width, rows), lambda e, me: (e, 0, 0))] * n
             + [pl.BlockSpec((1, 1, depth), lambda e, me: (e, 0, 0))],
-            scratch_shapes=[pltpu.VMEM((depth, rows), jnp.bfloat16)],
+            scratch_shapes=[pltpu.VMEM((depth, rows), jnp.float32)],
         ),
         out_shape=[jax.ShapeDtypeStruct((count, width, rows), jnp.bfloat16)] * n
         + [jax.ShapeDtypeStruct((count, 1, depth), jnp.float32)],
@@ -78,19 +78,16 @@
     top = jnp.concatenate([t[pl.ds(expert, 1), start : start + width] for t in tops], axis=0)
     ratios[...] = (top / jnp.max(top, axis=0, keepdims=True)).T
 
-    def some_rows(i, _):
-        part = pl.ds(pl.multiple_of(i * step, step), step)
+    for i in range(width // step):
+        part = slice(i * step, (i + 1) * step)
         ratio = ratios[part, :]
         for k in range(n):
             code = pieces[k][0, part, :].astype(jnp.float32)
             root = jnp.log(jnp.abs(code)) * (1.0 / (SPAN * LN2)) + 0.5
-            value = root * root * ratio[:, k : k + 1]
-            value = jnp.where(code < 0, -value, value).astype(jnp.bfloat16)
+            up = ratio[:, k : k + 1]
+            value = root * root * jnp.where(code < 0, -up, up)
             source = lax.rem(me_ref[0] + (n - k), n)
-            out[0, part, pl.ds(pl.multiple_of(source * rows, rows), rows)] = value
-        return 0
-
-    lax.fori_loop(0, width // step, some_rows, 0)
+            out[0, part, pl.ds(pl.multiple_of(source * rows, rows), rows)] = value.astype(jnp.bfloat16)
 
 
 def unpack(me, tops, start, pieces, whole, first, shape):
@@ -116,26 +113,33 @@
     )(me, *operands)
 
 
-def join_body(n, me_ref, *refs):
-    out, half = refs[-1], n // 2
-    columns, rows = refs[0].shape[0] // 2, refs[0].shape[1]
+def join_body(n, me_ref, gathered, out):
+    half = n // 2
+    rows = gathered.shape[1]
+    columns = out.shape[0]
     place = lax.rem(me_ref[0], half)
     for k in range(half):
         source = me_ref[0] - place + lax.rem(place + (half - k), half)
         for part in range(2):
             at = lax.rem(source + part * half, n) * rows
-            out[:, pl.ds(pl.multiple_of(at, rows), rows)] = refs[k][columns * part : columns * (part + 1), :]
-
-
-def join(n, me, pairs):
-    columns, rows = pairs[0].shape[0] // 2, pairs[0].shape[1]
+            here = slice((2 * k + part) * columns, (2 * k + part + 1) * columns)
+            out[:, pl.ds(pl.multiple_of(at, rows), rows)] = gathered[here, :]
+
+
+def join(n, me, gathered, owners):
+    rows = gathered.shape[1]
+    columns = gathered.shape[0] // (owners * n)
     return pl.pallas_call(
         functools.partial(join_body, n),
-        in_specs=[pl.BlockSpec(memory_space=pltpu.SMEM)] + [pl.BlockSpec(memory_space=pltpu.VMEM)] * len(pairs),
-        out_specs=pl.BlockSpec(memory_space=pltpu.VMEM),
-        out_shape=jax.ShapeDtypeStruct((columns, n * rows), jnp.bfloat16),
+        grid_spec=pltpu.PrefetchScalarGridSpec(
+            num_scalar_prefetch=1,
+            grid=(owners,),
+            in_specs=[pl.BlockSpec((n * columns, rows), lambda o, me: (o, 0))],
+            out_specs=pl.BlockSpec((columns, n * rows), lambda o, me: (o, 0)),
+        ),
+        out_shape=jax.ShapeDtypeStruct((owners * columns, n * rows), jnp.bfloat16),
         name="join",
-    )(me, *pairs)
+    )(me, gathered)
 
 
 def plan(experts):
@@ -187,7 +191,8 @@
     for k in range(1, half):
         inside = [(r, r // half * half + (r + k) % half) for r in range(n)]
         pairs.append(lax.ppermute(pairs[0], "rows", inside))
-    serve_router = lax.all_gather(join(n, here, pairs), "owner", axis=0, tiled=True).T
+    gathered = lax.all_gather(jnp.concatenate(pairs, axis=0), "owner", axis=0, tiled=True)
+    serve_router = join(n, here, gathered, gathered.shape[0] // pairs[0].shape[0] // half).T
     return (*finals, scale[:, :width], scale[:, width:], serve_router)
 
 

time: 635 us -> 615 us (0.969)
  waiting for transfers between devices: 199 us -> 117 us
  starting transfers between devices: 289 us -> 369 us
  Pallas kernels: 115 us -> 100 us
    ppermute x56, waiting for transfers between devices: 188 us -> 105 us  [send(): came[k] = lax.ppermute(pieces[k], 'rows', turns[k])]
    ppermute x56, starting transfers between devices: 286 us -> 367 us  [send(): came[k] = lax.ppermute(pieces[k], 'rows', turns[k])]
    pallas_call x7, Pallas kernels: 57.1 us -> 47.5 us  [unpack(): pl.pallas_call(functools.partial(unpack_body, n, first, start), grid_spec...]
    pallas_call x7, Pallas kernels: 56.1 us -> 49.6 us  [pack(): pl.pallas_call(functools.partial(pack_body, n), grid_spec=pltpu.PrefetchS...]
  transfers between devices with their start and end apart: 60 -> 60, of which waited for: 15 -> 10; matrix products, arithmetic and copies ran while one was open for 0% -> 0% of each run, Pallas kernels for 7% -> 6%
where the time goes in v3:
time: 615 us; the launch traced here: 613 us
  starting transfers between devices  369 us (60%)
  waiting for transfers between devices  117 us (19%)
  Pallas kernels  100 us (16%)
  blocking collectives  14.7 us (2%)
  local copies, waits for them, and re-layouts  7.54 us (1%)
    ppermute x56, starting transfers between devices, send(): came[k] = lax.ppermute(pieces[k], 'rows', turns[k])  367 us
    ppermute x56, waiting for transfers between devices, send(): came[k] = lax.ppermute(pieces[k], 'rows', turns[k])  105 us
    pallas_call x7, Pallas kernels, pack(): pl.pallas_call(functools.partial(pack_body, n), grid_spec=pltpu.PrefetchS...  49.6 us
    pallas_call x7, Pallas kernels, unpack(): pl.pallas_call(functools.partial(unpack_body, n, first, start), grid_spec...  47.5 us
    all_gather x1, blocking collectives, fast_shards(): lax.all_gather(jnp.concatenate(pairs, axis=0), 'owner', axis=0, tiled=True)  14.7 us
  transfers between devices with their start and end apart: 60, of which 10 were waited for; matrix products, arithmetic and copies ran while one was open for 0% of the time, Pallas kernels for 6%

profile of v3, /device:TPU:17, one launch (start us, length us, event | category | flops | bytes accessed | tf_op | source)
XLA Modules:
  0.0 612.8 jit_solution(15740080085274021069)
XLA Ops:
  0.6 12.5 %shard_map.85 = (bf16[9,176,256]{2,1,0:T(8,128)(2,1)}, bf16[9,176,256]{2,1,0:T(8,128)(2,1)}, bf16[9,176,256]{2,1,0:T(8,128)(2,1)}, bf16[9,176,256]{2,1,0:T(8,128...) custom-call(s32[1]{0:T(128)} %bitcast.me_ref, ...), custom_call_target="tpu_custom_call" | custom-call | flops 129761280 | bytes 19464192 | tf_op jit(solution)/shard_map/pallas_call | solution.py:55
  13.1 7.7 %shard_map.84 = (bf16[5,176,256]{2,1,0:T(8,128)(2,1)}, bf16[5,176,256]{2,1,0:T(8,128)(2,1)}, bf16[5,176,256]{2,1,0:T(8,128)(2,1)}, bf16[5,176,256]{2,1,0:T(8,128...) custom-call(s32[1]{0:T(128)} %bitcast.me_ref, ...), custom_call_target="tpu_custom_call" | custom-call | flops 72089600 | bytes 10813440 | tf_op jit(solution)/shard_map/pallas_call | solution.py:55
  20.9 12.5 %shard_map.86 = (bf16[9,176,256]{2,1,0:T(8,128)(2,1)}, bf16[9,176,256]{2,1,0:T(8,128)(2,1)}, bf16[9,176,256]{2,1,0:T(8,128)(2,1)}, bf16[9,176,256]{2,1,0:T(8,128...) custom-call(s32[1]{0:T(128)} %bitcast.me_ref, ...), custom_call_target="tpu_custom_call" | custom-call | flops 129761280 | bytes 19464192 | tf_op jit(solution)/shard_map/pallas_call | solution.py:55
  33.3 6.2 %shard_map.87 = (bf16[4,176,256]{2,1,0:T(8,128)(2,1)}, bf16[4,176,256]{2,1,0:T(8,128)(2,1)}, bf16[4,176,256]{2,1,0:T(8,128)(2,1)}, bf16[4,176,256]{2,1,0:T(8,128...) custom-call(s32[1]{0:T(128)} %bitcast.me_ref, ...), custom_call_target="tpu_custom_call" | custom-call | flops 57671680 | bytes 8650752 | tf_op jit(solution)/shard_map/pallas_call | solution.py:55
  39.6 3.8 shard_map.88
  43.3 3.7 shard_map.83
  47.2 3.1 shard_map.89
  50.5 1.1 fusion.3
  52.0 1.2 collective-permute-start
  53.3 1.3 collective-permute-start.1
  55.6 1.4 collective-permute-start.3
  57.1 1.0 collective-permute-start.56
  58.2 2.6 collective-permute-done.56
  61.7 1.0 collective-permute-start.5
  62.8 1.7 collective-permute-start.6
  64.7 4.2 collective-permute-start.30
  69.1 4.9 collective-permute-done.57
  74.7 2.2 collective-permute-done.58
  77.2 2.3 collective-permute-done.59
  79.4 2.9 collective-permute-start.32
  82.4 1.0 collective-permute-start.35
  83.8 3.0 collective-permute-start.37
  87.3 1.1 collective-permute-start.34
  88.5 14.3 %collective-permute-done.34.refs_15_ = bf16[1,176,256]{2,1,0:T(8,128)(2,1)} collective-permute-done((bf16[1,176,256]{2,1,0:T(8,128)(2,1)}, bf16[1,176,256]{2,1,0:T(8,128)(2,1)}, u32[]{:S(2)}, u32[]{:S(2)}) %collective-permute-start.34) | collective-permute-done | bytes 90144 | tf_op jit(solution)/shard_map/ppermute | solution.py:166
  102.9 3.1 collective-permute-start.41
  107.5 1.7 collective-permute-start.22
  109.9 5.2 collective-permute-start.23
  115.8 3.2 collective-permute-start.24
  119.0 6.3 %collective-permute-start.42 = (bf16[4,176,256]{2,1,0:T(8,128)(2,1)}, bf16[4,176,256]{2,1,0:T(8,128)(2,1)S(1)}, u32[]{:S(2)}, u32[]{:S(2)}) collective-permute-start(bf16[4,176,256]{2,1,0:T(8,128)(2,1)} %get-tuple-element.116), channel_id=1, source_target_pairs={{0,1},{1,2},{2,3},{3,4},{4,5},{5,6},{6,7},{7,0},{8,9},{9,10},{10,1... | collective-permute-start | bytes 1081352 | tf_op jit(solution)/shard_map/ppermute | solution.py:166
  126.8 5.7 collective-permute-start.26
  132.5 3.7 collective-permute-start.27
  136.2 7.6 %collective-permute-done.25.refs_13_ = bf16[2,176,256]{2,1,0:T(8,128)(2,1)S(1)} collective-permute-done((bf16[2,176,256]{2,1,0:T(8,128)(2,1)}, bf16[2,176,256]{2,1,0:T(8,128)(2,1)S(1)}, u32[]{:S(2)}, u32[]{:S(2)}) %collective-permute-start.25) | collective-permute-done | bytes 180256 | tf_op jit(solution)/shard_map/ppermute | solution.py:166
  143.8 9.5 %collective-permute-start.44 = (bf16[4,176,256]{2,1,0:T(8,128)(2,1)}, bf16[4,176,256]{2,1,0:T(8,128)(2,1)S(1)}, u32[]{:S(2)}, u32[]{:S(2)}) collective-permute-start(bf16[4,176,256]{2,1,0:T(8,128)(2,1)} %get-tuple-element.118), channel_id=1, source_target_pairs={{0,3},{1,4},{2,5},{3,6},{4,7},{5,0},{6,1},{7,2},{8,11},{9,12},{10,... | collective-permute-start | bytes 1081352 | tf_op jit(solution)/shard_map/ppermute | solution.py:166
  154.6 12.7 %collective-permute-start.46 = (bf16[4,176,256]{2,1,0:T(8,128)(2,1)S(1)}, bf16[4,176,256]{2,1,0:T(8,128)(2,1)S(1)}, u32[]{:S(2)}, u32[]{:S(2)}) collective-permute-start(bf16[4,176,256]{2,1,0:T(8,128)(2,1)S(1)} %copy-done.57), channel_id=1, source_target_pairs={{0,5},{1,6},{2,7},{3,0},{4,1},{5,2},{6,3},{7,4},{8,13},{9,14},{10,... | collective-permute-start | bytes 1081352 | tf_op jit(solution)/shard_map/ppermute | solution.py:166
  167.4 1.9 collective-permute-start.47
  170.0 10.8 %collective-permute-start.14 = (bf16[5,176,256]{2,1,0:T(8,128)(2,1)S(1)}, bf16[5,176,256]{2,1,0:T(8,128)(2,1)S(1)}, u32[]{:S(2)}, u32[]{:S(2)}) collective-permute-start(bf16[5,176,256]{2,1,0:T(8,128)(2,1)S(1)} %copy-done.54), channel_id=1, source_target_pairs={{0,1},{1,2},{2,3},{3,4},{4,5},{5,6},{6,7},{7,0},{8,9},{9,10},{10,1... | collective-permute-start | bytes 1351688 | tf_op jit(solution)/shard_map/ppermute | solution.py:166
  180.9 27.3 %collective-permute-start.15 = (bf16[5,176,256]{2,1,0:T(8,128)(2,1)S(1)}, bf16[5,176,256]{2,1,0:T(8,128)(2,1)S(1)}, u32[]{:S(2)}, u32[]{:S(2)}) collective-permute-start(bf16[5,176,256]{2,1,0:T(8,128)(2,1)S(1)} %copy-done.53), channel_id=1, source_target_pairs={{0,2},{1,3},{2,4},{3,5},{4,6},{5,7},{6,0},{7,1},{8,10},{9,11},{10,... | collective-permute-start | bytes 1351688 | tf_op jit(solution)/shard_map/ppermute | solution.py:166
  208.2 8.4 %collective-permute-start.16 = (bf16[5,176,256]{2,1,0:T(8,128)(2,1)S(1)}, bf16[5,176,256]{2,1,0:T(8,128)(2,1)S(1)}, u32[]{:S(2)}, u32[]{:S(2)}) collective-permute-start(bf16[5,176,256]{2,1,0:T(8,128)(2,1)S(1)} %copy-done.52), channel_id=1, source_target_pairs={{0,3},{1,4},{2,5},{3,6},{4,7},{5,0},{6,1},{7,2},{8,11},{9,12},{10,... | collective-permute-start | bytes 1351688 | tf_op jit(solution)/shard_map/ppermute | solution.py:166
  216.6 26.5 %collective-permute-start.18 = (bf16[5,176,256]{2,1,0:T(8,128)(2,1)}, bf16[5,176,256]{2,1,0:T(8,128)(2,1)S(1)}, u32[]{:S(2)}, u32[]{:S(2)}) collective-permute-start(bf16[5,176,256]{2,1,0:T(8,128)(2,1)} %get-tuple-element.88), channel_id=1, source_target_pairs={{0,5},{1,6},{2,7},{3,0},{4,1},{5,2},{6,3},{7,4},{8,13},{9,14},{10,... | collective-permute-start | bytes 1351688 | tf_op jit(solution)/shard_map/ppermute | solution.py:166
  243.2 2.2 collective-permute-start.19
  245.5 19.1 %collective-permute-start.50 = (bf16[9,176,256]{2,1,0:T(8,128)(2,1)}, bf16[9,176,256]{2,1,0:T(8,128)(2,1)S(1)}, u32[]{:S(2)}, u32[]{:S(2)}) collective-permute-start(bf16[9,176,256]{2,1,0:T(8,128)(2,1)} %get-tuple-element.125), channel_id=1, source_target_pairs={{0,2},{1,3},{2,4},{3,5},{4,6},{5,7},{6,0},{7,1},{8,10},{9,11},{10,... | collective-permute-start | bytes 2433032 | tf_op jit(solution)/shard_map/ppermute | solution.py:166
  264.6 19.8 %collective-permute-start.51 = (bf16[9,176,256]{2,1,0:T(8,128)(2,1)}, bf16[9,176,256]{2,1,0:T(8,128)(2,1)S(1)}, u32[]{:S(2)}, u32[]{:S(2)}) collective-permute-start(bf16[9,176,256]{2,1,0:T(8,128)(2,1)} %get-tuple-element.126), channel_id=1, source_target_pairs={{0,3},{1,4},{2,5},{3,6},{4,7},{5,0},{6,1},{7,2},{8,11},{9,12},{10,... | collective-permute-start | bytes 2433032 | tf_op jit(solution)/shard_map/ppermute | solution.py:166
  284.5 20.5 %collective-permute-done.19.refs_14_ = bf16[5,176,256]{2,1,0:T(8,128)(2,1)S(1)} collective-permute-done((bf16[5,176,256]{2,1,0:T(8,128)(2,1)}, bf16[5,176,256]{2,1,0:T(8,128)(2,1)S(1)}, u32[]{:S(2)}, u32[]{:S(2)}) %collective-permute-start.19) | collective-permute-done | bytes 450592 | tf_op jit(solution)/shard_map/ppermute | solution.py:166
  305.1 55.7 %collective-permute-start.20 = (bf16[5,176,256]{2,1,0:T(8,128)(2,1)}, bf16[5,176,256]{2,1,0:T(8,128)(2,1)S(1)}, u32[]{:S(2)}, u32[]{:S(2)}) collective-permute-start(bf16[5,176,256]{2,1,0:T(8,128)(2,1)} %get-tuple-element.90), channel_id=1, source_target_pairs={{0,7},{1,0},{2,1},{3,2},{4,3},{5,4},{6,5},{7,6},{8,15},{9,8},{10,9... | collective-permute-start | bytes 1351688 | tf_op jit(solution)/shard_map/ppermute | solution.py:166
  360.8 24.7 %collective-permute-done.20.refs_15_ = bf16[5,176,256]{2,1,0:T(8,128)(2,1)S(1)} collective-permute-done((bf16[5,176,256]{2,1,0:T(8,128)(2,1)}, bf16[5,176,256]{2,1,0:T(8,128)(2,1)S(1)}, u32[]{:S(2)}, u32[]{:S(2)}) %collective-permute-start.20) | collective-permute-done | bytes 450592 | tf_op jit(solution)/shard_map/ppermute | solution.py:166
  385.6 3.1 collective-permute-start.55
  388.7 0.9 copy-done.11
  389.6 3.2 collective-permute-start.10
  393.7 3.7 collective-permute-start.11
  397.4 23.1 %collective-permute-done.53.refs_13_ = bf16[9,176,256]{2,1,0:T(8,128)(2,1)S(1)} collective-permute-done((bf16[9,176,256]{2,1,0:T(8,128)(2,1)}, bf16[9,176,256]{2,1,0:T(8,128)(2,1)S(1)}, u32[]{:S(2)}, u32[]{:S(2)}) %collective-permute-start.53) | collective-permute-done | bytes 811040 | tf_op jit(solution)/shard_map/ppermute | solution.py:166
  420.5 70.5 %collective-permute-start.12 = (bf16[9,176,256]{2,1,0:T(8,128)(2,1)}, bf16[9,176,256]{2,1,0:T(8,128)(2,1)}, u32[]{:S(2)}, u32[]{:S(2)}) collective-permute-start(bf16[9,176,256]{2,1,0:T(8,128)(2,1)} %get-tuple-element.81), channel_id=1, source_target_pairs={{0,6},{1,7},{2,0},{3,1},{4,2},{5,3},{6,4},{7,5},{8,14},{9,15},{10,... | collective-permute-start | bytes 2433032 | tf_op jit(solution)/shard_map/ppermute | solution.py:166
  491.0 1.4 collective-permute-start.7
  492.5 15.0 %collective-permute-done.10.refs_12_ = bf16[9,176,256]{2,1,0:T(8,128)(2,1)S(1)} collective-permute-done((bf16[9,176,256]{2,1,0:T(8,128)(2,1)}, bf16[9,176,256]{2,1,0:T(8,128)(2,1)S(1)}, u32[]{:S(2)}, u32[]{:S(2)}) %collective-permute-start.10) | collective-permute-done | bytes 811040 | tf_op jit(solution)/shard_map/ppermute | solution.py:166
  507.5 20.2 %collective-permute-start.8 = (bf16[9,176,256]{2,1,0:T(8,128)(2,1)}, bf16[9,176,256]{2,1,0:T(8,128)(2,1)}, u32[]{:S(2)}, u32[]{:S(2)}) collective-permute-start(bf16[9,176,256]{2,1,0:T(8,128)(2,1)} %get-tuple-element.77), channel_id=1, source_target_pairs={{0,2},{1,3},{2,4},{3,5},{4,6},{5,7},{6,0},{7,1},{8,10},{9,11},{10,... | collective-permute-start | bytes 2433032 | tf_op jit(solution)/shard_map/ppermute | solution.py:166
  527.7 18.3 %collective-permute-start.9 = (bf16[9,176,256]{2,1,0:T(8,128)(2,1)}, bf16[9,176,256]{2,1,0:T(8,128)(2,1)}, u32[]{:S(2)}, u32[]{:S(2)}) collective-permute-start(bf16[9,176,256]{2,1,0:T(8,128)(2,1)} %get-tuple-element.78), channel_id=1, source_target_pairs={{0,3},{1,4},{2,5},{3,6},{4,7},{5,0},{6,1},{7,2},{8,11},{9,12},{10,... | collective-permute-start | bytes 2433032 | tf_op jit(solution)/shard_map/ppermute | solution.py:166
  547.4 14.7 %all_gather.3.gathered = bf16[512,256]{1,0:T(8,128)(2,1)} all-gather(bf16[128,256]{1,0:T(8,128)(2,1)S(1)} %constant_dynamic-update-slice_fusion), channel_id=1, replica_groups=mesh['owner'=4,'rows'=8] {'owner'}, dimensions={0}, use_global_device_ids=true | all-gather | bytes 327680 | tf_op jit(solution)/shard_map/all_gather | solution.py:194
  562.0 3.0 join.1
  565.0 3.7 shard_map.90.refs_16_
  568.8 7.3 %shard_map.91.refs_16_ = bf16[16,176,2048]{2,1,0:T(8,128)(2,1)} custom-call(s32[1]{0:T(128)} %bitcast.me_ref, f32[16,352]{1,0:T(8,128)} %get-tuple-element.134.refs_0_, f32[16,352]{1,0:T(8,128)} %copy-done, f32[16,352]{1,0:T(8,128)} %copy-done.1, f32[16,352]{1,0:T(8,128)} %copy-done.2, f32[16,352]{1,0:T(8,128)} %copy-done.3, ...), custom_call_target="tpu_custom_call", output_to_operand_aliasing={{}: (17, {})} | custom-call | flops 54067200 | bytes 7208960 | tf_op jit(solution)/shard_map/pallas_call | solution.py:97
  576.1 12.0 %shard_map.93.refs_16_ = bf16[16,176,2048]{2,1,0:T(8,128)(2,1)} custom-call(s32[1]{0:T(128)} %bitcast.me_ref, f32[16,352]{1,0:T(8,128)} %get-tuple-element.134.refs_0_, f32[16,352]{1,0:T(8,128)} %copy-done, f32[16,352]{1,0:T(8,128)} %copy-done.1, f32[16,352]{1,0:T(8,128)} %copy-done.2, f32[16,352]{1,0:T(8,128)} %copy-done.3, f32[16,352]{1,0:T(8,128)} %copy-done.4, ...), custom_call_target="tpu_custom_call" | custom-call | flops 97320960 | bytes 12976128 | tf_op jit(solution)/shard_map/pallas_call | solution.py:97
  588.1 6.1 shard_map.94.refs_16_
  594.2 3.8 shard_map.95.refs_16_
  598.0 2.9 shard_map.96
  601.0 11.7 %shard_map.92 = bf16[16,176,2048]{2,1,0:T(8,128)(2,1)} custom-call(s32[1]{0:T(128)} %bitcast.me_ref, f32[16,352]{1,0:T(8,128)} %get-tuple-element.134.refs_0_, f32[16,352]{1,0:T(8,128)} %copy-done, f32[16,352]{1,0:T(8,128)} %copy-done.1, f32[16,352]{1,0:T(8,128)} %copy-done.2, f32[16,352]{1,0:T(8,128)} %copy-done.3, ...), custom_call_target="tpu_custom_call", output_to_operand_aliasing={{}: (17, {})} | custom-call | flops 97320960 | bytes 12976128 | tf_op jit(solution)/shard_map/pallas_call | solution.py:97
  (216 shorter events, 14.1 us)
Async XLA Ops:
  52.0 9.7 %collective-permute-start = (f32[16,352]{1,0:T(8,128)S(1)}, f32[16,352]{1,0:T(8,128)S(1)}, u32[]{:S(2)}, u32[]{:S(2)}) collective-permute-start(f32[16,352]{1,0:T(8,128)S(1)} %pad_maximum_fusion.1), channel_id=1, source_target_pairs={{0,1},{1,2},{2,3},{3,4},{4,5},{5,6},{6,7},{7,0},{8,9},{9,10},{10,1... | collective-permute-start | bytes 67592 | tf_op jit(solution)/shard_map/ppermute | solution.py:166
  53.3 9.5 %collective-permute-start.1 = (f32[16,352]{1,0:T(8,128)S(1)}, f32[16,352]{1,0:T(8,128)S(1)}, u32[]{:S(2)}, u32[]{:S(2)}) collective-permute-start(f32[16,352]{1,0:T(8,128)S(1)} %pad_maximum_fusion.2), channel_id=1, source_target_pairs={{0,2},{1,3},{2,4},{3,5},{4,6},{5,7},{6,0},{7,1},{8,10},{9,11},{10,... | collective-permute-start | bytes 67592 | tf_op jit(solution)/shard_map/ppermute | solution.py:166
  54.7 9.8 %collective-permute-start.2 = (f32[16,352]{1,0:T(8,128)S(1)}, f32[16,352]{1,0:T(8,128)S(1)}, u32[]{:S(2)}, u32[]{:S(2)}) collective-permute-start(f32[16,352]{1,0:T(8,128)S(1)} %pad_maximum_fusion.3), channel_id=1, source_target_pairs={{0,3},{1,4},{2,5},{3,6},{4,7},{5,0},{6,1},{7,2},{8,11},{9,12},{10,... | collective-permute-start | bytes 67592 | tf_op jit(solution)/shard_map/ppermute | solution.py:166
  55.6 8.8 %collective-permute-start.3 = (f32[16,352]{1,0:T(8,128)S(1)}, f32[16,352]{1,0:T(8,128)S(1)}, u32[]{:S(2)}, u32[]{:S(2)}) collective-permute-start(f32[16,352]{1,0:T(8,128)S(1)} %pad_maximum_fusion.4), channel_id=1, source_target_pairs={{0,4},{1,5},{2,6},{3,7},{4,0},{5,1},{6,2},{7,3},{8,12},{9,13},{10,... | collective-permute-start | bytes 67592 | tf_op jit(solution)/shard_map/ppermute | solution.py:166
  57.1 3.8 collective-permute-start.56
  60.8 3.9 collective-permute-start.4
  61.7 503.3 %copy-start = (f32[16,352]{1,0:T(8,128)}, f32[16,352]{1,0:T(8,128)S(1)}, u32[]{:S(2)}) copy-start(f32[16,352]{1,0:T(8,128)S(1)} %collective-permute-done.refs_1_) | copy-start | bytes 67588
  61.7 7.3 %collective-permute-start.5 = (f32[16,352]{1,0:T(8,128)S(1)}, f32[16,352]{1,0:T(8,128)S(1)}, u32[]{:S(2)}, u32[]{:S(2)}) collective-permute-start(f32[16,352]{1,0:T(8,128)S(1)} %pad_maximum_fusion.6), channel_id=1, source_target_pairs={{0,6},{1,7},{2,0},{3,1},{4,2},{5,3},{6,4},{7,5},{8,14},{9,15},{10,... | collective-permute-start | bytes 67592 | tf_op jit(solution)/shard_map/ppermute | solution.py:166
  62.8 502.2 %copy-start.1 = (f32[16,352]{1,0:T(8,128)}, f32[16,352]{1,0:T(8,128)S(1)}, u32[]{:S(2)}) copy-start(f32[16,352]{1,0:T(8,128)S(1)} %collective-permute-done.1.refs_2_) | copy-start | bytes 67588
  62.8 6.2 %collective-permute-start.6 = (f32[16,352]{1,0:T(8,128)S(1)}, f32[16,352]{1,0:T(8,128)S(1)}, u32[]{:S(2)}, u32[]{:S(2)}) collective-permute-start(f32[16,352]{1,0:T(8,128)S(1)} %pad_maximum_fusion.7), channel_id=1, source_target_pairs={{0,7},{1,0},{2,1},{3,2},{4,3},{5,4},{6,5},{7,6},{8,15},{9,8},{10,9... | collective-permute-start | bytes 67592 | tf_op jit(solution)/shard_map/ppermute | solution.py:166
  64.4 500.6 %copy-start.2 = (f32[16,352]{1,0:T(8,128)}, f32[16,352]{1,0:T(8,128)S(1)}, u32[]{:S(2)}) copy-start(f32[16,352]{1,0:T(8,128)S(1)} %collective-permute-done.2.refs_3_) | copy-start | bytes 67588
  64.4 17.9 %collective-permute-start.28 = (bf16[1,176,256]{2,1,0:T(8,128)(2,1)}, bf16[1,176,256]{2,1,0:T(8,128)(2,1)}, u32[]{:S(2)}, u32[]{:S(2)}) collective-permute-start(bf16[1,176,256]{2,1,0:T(8,128)(2,1)} %get-tuple-element.100), channel_id=1, source_target_pairs={{0,1},{1,2},{2,3},{3,4},{4,5},{5,6},{6,7},{7,0},{8,9},{9,10},{10,1... | collective-permute-start | bytes 270344 | tf_op jit(solution)/shard_map/ppermute | solution.py:166
  64.4 500.6 %copy-start.3 = (f32[16,352]{1,0:T(8,128)}, f32[16,352]{1,0:T(8,128)S(1)}, u32[]{:S(2)}) copy-start(f32[16,352]{1,0:T(8,128)S(1)} %collective-permute-done.3.refs_4_) | copy-start | bytes 67588
  64.4 18.0 %collective-permute-start.29 = (bf16[1,176,256]{2,1,0:T(8,128)(2,1)}, bf16[1,176,256]{2,1,0:T(8,128)(2,1)}, u32[]{:S(2)}, u32[]{:S(2)}) collective-permute-start(bf16[1,176,256]{2,1,0:T(8,128)(2,1)} %get-tuple-element.101), channel_id=1, source_target_pairs={{0,2},{1,3},{2,4},{3,5},{4,6},{5,7},{6,0},{7,1},{8,10},{9,11},{10,... | collective-permute-start | bytes 270344 | tf_op jit(solution)/shard_map/ppermute | solution.py:166
  64.7 18.6 %collective-permute-start.30 = (bf16[1,176,256]{2,1,0:T(8,128)(2,1)}, bf16[1,176,256]{2,1,0:T(8,128)(2,1)}, u32[]{:S(2)}, u32[]{:S(2)}) collective-permute-start(bf16[1,176,256]{2,1,0:T(8,128)(2,1)} %get-tuple-element.102), channel_id=1, source_target_pairs={{0,3},{1,4},{2,5},{3,6},{4,7},{5,0},{6,1},{7,2},{8,11},{9,12},{10,... | collective-permute-start | bytes 270344 | tf_op jit(solution)/shard_map/ppermute | solution.py:166
  69.0 14.9 %collective-permute-start.31 = (bf16[1,176,256]{2,1,0:T(8,128)(2,1)}, bf16[1,176,256]{2,1,0:T(8,128)(2,1)}, u32[]{:S(2)}, u32[]{:S(2)}) collective-permute-start(bf16[1,176,256]{2,1,0:T(8,128)(2,1)} %get-tuple-element.103), channel_id=1, source_target_pairs={{0,4},{1,5},{2,6},{3,7},{4,0},{5,1},{6,2},{7,3},{8,12},{9,13},{10,... | collective-permute-start | bytes 270344 | tf_op jit(solution)/shard_map/ppermute | solution.py:166
  69.0 5.0 collective-permute-start.57
  74.0 2.9 collective-permute-start.58
  76.8 2.6 collective-permute-start.59
  79.4 7.4 %collective-permute-start.32 = (bf16[1,176,256]{2,1,0:T(8,128)(2,1)}, bf16[1,176,256]{2,1,0:T(8,128)(2,1)}, u32[]{:S(2)}, u32[]{:S(2)}) collective-permute-start(bf16[1,176,256]{2,1,0:T(8,128)(2,1)} %get-tuple-element.104), channel_id=1, source_target_pairs={{0,5},{1,6},{2,7},{3,0},{4,1},{5,2},{6,3},{7,4},{8,13},{9,14},{10,... | collective-permute-start | bytes 270344 | tf_op jit(solution)/shard_map/ppermute | solution.py:166
  82.3 5.0 collective-permute-start.33
  82.4 20.4 %collective-permute-start.35 = (bf16[2,176,256]{2,1,0:T(8,128)(2,1)}, bf16[2,176,256]{2,1,0:T(8,128)(2,1)S(1)}, u32[]{:S(2)}, u32[]{:S(2)}) collective-permute-start(bf16[2,176,256]{2,1,0:T(8,128)(2,1)} %get-tuple-element.108), channel_id=1, source_target_pairs={{0,1},{1,2},{2,3},{3,4},{4,5},{5,6},{6,7},{7,0},{8,9},{9,10},{10,1... | collective-permute-start | bytes 540680 | tf_op jit(solution)/shard_map/ppermute | solution.py:166
  83.4 19.5 %collective-permute-start.36 = (bf16[2,176,256]{2,1,0:T(8,128)(2,1)}, bf16[2,176,256]{2,1,0:T(8,128)(2,1)S(1)}, u32[]{:S(2)}, u32[]{:S(2)}) collective-permute-start(bf16[2,176,256]{2,1,0:T(8,128)(2,1)} %get-tuple-element.109), channel_id=1, source_target_pairs={{0,2},{1,3},{2,4},{3,5},{4,6},{5,7},{6,0},{7,1},{8,10},{9,11},{10,... | collective-permute-start | bytes 540680 | tf_op jit(solution)/shard_map/ppermute | solution.py:166
  83.8 22.1 %collective-permute-start.37 = (bf16[2,176,256]{2,1,0:T(8,128)(2,1)}, bf16[2,176,256]{2,1,0:T(8,128)(2,1)S(1)}, u32[]{:S(2)}, u32[]{:S(2)}) collective-permute-start(bf16[2,176,256]{2,1,0:T(8,128)(2,1)} %get-tuple-element.110), channel_id=1, source_target_pairs={{0,3},{1,4},{2,5},{3,6},{4,7},{5,0},{6,1},{7,2},{8,11},{9,12},{10,... | collective-permute-start | bytes 540680 | tf_op jit(solution)/shard_map/ppermute | solution.py:166
  86.9 20.6 %collective-permute-start.38 = (bf16[2,176,256]{2,1,0:T(8,128)(2,1)}, bf16[2,176,256]{2,1,0:T(8,128)(2,1)S(1)}, u32[]{:S(2)}, u32[]{:S(2)}) collective-permute-start(bf16[2,176,256]{2,1,0:T(8,128)(2,1)} %get-tuple-element.111), channel_id=1, source_target_pairs={{0,4},{1,5},{2,6},{3,7},{4,0},{5,1},{6,2},{7,3},{8,12},{9,13},{10,... | collective-permute-start | bytes 540680 | tf_op jit(solution)/shard_map/ppermute | solution.py:166
  87.3 15.5 %collective-permute-start.34 = (bf16[1,176,256]{2,1,0:T(8,128)(2,1)}, bf16[1,176,256]{2,1,0:T(8,128)(2,1)}, u32[]{:S(2)}, u32[]{:S(2)}) collective-permute-start(bf16[1,176,256]{2,1,0:T(8,128)(2,1)} %get-tuple-element.106), channel_id=1, source_target_pairs={{0,7},{1,0},{2,1},{3,2},{4,3},{5,4},{6,5},{7,6},{8,15},{9,8},{10,9... | collective-permute-start | bytes 270344 | tf_op jit(solution)/shard_map/ppermute | solution.py:166
  102.8 6.4 %collective-permute-start.39 = (bf16[2,176,256]{2,1,0:T(8,128)(2,1)}, bf16[2,176,256]{2,1,0:T(8,128)(2,1)S(1)}, u32[]{:S(2)}, u32[]{:S(2)}) collective-permute-start(bf16[2,176,256]{2,1,0:T(8,128)(2,1)} %get-tuple-element.112), channel_id=1, source_target_pairs={{0,5},{1,6},{2,7},{3,0},{4,1},{5,2},{6,3},{7,4},{8,13},{9,14},{10,... | collective-permute-start | bytes 540680 | tf_op jit(solution)/shard_map/ppermute | solution.py:166
  102.8 12.3 %collective-permute-start.40 = (bf16[2,176,256]{2,1,0:T(8,128)(2,1)}, bf16[2,176,256]{2,1,0:T(8,128)(2,1)S(1)}, u32[]{:S(2)}, u32[]{:S(2)}) collective-permute-start(bf16[2,176,256]{2,1,0:T(8,128)(2,1)} %get-tuple-element.113), channel_id=1, source_target_pairs={{0,6},{1,7},{2,0},{3,1},{4,2},{5,3},{6,4},{7,5},{8,14},{9,15},{10,... | collective-permute-start | bytes 540680 | tf_op jit(solution)/shard_map/ppermute | solution.py:166
  102.9 16.0 %collective-permute-start.41 = (bf16[2,176,256]{2,1,0:T(8,128)(2,1)}, bf16[2,176,256]{2,1,0:T(8,128)(2,1)S(1)}, u32[]{:S(2)}, u32[]{:S(2)}) collective-permute-start(bf16[2,176,256]{2,1,0:T(8,128)(2,1)} %get-tuple-element.114), channel_id=1, source_target_pairs={{0,7},{1,0},{2,1},{3,2},{4,3},{5,4},{6,5},{7,6},{8,15},{9,8},{10,9... | collective-permute-start | bytes 540680 | tf_op jit(solution)/shard_map/ppermute | solution.py:166
  106.6 18.6 %collective-permute-start.21 = (bf16[2,176,256]{2,1,0:T(8,128)(2,1)}, bf16[2,176,256]{2,1,0:T(8,128)(2,1)S(1)}, u32[]{:S(2)}, u32[]{:S(2)}) collective-permute-start(bf16[2,176,256]{2,1,0:T(8,128)(2,1)} %get-tuple-element.92), channel_id=1, source_target_pairs={{0,1},{1,2},{2,3},{3,4},{4,5},{5,6},{6,7},{7,0},{8,9},{9,10},{10,1... | collective-permute-start | bytes 540680 | tf_op jit(solution)/shard_map/ppermute | solution.py:166
  107.5 19.2 %collective-permute-start.22 = (bf16[2,176,256]{2,1,0:T(8,128)(2,1)}, bf16[2,176,256]{2,1,0:T(8,128)(2,1)S(1)}, u32[]{:S(2)}, u32[]{:S(2)}) collective-permute-start(bf16[2,176,256]{2,1,0:T(8,128)(2,1)} %get-tuple-element.93), channel_id=1, source_target_pairs={{0,2},{1,3},{2,4},{3,5},{4,6},{5,7},{6,0},{7,1},{8,10},{9,11},{10,... | collective-permute-start | bytes 540680 | tf_op jit(solution)/shard_map/ppermute | solution.py:166
  109.9 16.9 %collective-permute-start.23 = (bf16[2,176,256]{2,1,0:T(8,128)(2,1)}, bf16[2,176,256]{2,1,0:T(8,128)(2,1)S(1)}, u32[]{:S(2)}, u32[]{:S(2)}) collective-permute-start(bf16[2,176,256]{2,1,0:T(8,128)(2,1)} %get-tuple-element.94), channel_id=1, source_target_pairs={{0,3},{1,4},{2,5},{3,6},{4,7},{5,0},{6,1},{7,2},{8,11},{9,12},{10,... | collective-permute-start | bytes 540680 | tf_op jit(solution)/shard_map/ppermute | solution.py:166
  115.8 16.7 %collective-permute-start.24 = (bf16[2,176,256]{2,1,0:T(8,128)(2,1)}, bf16[2,176,256]{2,1,0:T(8,128)(2,1)S(1)}, u32[]{:S(2)}, u32[]{:S(2)}) collective-permute-start(bf16[2,176,256]{2,1,0:T(8,128)(2,1)} %get-tuple-element.95), channel_id=1, source_target_pairs={{0,4},{1,5},{2,6},{3,7},{4,0},{5,1},{6,2},{7,3},{8,12},{9,13},{10,... | collective-permute-start | bytes 540680 | tf_op jit(solution)/shard_map/ppermute | solution.py:166
  119.0 48.4 %collective-permute-start.42 = (bf16[4,176,256]{2,1,0:T(8,128)(2,1)}, bf16[4,176,256]{2,1,0:T(8,128)(2,1)S(1)}, u32[]{:S(2)}, u32[]{:S(2)}) collective-permute-start(bf16[4,176,256]{2,1,0:T(8,128)(2,1)} %get-tuple-element.116), channel_id=1, source_target_pairs={{0,1},{1,2},{2,3},{3,4},{4,5},{5,6},{6,7},{7,0},{8,9},{9,10},{10,1... | collective-permute-start | bytes 1081352 | tf_op jit(solution)/shard_map/ppermute | solution.py:166
  125.9 43.3 %collective-permute-start.43 = (bf16[4,176,256]{2,1,0:T(8,128)(2,1)S(1)}, bf16[4,176,256]{2,1,0:T(8,128)(2,1)S(1)}, u32[]{:S(2)}, u32[]{:S(2)}) collective-permute-start(bf16[4,176,256]{2,1,0:T(8,128)(2,1)S(1)} %copy-done.58), channel_id=1, source_target_pairs={{0,2},{1,3},{2,4},{3,5},{4,6},{5,7},{6,0},{7,1},{8,10},{9,11},{10,... | collective-permute-start | bytes 1081352 | tf_op jit(solution)/shard_map/ppermute | solution.py:166
  126.7 17.0 %collective-permute-start.25 = (bf16[2,176,256]{2,1,0:T(8,128)(2,1)}, bf16[2,176,256]{2,1,0:T(8,128)(2,1)S(1)}, u32[]{:S(2)}, u32[]{:S(2)}) collective-permute-start(bf16[2,176,256]{2,1,0:T(8,128)(2,1)} %get-tuple-element.96), channel_id=1, source_target_pairs={{0,5},{1,6},{2,7},{3,0},{4,1},{5,2},{6,3},{7,4},{8,13},{9,14},{10,... | collective-permute-start | bytes 540680 | tf_op jit(solution)/shard_map/ppermute | solution.py:166
  126.8 26.5 %collective-permute-start.26 = (bf16[2,176,256]{2,1,0:T(8,128)(2,1)}, bf16[2,176,256]{2,1,0:T(8,128)(2,1)S(1)}, u32[]{:S(2)}, u32[]{:S(2)}) collective-permute-start(bf16[2,176,256]{2,1,0:T(8,128)(2,1)} %get-tuple-element.97), channel_id=1, source_target_pairs={{0,6},{1,7},{2,0},{3,1},{4,2},{5,3},{6,4},{7,5},{8,14},{9,15},{10,... | collective-permute-start | bytes 540680 | tf_op jit(solution)/shard_map/ppermute | solution.py:166
  132.5 20.9 %collective-permute-start.27 = (bf16[2,176,256]{2,1,0:T(8,128)(2,1)S(1)}, bf16[2,176,256]{2,1,0:T(8,128)(2,1)S(1)}, u32[]{:S(2)}, u32[]{:S(2)}) collective-permute-start(bf16[2,176,256]{2,1,0:T(8,128)(2,1)S(1)} %copy-done.59), channel_id=1, source_target_pairs={{0,7},{1,0},{2,1},{3,2},{4,3},{5,4},{6,5},{7,6},{8,15},{9,8},{10,9... | collective-permute-start | bytes 540680 | tf_op jit(solution)/shard_map/ppermute | solution.py:166
  143.8 25.6 %collective-permute-start.44 = (bf16[4,176,256]{2,1,0:T(8,128)(2,1)}, bf16[4,176,256]{2,1,0:T(8,128)(2,1)S(1)}, u32[]{:S(2)}, u32[]{:S(2)}) collective-permute-start(bf16[4,176,256]{2,1,0:T(8,128)(2,1)} %get-tuple-element.118), channel_id=1, source_target_pairs={{0,3},{1,4},{2,5},{3,6},{4,7},{5,0},{6,1},{7,2},{8,11},{9,12},{10,... | collective-permute-start | bytes 1081352 | tf_op jit(solution)/shard_map/ppermute | solution.py:166
  153.3 27.6 %collective-permute-start.45 = (bf16[4,176,256]{2,1,0:T(8,128)(2,1)}, bf16[4,176,256]{2,1,0:T(8,128)(2,1)S(1)}, u32[]{:S(2)}, u32[]{:S(2)}) collective-permute-start(bf16[4,176,256]{2,1,0:T(8,128)(2,1)} %get-tuple-element.119), channel_id=1, source_target_pairs={{0,4},{1,5},{2,6},{3,7},{4,0},{5,1},{6,2},{7,3},{8,12},{9,13},{10,... | collective-permute-start | bytes 1081352 | tf_op jit(solution)/shard_map/ppermute | solution.py:166
  154.6 53.6 %collective-permute-start.46 = (bf16[4,176,256]{2,1,0:T(8,128)(2,1)S(1)}, bf16[4,176,256]{2,1,0:T(8,128)(2,1)S(1)}, u32[]{:S(2)}, u32[]{:S(2)}) collective-permute-start(bf16[4,176,256]{2,1,0:T(8,128)(2,1)S(1)} %copy-done.57), channel_id=1, source_target_pairs={{0,5},{1,6},{2,7},{3,0},{4,1},{5,2},{6,3},{7,4},{8,13},{9,14},{10,... | collective-permute-start | bytes 1081352 | tf_op jit(solution)/shard_map/ppermute | solution.py:166
  167.4 49.2 %collective-permute-start.47 = (bf16[4,176,256]{2,1,0:T(8,128)(2,1)S(1)}, bf16[4,176,256]{2,1,0:T(8,128)(2,1)S(1)}, u32[]{:S(2)}, u32[]{:S(2)}) collective-permute-start(bf16[4,176,256]{2,1,0:T(8,128)(2,1)S(1)} %copy-done.56), channel_id=1, source_target_pairs={{0,6},{1,7},{2,0},{3,1},{4,2},{5,3},{6,4},{7,5},{8,14},{9,15},{10,... | collective-permute-start | bytes 1081352 | tf_op jit(solution)/shard_map/ppermute | solution.py:166
  169.3 47.3 %collective-permute-start.48 = (bf16[4,176,256]{2,1,0:T(8,128)(2,1)S(1)}, bf16[4,176,256]{2,1,0:T(8,128)(2,1)S(1)}, u32[]{:S(2)}, u32[]{:S(2)}) collective-permute-start(bf16[4,176,256]{2,1,0:T(8,128)(2,1)S(1)} %copy-done.55), channel_id=1, source_target_pairs={{0,7},{1,0},{2,1},{3,2},{4,3},{5,4},{6,5},{7,6},{8,15},{9,8},{10,9... | collective-permute-start | bytes 1081352 | tf_op jit(solution)/shard_map/ppermute | solution.py:166
  170.0 73.2 %collective-permute-start.14 = (bf16[5,176,256]{2,1,0:T(8,128)(2,1)S(1)}, bf16[5,176,256]{2,1,0:T(8,128)(2,1)S(1)}, u32[]{:S(2)}, u32[]{:S(2)}) collective-permute-start(bf16[5,176,256]{2,1,0:T(8,128)(2,1)S(1)} %copy-done.54), channel_id=1, source_target_pairs={{0,1},{1,2},{2,3},{3,4},{4,5},{5,6},{6,7},{7,0},{8,9},{9,10},{10,1... | collective-permute-start | bytes 1351688 | tf_op jit(solution)/shard_map/ppermute | solution.py:166
  180.9 64.6 %collective-permute-start.15 = (bf16[5,176,256]{2,1,0:T(8,128)(2,1)S(1)}, bf16[5,176,256]{2,1,0:T(8,128)(2,1)S(1)}, u32[]{:S(2)}, u32[]{:S(2)}) collective-permute-start(bf16[5,176,256]{2,1,0:T(8,128)(2,1)S(1)} %copy-done.53), channel_id=1, source_target_pairs={{0,2},{1,3},{2,4},{3,5},{4,6},{5,7},{6,0},{7,1},{8,10},{9,11},{10,... | collective-permute-start | bytes 1351688 | tf_op jit(solution)/shard_map/ppermute | solution.py:166
  208.2 37.2 %collective-permute-start.16 = (bf16[5,176,256]{2,1,0:T(8,128)(2,1)S(1)}, bf16[5,176,256]{2,1,0:T(8,128)(2,1)S(1)}, u32[]{:S(2)}, u32[]{:S(2)}) collective-permute-start(bf16[5,176,256]{2,1,0:T(8,128)(2,1)S(1)} %copy-done.52), channel_id=1, source_target_pairs={{0,3},{1,4},{2,5},{3,6},{4,7},{5,0},{6,1},{7,2},{8,11},{9,12},{10,... | collective-permute-start | bytes 1351688 | tf_op jit(solution)/shard_map/ppermute | solution.py:166
  216.6 48.0 %collective-permute-start.17 = (bf16[5,176,256]{2,1,0:T(8,128)(2,1)}, bf16[5,176,256]{2,1,0:T(8,128)(2,1)S(1)}, u32[]{:S(2)}, u32[]{:S(2)}) collective-permute-start(bf16[5,176,256]{2,1,0:T(8,128)(2,1)} %get-tuple-element.87), channel_id=1, source_target_pairs={{0,4},{1,5},{2,6},{3,7},{4,0},{5,1},{6,2},{7,3},{8,12},{9,13},{10,... | collective-permute-start | bytes 1351688 | tf_op jit(solution)/shard_map/ppermute | solution.py:166
  216.6 67.8 %collective-permute-start.18 = (bf16[5,176,256]{2,1,0:T(8,128)(2,1)}, bf16[5,176,256]{2,1,0:T(8,128)(2,1)S(1)}, u32[]{:S(2)}, u32[]{:S(2)}) collective-permute-start(bf16[5,176,256]{2,1,0:T(8,128)(2,1)} %get-tuple-element.88), channel_id=1, source_target_pairs={{0,5},{1,6},{2,7},{3,0},{4,1},{5,2},{6,3},{7,4},{8,13},{9,14},{10,... | collective-permute-start | bytes 1351688 | tf_op jit(solution)/shard_map/ppermute | solution.py:166
  243.2 61.9 %collective-permute-start.19 = (bf16[5,176,256]{2,1,0:T(8,128)(2,1)}, bf16[5,176,256]{2,1,0:T(8,128)(2,1)S(1)}, u32[]{:S(2)}, u32[]{:S(2)}) collective-permute-start(bf16[5,176,256]{2,1,0:T(8,128)(2,1)} %get-tuple-element.89), channel_id=1, source_target_pairs={{0,6},{1,7},{2,0},{3,1},{4,2},{5,3},{6,4},{7,5},{8,14},{9,15},{10,... | collective-permute-start | bytes 1351688 | tf_op jit(solution)/shard_map/ppermute | solution.py:166
  245.4 140.1 %collective-permute-start.49 = (bf16[9,176,256]{2,1,0:T(8,128)(2,1)}, bf16[9,176,256]{2,1,0:T(8,128)(2,1)S(1)}, u32[]{:S(2)}, u32[]{:S(2)}) collective-permute-start(bf16[9,176,256]{2,1,0:T(8,128)(2,1)} %get-tuple-element.124), channel_id=1, source_target_pairs={{0,1},{1,2},{2,3},{3,4},{4,5},{5,6},{6,7},{7,0},{8,9},{9,10},{10,1... | collective-permute-start | bytes 2433032 | tf_op jit(solution)/shard_map/ppermute | solution.py:166
  245.5 140.1 %collective-permute-start.50 = (bf16[9,176,256]{2,1,0:T(8,128)(2,1)}, bf16[9,176,256]{2,1,0:T(8,128)(2,1)S(1)}, u32[]{:S(2)}, u32[]{:S(2)}) collective-permute-start(bf16[9,176,256]{2,1,0:T(8,128)(2,1)} %get-tuple-element.125), channel_id=1, source_target_pairs={{0,2},{1,3},{2,4},{3,5},{4,6},{5,7},{6,0},{7,1},{8,10},{9,11},{10,... | collective-permute-start | bytes 2433032 | tf_op jit(solution)/shard_map/ppermute | solution.py:166
  264.6 124.1 %collective-permute-start.51 = (bf16[9,176,256]{2,1,0:T(8,128)(2,1)}, bf16[9,176,256]{2,1,0:T(8,128)(2,1)S(1)}, u32[]{:S(2)}, u32[]{:S(2)}) collective-permute-start(bf16[9,176,256]{2,1,0:T(8,128)(2,1)} %get-tuple-element.126), channel_id=1, source_target_pairs={{0,3},{1,4},{2,5},{3,6},{4,7},{5,0},{6,1},{7,2},{8,11},{9,12},{10,... | collective-permute-start | bytes 2433032 | tf_op jit(solution)/shard_map/ppermute | solution.py:166
  284.4 108.3 %collective-permute-start.52 = (bf16[9,176,256]{2,1,0:T(8,128)(2,1)}, bf16[9,176,256]{2,1,0:T(8,128)(2,1)S(1)}, u32[]{:S(2)}, u32[]{:S(2)}) collective-permute-start(bf16[9,176,256]{2,1,0:T(8,128)(2,1)} %get-tuple-element.127), channel_id=1, source_target_pairs={{0,4},{1,5},{2,6},{3,7},{4,0},{5,1},{6,2},{7,3},{8,12},{9,13},{10,... | collective-permute-start | bytes 2433032 | tf_op jit(solution)/shard_map/ppermute | solution.py:166
  305.1 80.5 %collective-permute-start.20 = (bf16[5,176,256]{2,1,0:T(8,128)(2,1)}, bf16[5,176,256]{2,1,0:T(8,128)(2,1)S(1)}, u32[]{:S(2)}, u32[]{:S(2)}) collective-permute-start(bf16[5,176,256]{2,1,0:T(8,128)(2,1)} %get-tuple-element.90), channel_id=1, source_target_pairs={{0,7},{1,0},{2,1},{3,2},{4,3},{5,4},{6,5},{7,6},{8,15},{9,8},{10,9... | collective-permute-start | bytes 1351688 | tf_op jit(solution)/shard_map/ppermute | solution.py:166
  385.5 35.0 %collective-permute-start.53 = (bf16[9,176,256]{2,1,0:T(8,128)(2,1)}, bf16[9,176,256]{2,1,0:T(8,128)(2,1)S(1)}, u32[]{:S(2)}, u32[]{:S(2)}) collective-permute-start(bf16[9,176,256]{2,1,0:T(8,128)(2,1)} %get-tuple-element.128), channel_id=1, source_target_pairs={{0,5},{1,6},{2,7},{3,0},{4,1},{5,2},{6,3},{7,4},{8,13},{9,14},{10,... | collective-permute-start | bytes 2433032 | tf_op jit(solution)/shard_map/ppermute | solution.py:166
  385.5 105.5 %collective-permute-start.54 = (bf16[9,176,256]{2,1,0:T(8,128)(2,1)}, bf16[9,176,256]{2,1,0:T(8,128)(2,1)S(1)}, u32[]{:S(2)}, u32[]{:S(2)}) collective-permute-start(bf16[9,176,256]{2,1,0:T(8,128)(2,1)} %get-tuple-element.129), channel_id=1, source_target_pairs={{0,6},{1,7},{2,0},{3,1},{4,2},{5,3},{6,4},{7,5},{8,14},{9,15},{10,... | collective-permute-start | bytes 2433032 | tf_op jit(solution)/shard_map/ppermute | solution.py:166
  385.6 105.4 %collective-permute-start.55 = (bf16[9,176,256]{2,1,0:T(8,128)(2,1)}, bf16[9,176,256]{2,1,0:T(8,128)(2,1)S(1)}, u32[]{:S(2)}, u32[]{:S(2)}) collective-permute-start(bf16[9,176,256]{2,1,0:T(8,128)(2,1)} %get-tuple-element.130), channel_id=1, source_target_pairs={{0,7},{1,0},{2,1},{3,2},{4,3},{5,4},{6,5},{7,6},{8,15},{9,8},{10,9... | collective-permute-start | bytes 2433032 | tf_op jit(solution)/shard_map/ppermute | solution.py:166
  389.6 117.9 %collective-permute-start.10 = (bf16[9,176,256]{2,1,0:T(8,128)(2,1)}, bf16[9,176,256]{2,1,0:T(8,128)(2,1)S(1)}, u32[]{:S(2)}, u32[]{:S(2)}) collective-permute-start(bf16[9,176,256]{2,1,0:T(8,128)(2,1)} %get-tuple-element.79), channel_id=1, source_target_pairs={{0,4},{1,5},{2,6},{3,7},{4,0},{5,1},{6,2},{7,3},{8,12},{9,13},{10,... | collective-permute-start | bytes 2433032 | tf_op jit(solution)/shard_map/ppermute | solution.py:166
  393.7 134.0 %collective-permute-start.11 = (bf16[9,176,256]{2,1,0:T(8,128)(2,1)}, bf16[9,176,256]{2,1,0:T(8,128)(2,1)S(1)}, u32[]{:S(2)}, u32[]{:S(2)}) collective-permute-start(bf16[9,176,256]{2,1,0:T(8,128)(2,1)} %get-tuple-element.80), channel_id=1, source_target_pairs={{0,5},{1,6},{2,7},{3,0},{4,1},{5,2},{6,3},{7,4},{8,13},{9,14},{10,... | collective-permute-start | bytes 2433032 | tf_op jit(solution)/shard_map/ppermute | solution.py:166
  420.5 180.4 %collective-permute-start.12 = (bf16[9,176,256]{2,1,0:T(8,128)(2,1)}, bf16[9,176,256]{2,1,0:T(8,128)(2,1)}, u32[]{:S(2)}, u32[]{:S(2)}) collective-permute-start(bf16[9,176,256]{2,1,0:T(8,128)(2,1)} %get-tuple-element.81), channel_id=1, source_target_pairs={{0,6},{1,7},{2,0},{3,1},{4,2},{5,3},{6,4},{7,5},{8,14},{9,15},{10,... | collective-permute-start | bytes 2433032 | tf_op jit(solution)/shard_map/ppermute | solution.py:166
  491.0 109.9 %collective-permute-start.13 = (bf16[9,176,256]{2,1,0:T(8,128)(2,1)}, bf16[9,176,256]{2,1,0:T(8,128)(2,1)}, u32[]{:S(2)}, u32[]{:S(2)}) collective-permute-start(bf16[9,176,256]{2,1,0:T(8,128)(2,1)} %get-tuple-element.82), channel_id=1, source_target_pairs={{0,7},{1,0},{2,1},{3,2},{4,3},{5,4},{6,5},{7,6},{8,15},{9,8},{10,9... | collective-permute-start | bytes 2433032 | tf_op jit(solution)/shard_map/ppermute | solution.py:166
  491.0 109.9 %collective-permute-start.7 = (bf16[9,176,256]{2,1,0:T(8,128)(2,1)}, bf16[9,176,256]{2,1,0:T(8,128)(2,1)}, u32[]{:S(2)}, u32[]{:S(2)}) collective-permute-start(bf16[9,176,256]{2,1,0:T(8,128)(2,1)} %get-tuple-element.76), channel_id=1, source_target_pairs={{0,1},{1,2},{2,3},{3,4},{4,5},{5,6},{6,7},{7,0},{8,9},{9,10},{10,1... | collective-permute-start | bytes 2433032 | tf_op jit(solution)/shard_map/ppermute | solution.py:166
  507.5 93.5 %collective-permute-start.8 = (bf16[9,176,256]{2,1,0:T(8,128)(2,1)}, bf16[9,176,256]{2,1,0:T(8,128)(2,1)}, u32[]{:S(2)}, u32[]{:S(2)}) collective-permute-start(bf16[9,176,256]{2,1,0:T(8,128)(2,1)} %get-tuple-element.77), channel_id=1, source_target_pairs={{0,2},{1,3},{2,4},{3,5},{4,6},{5,7},{6,0},{7,1},{8,10},{9,11},{10,... | collective-permute-start | bytes 2433032 | tf_op jit(solution)/shard_map/ppermute | solution.py:166
  527.7 73.3 %collective-permute-start.9 = (bf16[9,176,256]{2,1,0:T(8,128)(2,1)}, bf16[9,176,256]{2,1,0:T(8,128)(2,1)}, u32[]{:S(2)}, u32[]{:S(2)}) collective-permute-start(bf16[9,176,256]{2,1,0:T(8,128)(2,1)} %get-tuple-element.78), channel_id=1, source_target_pairs={{0,3},{1,4},{2,5},{3,6},{4,7},{5,0},{6,1},{7,2},{8,11},{9,12},{10,... | collective-permute-start | bytes 2433032 | tf_op jit(solution)/shard_map/ppermute | solution.py:166
  (56 other events, 4067.6 us)

commit v4 on v3

--- a/solution.py
+++ b/solution.py
@@ -30,23 +30,66 @@
     return (*finals, *scales, serve_router)
 
 
+def coded(x):
+    size = jnp.abs(x)
+    top = jnp.max(size, axis=0, keepdims=True)
+    square = size * (SPAN * SPAN / jnp.maximum(top, TINY))
+    root = square * lax.rsqrt(jnp.maximum(square, TINY))
+    code = jnp.exp2(root - SPAN / 2)
+    return jnp.where(x < 0, -code, code), top
+
+
 def pack_body(n, me_ref, x_ref, *refs):
     pieces, top_ref, turned = refs[:n], refs[n], refs[n + 1]
     depth = turned.shape[0]
     width = depth // n
     for c in range(depth // 128):
         cols = slice(128 * c, 128 * (c + 1))
-        x = x_ref[0, :, cols]
-        size = jnp.abs(x)
-        top = jnp.max(size, axis=0, keepdims=True)
-        top_ref[0, :, cols] = top
-        square = size * (SPAN * SPAN / jnp.maximum(top, TINY))
-        root = square * lax.rsqrt(jnp.maximum(square, TINY))
-        code = jnp.exp2(root - SPAN / 2)
-        turned[cols, :] = jnp.where(x < 0, -code, code).T
+        code, top_ref[0, :, cols] = coded(x_ref[0, :, cols])
+        turned[cols, :] = code.T
     for k in range(n):
         to = lax.rem(me_ref[0] + k, n)
         pieces[k][0] = turned[pl.ds(pl.multiple_of(to * width, width), width), :].astype(jnp.bfloat16)
+
+
+def window(n, me, depth, tiles):
+    column = lax.rem(me + n // 2, n) * (depth // n)
+    return column, jnp.minimum(lax.div(column, 128), depth // 128 - tiles)
+
+
+def lead_body(n, depth, me_ref, *refs):
+    tiles, piece, turned = refs[:-2], refs[-2], refs[-1]
+    column, tile = window(n, me_ref[0], depth, len(tiles))
+    width = depth // n
+    at = pl.multiple_of(column - tile * 128, 16)
+    for e in range(piece.shape[0]):
+        for c, part in enumerate(tiles):
+            turned[e, 128 * c : 128 * (c + 1), :] = coded(part[e])[0].T
+        piece[e] = turned[e, pl.ds(at, width), :].astype(jnp.bfloat16)
+
+
+def lead(me, master, first, count, n):
+    _, rows, depth = master.shape
+    width = depth // n
+    tiles = min((width - 16) // 128 + 2, depth // 128)
+    spec = lambda c: pl.BlockSpec(
+        (count, rows, 128), lambda e, me: (first // count, 0, window(n, me[0], depth, tiles)[1] + c)
+    )
+    return pl.pallas_call(
+        functools.partial(lead_body, n, depth),
+        grid_spec=pltpu.PrefetchScalarGridSpec(
+            num_scalar_prefetch=1,
+            grid=(1,),
+            in_specs=[spec(c) for c in range(tiles)],
+            out_specs=pl.BlockSpec((count, width, rows), lambda e, me: (0, 0, 0)),
+            scratch_shapes=[pltpu.VMEM((count, tiles * 128, rows), jnp.float32)],
+        ),
+        out_shape=jax.ShapeDtypeStruct((count, width, rows), jnp.bfloat16),
+        cost_estimate=pl.CostEstimate(
+            flops=count * rows * width * 40, bytes_accessed=count * rows * width * 8, transcendentals=0
+        ),
+        name="lead",
+    )(me, *[master] * tiles)
 
 
 def pack(me, master, first, count, n):
@@ -70,24 +113,77 @@
     )(me, master)
 
 
+def ratios_of(tops, expert, start, width):
+    top = jnp.concatenate([t[pl.ds(expert, 1), start : start + width] for t in tops], axis=0)
+    return (top / jnp.max(top, axis=0, keepdims=True)).T
+
+
+def decoded(code, up):
+    code = code.astype(jnp.float32)
+    root = jnp.log(jnp.abs(code)) * (1.0 / (SPAN * LN2)) + 0.5
+    return (root * root * jnp.where(code < 0, -up, up)).astype(jnp.bfloat16)
+
+
 def unpack_body(n, first, start, me_ref, *refs):
     tops, pieces, out, ratios = refs[:n], refs[n : 2 * n], refs[-2], refs[-1]
     width, rows = pieces[0].shape[1:]
     step = 16
-    expert = first + pl.program_id(0)
-    top = jnp.concatenate([t[pl.ds(expert, 1), start : start + width] for t in tops], axis=0)
-    ratios[...] = (top / jnp.max(top, axis=0, keepdims=True)).T
-
+    ratios[...] = ratios_of(tops, first + pl.program_id(0), start, width)
     for i in range(width // step):
         part = slice(i * step, (i + 1) * step)
         ratio = ratios[part, :]
         for k in range(n):
-            code = pieces[k][0, part, :].astype(jnp.float32)
-            root = jnp.log(jnp.abs(code)) * (1.0 / (SPAN * LN2)) + 0.5
-            up = ratio[:, k : k + 1]
-            value = root * root * jnp.where(code < 0, -up, up)
             source = lax.rem(me_ref[0] + (n - k), n)
-            out[0, part, pl.ds(pl.multiple_of(source * rows, rows), rows)] = value.astype(jnp.bfloat16)
+            lanes = pl.ds(pl.multiple_of(source * rows, rows), rows)
+            out[0, part, lanes] = decoded(pieces[k][0, part, :], ratio[:, k : k + 1])
+
+
+def unpack_some_body(n, sources, first, start, me_ref, *refs):
+    m = len(sources)
+    tops, pieces = refs[:n], refs[n : n + m]
+    out, done, ratios, sems = refs[-4:]
+    count, width, rows = pieces[0].shape
+    step = 16
+    for e in range(count):
+        ratios[e] = ratios_of(tops, first + e, start, width)
+    copies = []
+    for p, k in enumerate(sources):
+        for e in range(count):
+            for i in range(width // step):
+                part = slice(i * step, (i + 1) * step)
+                done[p, e, part, :] = decoded(pieces[p][e, part, :], ratios[e, part, k : k + 1])
+        lane = pl.multiple_of(lax.rem(me_ref[0] + (n - k), n) * rows, rows)
+        target = out.at[pl.ds(first, count), :, pl.ds(lane, rows)]
+        copies.append(pltpu.make_async_copy(done.at[p], target, sems.at[p]))
+        copies[-1].start()
+    for copy in copies:
+        copy.wait()
+
+
+def unpack_some(me, tops, start, pieces, sources, whole, first):
+    n, m = len(tops), len(sources)
+    count, width, rows = pieces[0].shape
+    return pl.pallas_call(
+        functools.partial(unpack_some_body, n, sources, first, start),
+        grid_spec=pltpu.PrefetchScalarGridSpec(
+            num_scalar_prefetch=1,
+            grid=(1,),
+            in_specs=[pl.BlockSpec(tops[0].shape, lambda e, me: (0, 0))] * n
+            + [pl.BlockSpec((count, width, rows), lambda e, me: (0, 0, 0))] * m
+            + [pl.BlockSpec(memory_space=pl.ANY)],
+            out_specs=pl.BlockSpec(memory_space=pl.ANY),
+            scratch_shapes=[
+                pltpu.VMEM((m, count, width, rows), jnp.bfloat16),
+                pltpu.VMEM((count, width, n), jnp.float32),
+                pltpu.SemaphoreType.DMA((m,)),
+            ],
+        ),
+        out_shape=jax.ShapeDtypeStruct(whole.shape, jnp.bfloat16),
+        input_output_aliases={n + m + 1: 0},
+        cost_estimate=pl.CostEstimate(
+            flops=count * rows * width * m * 30, bytes_accessed=count * rows * width * m * 4, transcendentals=0
+        ),
+    )(me, *tops, *pieces, whole)
 
 
 def unpack(me, tops, start, pieces, whole, first, shape):
@@ -143,14 +239,18 @@
 
 
 def plan(experts):
-    first = [c for c in (experts // 8, experts // 3) if c]
-    last = [c for c in (experts // 4, experts // 8, experts // 16) if c]
-    counts = ((*first, experts - sum(first)), (experts - sum(last), *last))
+    first = (3 * experts // 16, experts // 3)
+    counts = ((*first, experts - sum(first)), (experts - experts // 4, experts // 4))
     return [(a, sum(counts[a][:c]), count) for a in range(2) for c, count in enumerate(counts[a])]
 
 
 def send_order(n):
     return sorted(range(1, n), key=lambda k: abs(2 * k - n))
+
+
+def last_groups(n):
+    line = [0, *send_order(n)]
+    return (line[: n // 2], line[n // 2 :])
 
 
 def fast_shards(n, masters, router_weight, router_gain):
@@ -168,8 +268,10 @@
 
     chunks = plan(experts)
     packed, tops = [], [[], []]
-    for a, first, count in chunks:
+    for c, (a, first, count) in enumerate(chunks):
         *pieces, top = pack(here, masters[a], first, count, n)
+        if c == 0:
+            pieces[n // 2] = lead(here, masters[a], first, count, n)
         packed.append(pieces)
         tops[a].append(top[:, 0, :])
     came = [send(pieces) for pieces in packed]
@@ -181,6 +283,11 @@
 
     wholes = [None, None]
     for c, (a, first, count) in enumerate(chunks):
+        if c == len(chunks) - 1:
+            for sources in last_groups(n):
+                pieces = [came[c][k] for k in sources]
+                wholes[a] = unpack_some(here, tops, a * width, pieces, sources, wholes[a], first)
+            break
         wholes[a] = unpack(here, tops, a * width, came[c], wholes[a], first, (experts, width, n * rows))
     finals = [jnp.swapaxes(whole, 1, 2) for whole in wholes]
 
@@ -204,7 +311,7 @@
 
 
 def fits(n, experts, rows, depth):
-    return n % 2 == 0 and experts >= 8 and rows % 128 == 0 and depth % (16 * n) == 0 and depth % 128 == 0
+    return n % 2 == 0 and experts % 4 == 0 and experts >= 8 and rows % 128 == 0 and depth % (16 * n) == 0 and depth % 128 == 0
 
 
 def solution(mesh):

time: 615 us -> 634 us (1.031)
  the two profiles are of different devices: /device:TPU:17 before, /device:TPU:0 now
where the time goes in v4:
time: 634 us; the launch traced here: 631 us
  starting transfers between devices  352 us (56%)
  waiting for transfers between devices  166 us (26%)
  Pallas kernels  96.8 us (15%)
  local copies, waits for them, and re-layouts  7.17 us (1%)
  blocking collectives  6.39 us (1%)
    ppermute x42, starting transfers between devices, send(): came[k] = lax.ppermute(pieces[k], 'rows', turns[k])  345 us
    ppermute x42, waiting for transfers between devices, send(): came[k] = lax.ppermute(pieces[k], 'rows', turns[k])  159 us
    pallas_call x5, Pallas kernels, pack(): pl.pallas_call(functools.partial(pack_body, n), grid_spec=pltpu.PrefetchS...  46.5 us
    pallas_call x4, Pallas kernels, unpack(): pl.pallas_call(functools.partial(unpack_body, n, first, start), grid_spec...  37.8 us
  transfers between devices with their start and end apart: 46, of which 11 were waited for; matrix products, arithmetic and copies ran while one was open for 0% of the time, Pallas kernels for 7%

profile of v4, /device:TPU:0, one launch (start us, length us, event | category | flops | bytes accessed | tf_op | source)
XLA Modules:
  0.0 631.2 jit_solution(18320865977827705467)
XLA Ops:
  0.6 11.2 %shard_map.85 = (bf16[8,176,256]{2,1,0:T(8,128)(2,1)}, bf16[8,176,256]{2,1,0:T(8,128)(2,1)}, bf16[8,176,256]{2,1,0:T(8,128)(2,1)}, bf16[8,176,256]{2,1,0:T(8,128...) custom-call(s32[1]{0:T(128)} %bitcast.me_ref, ...), custom_call_target="tpu_custom_call" | custom-call | flops 115343360 | bytes 17301504 | tf_op jit(solution)/shard_map/pallas_call | solution.py:98
  11.8 7.7 %shard_map.84 = (bf16[5,176,256]{2,1,0:T(8,128)(2,1)}, bf16[5,176,256]{2,1,0:T(8,128)(2,1)}, bf16[5,176,256]{2,1,0:T(8,128)(2,1)}, bf16[5,176,256]{2,1,0:T(8,128...) custom-call(s32[1]{0:T(128)} %bitcast.me_ref, ...), custom_call_target="tpu_custom_call" | custom-call | flops 72089600 | bytes 10813440 | tf_op jit(solution)/shard_map/pallas_call | solution.py:98
  19.5 16.0 %shard_map.86 = (bf16[12,176,256]{2,1,0:T(8,128)(2,1)}, bf16[12,176,256]{2,1,0:T(8,128)(2,1)}, bf16[12,176,256]{2,1,0:T(8,128)(2,1)}, bf16[12,176,256]{2,1,0:T(8...) custom-call(s32[1]{0:T(128)} %bitcast.me_ref, ...), custom_call_target="tpu_custom_call" | custom-call | flops 173015040 | bytes 25952256 | tf_op jit(solution)/shard_map/pallas_call | solution.py:98
  35.5 6.2 shard_map.87
  41.8 5.4 shard_map.83
  47.3 0.8 copy.27
  48.7 3.0 collective-permute-start
  51.8 1.6 collective-permute-start.1
  53.5 2.5 collective-permute-start.2
  56.0 1.5 collective-permute-start.21
  58.1 4.0 collective-permute-done.42
  62.6 3.9 collective-permute-start.4
  66.5 4.1 collective-permute-start.5
  70.6 0.9 collective-permute-start.22
  71.6 1.2 collective-permute-start.43
  72.8 1.7 collective-permute-start.44
  74.5 3.3 collective-permute-start.45
  77.8 1.9 collective-permute-done.43
  79.8 1.4 collective-permute-done.44
  81.2 2.4 collective-permute-start.25
  83.6 1.7 collective-permute-start.27
  85.9 7.3 %collective-permute-done.23.refs_11_ = bf16[3,176,256]{2,1,0:T(8,128)(2,1)S(1)} collective-permute-done((bf16[3,176,256]{2,1,0:T(8,128)(2,1)S(1)}, bf16[3,176,256]{2,1,0:T(8,128)(2,1)S(1)}, u32[]{:S(2)}, u32[]{:S(2)}) %collective-permute-start.23) | collective-permute-done | bytes 270368 | tf_op jit(solution)/shard_map/ppermute | solution.py:266
  93.1 0.8 collective-permute-start.32
  94.5 0.7 copy-done.29
  95.2 10.7 %collective-permute-start.33 = (bf16[4,176,256]{2,1,0:T(8,128)(2,1)S(1)}, bf16[4,176,256]{2,1,0:T(8,128)(2,1)S(1)}, u32[]{:S(2)}, u32[]{:S(2)}) collective-permute-start(bf16[4,176,256]{2,1,0:T(8,128)(2,1)S(1)} %copy-done.41), channel_id=1, source_target_pairs={{0,3},{1,4},{2,5},{3,6},{4,7},{5,0},{6,1},{7,2},{8,11},{9,12},{10,... | collective-permute-start | bytes 1081352 | tf_op jit(solution)/shard_map/ppermute | solution.py:266
  105.9 2.6 lead.1
  108.4 19.0 %collective-permute-start.24 = (bf16[3,176,256]{2,1,0:T(8,128)(2,1)}, bf16[3,176,256]{2,1,0:T(8,128)(2,1)S(1)}, u32[]{:S(2)}, u32[]{:S(2)}) collective-permute-start(bf16[3,176,256]{2,1,0:T(8,128)(2,1)} %lead.1), channel_id=1, source_target_pairs={{0,4},{1,5},{2,6},{3,7},{4,0},{5,1},{6,2},{7,3},{8,12},{9,13},{10,... | collective-permute-start | bytes 811016 | tf_op jit(solution)/shard_map/ppermute | solution.py:266
  127.5 25.6 %collective-permute-done.24.refs_12_ = bf16[3,176,256]{2,1,0:T(8,128)(2,1)S(1)} collective-permute-done((bf16[3,176,256]{2,1,0:T(8,128)(2,1)}, bf16[3,176,256]{2,1,0:T(8,128)(2,1)S(1)}, u32[]{:S(2)}, u32[]{:S(2)}) %collective-permute-start.24) | collective-permute-done | bytes 270368 | tf_op jit(solution)/shard_map/ppermute | solution.py:266
  153.0 2.5 collective-permute-start.16
  155.5 3.3 collective-permute-start.17
  158.8 21.7 %collective-permute-done.33.refs_10_ = bf16[4,176,256]{2,1,0:T(8,128)(2,1)S(1)} collective-permute-done((bf16[4,176,256]{2,1,0:T(8,128)(2,1)S(1)}, bf16[4,176,256]{2,1,0:T(8,128)(2,1)S(1)}, u32[]{:S(2)}, u32[]{:S(2)}) %collective-permute-start.33) | collective-permute-done | bytes 360480 | tf_op jit(solution)/shard_map/ppermute | solution.py:266
  180.5 8.0 %collective-permute-start.18 = (bf16[5,176,256]{2,1,0:T(8,128)(2,1)}, bf16[5,176,256]{2,1,0:T(8,128)(2,1)S(1)}, u32[]{:S(2)}, u32[]{:S(2)}) collective-permute-start(bf16[5,176,256]{2,1,0:T(8,128)(2,1)} %get-tuple-element.67), channel_id=1, source_target_pairs={{0,5},{1,6},{2,7},{3,0},{4,1},{5,2},{6,3},{7,4},{8,13},{9,14},{10,... | collective-permute-start | bytes 1351688 | tf_op jit(solution)/shard_map/ppermute | solution.py:266
  188.5 1.0 collective-permute-start.19
  189.5 0.8 copy-done.18
  190.2 1.9 collective-permute-start.10
  192.2 5.1 collective-permute-done.16.refs_11_
  197.3 0.8 copy-done.19
  198.0 0.8 copy-done.20
  198.8 57.7 %collective-permute-start.11 = (bf16[8,176,256]{2,1,0:T(8,128)(2,1)}, bf16[8,176,256]{2,1,0:T(8,128)(2,1)S(1)}, u32[]{:S(2)}, u32[]{:S(2)}) collective-permute-start(bf16[8,176,256]{2,1,0:T(8,128)(2,1)} %get-tuple-element.59), channel_id=1, source_target_pairs={{0,5},{1,6},{2,7},{3,0},{4,1},{5,2},{6,3},{7,4},{8,13},{9,14},{10,... | collective-permute-start | bytes 2162696 | tf_op jit(solution)/shard_map/ppermute | solution.py:266
  256.6 0.8 copy-done.21
  257.3 24.3 %collective-permute-start.12 = (bf16[8,176,256]{2,1,0:T(8,128)(2,1)}, bf16[8,176,256]{2,1,0:T(8,128)(2,1)S(1)}, u32[]{:S(2)}, u32[]{:S(2)}) collective-permute-start(bf16[8,176,256]{2,1,0:T(8,128)(2,1)} %get-tuple-element.60), channel_id=1, source_target_pairs={{0,6},{1,7},{2,0},{3,1},{4,2},{5,3},{6,4},{7,5},{8,14},{9,15},{10,... | collective-permute-start | bytes 2162696 | tf_op jit(solution)/shard_map/ppermute | solution.py:266
  281.7 0.8 copy-done.22
  282.4 25.2 %collective-permute-start.13 = (bf16[8,176,256]{2,1,0:T(8,128)(2,1)}, bf16[8,176,256]{2,1,0:T(8,128)(2,1)S(1)}, u32[]{:S(2)}, u32[]{:S(2)}) collective-permute-start(bf16[8,176,256]{2,1,0:T(8,128)(2,1)} %get-tuple-element.61), channel_id=1, source_target_pairs={{0,7},{1,0},{2,1},{3,2},{4,3},{5,4},{6,5},{7,6},{8,15},{9,8},{10,9... | collective-permute-start | bytes 2162696 | tf_op jit(solution)/shard_map/ppermute | solution.py:266
  308.4 17.4 %collective-permute-start.36 = (bf16[12,176,256]{2,1,0:T(8,128)(2,1)}, bf16[12,176,256]{2,1,0:T(8,128)(2,1)S(1)}, u32[]{:S(2)}, u32[]{:S(2)}) collective-permute-start(bf16[12,176,256]{2,1,0:T(8,128)(2,1)} %get-tuple-element.87), channel_id=1, source_target_pairs={{0,2},{1,3},{2,4},{3,5},{4,6},{5,7},{6,0},{7,1},{8,10},{9,11},{10,... | collective-permute-start | bytes 3244040 | tf_op jit(solution)/shard_map/ppermute | solution.py:266
  325.8 32.8 %collective-permute-done.12.refs_14_ = bf16[8,176,256]{2,1,0:T(8,128)(2,1)S(1)} collective-permute-done((bf16[8,176,256]{2,1,0:T(8,128)(2,1)}, bf16[8,176,256]{2,1,0:T(8,128)(2,1)S(1)}, u32[]{:S(2)}, u32[]{:S(2)}) %collective-permute-start.12) | collective-permute-done | bytes 720928 | tf_op jit(solution)/shard_map/ppermute | solution.py:266
  358.6 3.1 collective-permute-start.8
  361.7 31.0 %collective-permute-start.9 = (bf16[8,176,256]{2,1,0:T(8,128)(2,1)}, bf16[8,176,256]{2,1,0:T(8,128)(2,1)S(1)}, u32[]{:S(2)}, u32[]{:S(2)}) collective-permute-start(bf16[8,176,256]{2,1,0:T(8,128)(2,1)} %get-tuple-element.57), channel_id=1, source_target_pairs={{0,3},{1,4},{2,5},{3,6},{4,7},{5,0},{6,1},{7,2},{8,11},{9,12},{10,... | collective-permute-start | bytes 2162696 | tf_op jit(solution)/shard_map/ppermute | solution.py:266
  392.8 62.2 %collective-permute-done.9.refs_11_ = bf16[8,176,256]{2,1,0:T(8,128)(2,1)S(1)} collective-permute-done((bf16[8,176,256]{2,1,0:T(8,128)(2,1)}, bf16[8,176,256]{2,1,0:T(8,128)(2,1)S(1)}, u32[]{:S(2)}, u32[]{:S(2)}) %collective-permute-start.9) | collective-permute-done | bytes 720928 | tf_op jit(solution)/shard_map/ppermute | solution.py:266
  455.0 18.1 %collective-permute-start.40 = (bf16[12,176,256]{2,1,0:T(8,128)(2,1)}, bf16[12,176,256]{2,1,0:T(8,128)(2,1)}, u32[]{:S(2)}, u32[]{:S(2)}) collective-permute-start(bf16[12,176,256]{2,1,0:T(8,128)(2,1)} %get-tuple-element.91), channel_id=1, source_target_pairs={{0,6},{1,7},{2,0},{3,1},{4,2},{5,3},{6,4},{7,5},{8,14},{9,15},{10,... | collective-permute-start | bytes 3244040 | tf_op jit(solution)/shard_map/ppermute | solution.py:266
  473.3 0.8 maximum_maximum_fusion
  474.1 0.7 fusion.12
  474.8 3.5 collective-permute-done.37.refs_11_
  478.3 62.5 %collective-permute-start.28 = (bf16[4,176,256]{2,1,0:T(8,128)(2,1)}, bf16[4,176,256]{2,1,0:T(8,128)(2,1)}, u32[]{:S(2)}, u32[]{:S(2)}) collective-permute-start(bf16[4,176,256]{2,1,0:T(8,128)(2,1)} %get-tuple-element.77), channel_id=1, source_target_pairs={{0,2},{1,3},{2,4},{3,5},{4,6},{5,7},{6,0},{7,1},{8,10},{9,11},{10,... | collective-permute-start | bytes 1081352 | tf_op jit(solution)/shard_map/ppermute | solution.py:266
  540.8 2.8 collective-permute-start.29
  543.7 32.5 %collective-permute-start.30 = (bf16[4,176,256]{2,1,0:T(8,128)(2,1)}, bf16[4,176,256]{2,1,0:T(8,128)(2,1)}, u32[]{:S(2)}, u32[]{:S(2)}) collective-permute-start(bf16[4,176,256]{2,1,0:T(8,128)(2,1)} %get-tuple-element.79), channel_id=1, source_target_pairs={{0,1},{1,2},{2,3},{3,4},{4,5},{5,6},{6,7},{7,0},{8,9},{9,10},{10,1... | collective-permute-start | bytes 1081352 | tf_op jit(solution)/shard_map/ppermute | solution.py:266
  576.1 0.7 constant_dynamic-update-slice_fusion
  576.8 6.4 %all_gather.3.gathered = bf16[512,256]{1,0:T(8,128)(2,1)} all-gather(bf16[128,256]{1,0:T(8,128)(2,1)S(1)} %constant_dynamic-update-slice_fusion), channel_id=1, replica_groups=mesh['owner'=4,'rows'=8] {'owner'}, dimensions={0}, use_global_device_ids=true | all-gather | bytes 327680 | tf_op jit(solution)/shard_map/all_gather | solution.py:301
  583.2 3.0 join.1
  586.2 5.1 shard_map.88.refs_16_
  591.3 7.3 %shard_map.89.refs_16_ = bf16[16,176,2048]{2,1,0:T(8,128)(2,1)} custom-call(s32[1]{0:T(128)} %bitcast.me_ref, f32[16,352]{1,0:T(8,128)} %get-tuple-element.96.refs_0_, f32[16,352]{1,0:T(8,128)} %copy-done, f32[16,352]{1,0:T(8,128)} %copy-done.1, f32[16,352]{1,0:T(8,128)} %copy-done.2, f32[16,352]{1,0:T(8,128)} %copy-done.3, ...), custom_call_target="tpu_custom_call", output_to_operand_aliasing={{}: (17, {})} | custom-call | flops 54067200 | bytes 7208960 | tf_op jit(solution)/shard_map/pallas_call | solution.py:193
  598.6 10.3 %shard_map.90 = bf16[16,176,2048]{2,1,0:T(8,128)(2,1)} custom-call(s32[1]{0:T(128)} %bitcast.me_ref, f32[16,352]{1,0:T(8,128)} %get-tuple-element.96.refs_0_, f32[16,352]{1,0:T(8,128)} %copy-done, f32[16,352]{1,0:T(8,128)} %copy-done.1, f32[16,352]{1,0:T(8,128)} %copy-done.2, f32[16,352]{1,0:T(8,128)} %copy-done.3, ...), custom_call_target="tpu_custom_call", output_to_operand_aliasing={{}: (17, {})} | custom-call | flops 86507520 | bytes 11534336 | tf_op jit(solution)/shard_map/pallas_call | solution.py:193
  608.9 15.1 %shard_map.91.refs_12_ = bf16[16,176,2048]{2,1,0:T(8,128)(2,1)} custom-call(s32[1]{0:T(128)} %bitcast.me_ref, f32[16,352]{1,0:T(8,128)} %get-tuple-element.96.refs_0_, f32[16,352]{1,0:T(8,128)} %copy-done, f32[16,352]{1,0:T(8,128)} %copy-done.1, f32[16,352]{1,0:T(8,128)} %copy-done.2, f32[16,352]{1,0:T(8,128)} %copy-done.3, f32[16,352]{1,0:T(8,128)} %copy-done.4, ...), custom_call_target="tpu_custom_call" | custom-call | flops 129761280 | bytes 17301504 | tf_op jit(solution)/shard_map/pallas_call | solution.py:193
  624.0 3.5 shard_map.92.refs_12_
  627.6 3.5 shard_map.93
  (157 shorter events, 3.9 us)
Async XLA Ops:
  48.7 13.8 %collective-permute-start = (f32[16,352]{1,0:T(8,128)S(1)}, f32[16,352]{1,0:T(8,128)S(1)}, u32[]{:S(2)}, u32[]{:S(2)}) collective-permute-start(f32[16,352]{1,0:T(8,128)S(1)} %pad_maximum_fusion.1), channel_id=1, source_target_pairs={{0,1},{1,2},{2,3},{3,4},{4,5},{5,6},{6,7},{7,0},{8,9},{9,10},{10,1... | collective-permute-start | bytes 67592 | tf_op jit(solution)/shard_map/ppermute | solution.py:266
  51.8 14.6 %collective-permute-start.1 = (f32[16,352]{1,0:T(8,128)S(1)}, f32[16,352]{1,0:T(8,128)S(1)}, u32[]{:S(2)}, u32[]{:S(2)}) collective-permute-start(f32[16,352]{1,0:T(8,128)S(1)} %pad_maximum_fusion.2), channel_id=1, source_target_pairs={{0,2},{1,3},{2,4},{3,5},{4,6},{5,7},{6,0},{7,1},{8,10},{9,11},{10,... | collective-permute-start | bytes 67592 | tf_op jit(solution)/shard_map/ppermute | solution.py:266
  53.5 17.1 %collective-permute-start.2 = (f32[16,352]{1,0:T(8,128)S(1)}, f32[16,352]{1,0:T(8,128)S(1)}, u32[]{:S(2)}, u32[]{:S(2)}) collective-permute-start(f32[16,352]{1,0:T(8,128)S(1)} %pad_maximum_fusion.3), channel_id=1, source_target_pairs={{0,3},{1,4},{2,5},{3,6},{4,7},{5,0},{6,1},{7,2},{8,11},{9,12},{10,... | collective-permute-start | bytes 67592 | tf_op jit(solution)/shard_map/ppermute | solution.py:266
  56.0 27.6 %collective-permute-start.21 = (bf16[3,176,256]{2,1,0:T(8,128)(2,1)S(1)}, bf16[3,176,256]{2,1,0:T(8,128)(2,1)S(1)}, u32[]{:S(2)}, u32[]{:S(2)}) collective-permute-start(bf16[3,176,256]{2,1,0:T(8,128)(2,1)S(1)} %copy-done.45), channel_id=1, source_target_pairs={{0,1},{1,2},{2,3},{3,4},{4,5},{5,6},{6,7},{7,0},{8,9},{9,10},{10,1... | collective-permute-start | bytes 811016 | tf_op jit(solution)/shard_map/ppermute | solution.py:266
  57.5 4.6 collective-permute-start.42
  62.1 8.5 %collective-permute-start.3 = (f32[16,352]{1,0:T(8,128)S(1)}, f32[16,352]{1,0:T(8,128)S(1)}, u32[]{:S(2)}, u32[]{:S(2)}) collective-permute-start(f32[16,352]{1,0:T(8,128)S(1)} %pad_maximum_fusion.4), channel_id=1, source_target_pairs={{0,4},{1,5},{2,6},{3,7},{4,0},{5,1},{6,2},{7,3},{8,12},{9,13},{10,... | collective-permute-start | bytes 67592 | tf_op jit(solution)/shard_map/ppermute | solution.py:266
  62.6 410.7 %copy-start = (f32[16,352]{1,0:T(8,128)}, f32[16,352]{1,0:T(8,128)S(1)}, u32[]{:S(2)}) copy-start(f32[16,352]{1,0:T(8,128)S(1)} %collective-permute-done.refs_1_) | copy-start | bytes 67588
  62.6 9.0 %collective-permute-start.4 = (f32[16,352]{1,0:T(8,128)S(1)}, f32[16,352]{1,0:T(8,128)S(1)}, u32[]{:S(2)}, u32[]{:S(2)}) collective-permute-start(f32[16,352]{1,0:T(8,128)S(1)} %pad_maximum_fusion.5), channel_id=1, source_target_pairs={{0,5},{1,6},{2,7},{3,0},{4,1},{5,2},{6,3},{7,4},{8,13},{9,14},{10,... | collective-permute-start | bytes 67592 | tf_op jit(solution)/shard_map/ppermute | solution.py:266
  66.5 406.8 %copy-start.1 = (f32[16,352]{1,0:T(8,128)}, f32[16,352]{1,0:T(8,128)S(1)}, u32[]{:S(2)}) copy-start(f32[16,352]{1,0:T(8,128)S(1)} %collective-permute-done.1.refs_2_) | copy-start | bytes 67588
  66.5 6.3 %collective-permute-start.5 = (f32[16,352]{1,0:T(8,128)S(1)}, f32[16,352]{1,0:T(8,128)S(1)}, u32[]{:S(2)}, u32[]{:S(2)}) collective-permute-start(f32[16,352]{1,0:T(8,128)S(1)} %pad_maximum_fusion.6), channel_id=1, source_target_pairs={{0,6},{1,7},{2,0},{3,1},{4,2},{5,3},{6,4},{7,5},{8,14},{9,15},{10,... | collective-permute-start | bytes 67592 | tf_op jit(solution)/shard_map/ppermute | solution.py:266
  70.6 402.6 %copy-start.2 = (f32[16,352]{1,0:T(8,128)}, f32[16,352]{1,0:T(8,128)S(1)}, u32[]{:S(2)}) copy-start(f32[16,352]{1,0:T(8,128)S(1)} %collective-permute-done.2.refs_3_) | copy-start | bytes 67588
  70.6 3.9 collective-permute-start.6
  70.6 402.6 %copy-start.3 = (f32[16,352]{1,0:T(8,128)}, f32[16,352]{1,0:T(8,128)S(1)}, u32[]{:S(2)}) copy-start(f32[16,352]{1,0:T(8,128)S(1)} %collective-permute-done.3.refs_4_) | copy-start | bytes 67588
  70.6 14.7 %collective-permute-start.22 = (bf16[3,176,256]{2,1,0:T(8,128)(2,1)S(1)}, bf16[3,176,256]{2,1,0:T(8,128)(2,1)S(1)}, u32[]{:S(2)}, u32[]{:S(2)}) collective-permute-start(bf16[3,176,256]{2,1,0:T(8,128)(2,1)S(1)} %copy-done.44), channel_id=1, source_target_pairs={{0,2},{1,3},{2,4},{3,5},{4,6},{5,7},{6,0},{7,1},{8,10},{9,11},{10,... | collective-permute-start | bytes 811016 | tf_op jit(solution)/shard_map/ppermute | solution.py:266
  71.6 401.7 %copy-start.4 = (f32[16,352]{1,0:T(8,128)}, f32[16,352]{1,0:T(8,128)S(1)}, u32[]{:S(2)}) copy-start(f32[16,352]{1,0:T(8,128)S(1)} %collective-permute-done.4.refs_5_) | copy-start | bytes 67588
  71.6 8.2 %collective-permute-start.43 = (bf16[32,256]{1,0:T(8,128)(2,1)S(1)}, bf16[32,256]{1,0:T(8,128)(2,1)S(1)}, u32[]{:S(2)}, u32[]{:S(2)}) collective-permute-start(bf16[32,256]{1,0:T(8,128)(2,1)S(1)} %pad_maximum_fusion.8), channel_id=1, source_target_pairs={{0,1},{1,2},{2,3},{3,0},{4,5},{5,6},{6,7},{7,4},{8,9},{9,10},{10,1... | collective-permute-start | bytes 49160 | tf_op jit(solution)/shard_map/ppermute | solution.py:300
  72.8 400.5 %copy-start.5 = (f32[16,352]{1,0:T(8,128)}, f32[16,352]{1,0:T(8,128)S(1)}, u32[]{:S(2)}) copy-start(f32[16,352]{1,0:T(8,128)S(1)} %collective-permute-done.5.refs_6_) | copy-start | bytes 67588
  72.8 8.4 %collective-permute-start.44 = (bf16[32,256]{1,0:T(8,128)(2,1)S(1)}, bf16[32,256]{1,0:T(8,128)(2,1)S(1)}, u32[]{:S(2)}, u32[]{:S(2)}) collective-permute-start(bf16[32,256]{1,0:T(8,128)(2,1)S(1)} %pad_maximum_fusion.8), channel_id=1, source_target_pairs={{0,2},{1,3},{2,0},{3,1},{4,6},{5,7},{6,4},{7,5},{8,10},{9,11},{10,... | collective-permute-start | bytes 49160 | tf_op jit(solution)/shard_map/ppermute | solution.py:300
  74.5 398.8 %copy-start.6 = (f32[16,352]{1,0:T(8,128)}, f32[16,352]{1,0:T(8,128)S(1)}, u32[]{:S(2)}) copy-start(f32[16,352]{1,0:T(8,128)S(1)} %collective-permute-done.6.refs_7_) | copy-start | bytes 67588
  74.5 9.1 %collective-permute-start.45 = (bf16[32,256]{1,0:T(8,128)(2,1)S(1)}, bf16[32,256]{1,0:T(8,128)(2,1)S(1)}, u32[]{:S(2)}, u32[]{:S(2)}) collective-permute-start(bf16[32,256]{1,0:T(8,128)(2,1)S(1)} %pad_maximum_fusion.8), channel_id=1, source_target_pairs={{0,3},{1,0},{2,1},{3,2},{4,7},{5,4},{6,5},{7,6},{8,11},{9,8},{10,9... | collective-permute-start | bytes 49160 | tf_op jit(solution)/shard_map/ppermute | solution.py:300
  79.8 13.4 %collective-permute-start.23 = (bf16[3,176,256]{2,1,0:T(8,128)(2,1)S(1)}, bf16[3,176,256]{2,1,0:T(8,128)(2,1)S(1)}, u32[]{:S(2)}, u32[]{:S(2)}) collective-permute-start(bf16[3,176,256]{2,1,0:T(8,128)(2,1)S(1)} %copy-done.43), channel_id=1, source_target_pairs={{0,3},{1,4},{2,5},{3,6},{4,7},{5,0},{6,1},{7,2},{8,11},{9,12},{10,... | collective-permute-start | bytes 811016 | tf_op jit(solution)/shard_map/ppermute | solution.py:266
  81.2 13.3 %collective-permute-start.25 = (bf16[3,176,256]{2,1,0:T(8,128)(2,1)S(1)}, bf16[3,176,256]{2,1,0:T(8,128)(2,1)S(1)}, u32[]{:S(2)}, u32[]{:S(2)}) collective-permute-start(bf16[3,176,256]{2,1,0:T(8,128)(2,1)S(1)} %copy-done.42), channel_id=1, source_target_pairs={{0,5},{1,6},{2,7},{3,0},{4,1},{5,2},{6,3},{7,4},{8,13},{9,14},{10,... | collective-permute-start | bytes 811016 | tf_op jit(solution)/shard_map/ppermute | solution.py:266
  83.6 24.8 %collective-permute-start.26 = (bf16[3,176,256]{2,1,0:T(8,128)(2,1)}, bf16[3,176,256]{2,1,0:T(8,128)(2,1)S(1)}, u32[]{:S(2)}, u32[]{:S(2)}) collective-permute-start(bf16[3,176,256]{2,1,0:T(8,128)(2,1)} %get-tuple-element.75), channel_id=1, source_target_pairs={{0,6},{1,7},{2,0},{3,1},{4,2},{5,3},{6,4},{7,5},{8,14},{9,15},{10,... | collective-permute-start | bytes 811016 | tf_op jit(solution)/shard_map/ppermute | solution.py:266
  83.6 43.8 %collective-permute-start.27 = (bf16[3,176,256]{2,1,0:T(8,128)(2,1)}, bf16[3,176,256]{2,1,0:T(8,128)(2,1)S(1)}, u32[]{:S(2)}, u32[]{:S(2)}) collective-permute-start(bf16[3,176,256]{2,1,0:T(8,128)(2,1)} %get-tuple-element.76), channel_id=1, source_target_pairs={{0,7},{1,0},{2,1},{3,2},{4,3},{5,4},{6,5},{7,6},{8,15},{9,8},{10,9... | collective-permute-start | bytes 811016 | tf_op jit(solution)/shard_map/ppermute | solution.py:266
  85.3 103.2 %collective-permute-start.14 = (bf16[5,176,256]{2,1,0:T(8,128)(2,1)}, bf16[5,176,256]{2,1,0:T(8,128)(2,1)S(1)}, u32[]{:S(2)}, u32[]{:S(2)}) collective-permute-start(bf16[5,176,256]{2,1,0:T(8,128)(2,1)} %get-tuple-element.63), channel_id=1, source_target_pairs={{0,1},{1,2},{2,3},{3,4},{4,5},{5,6},{6,7},{7,0},{8,9},{9,10},{10,1... | collective-permute-start | bytes 1351688 | tf_op jit(solution)/shard_map/ppermute | solution.py:266
  93.1 62.4 %collective-permute-start.32 = (bf16[4,176,256]{2,1,0:T(8,128)(2,1)}, bf16[4,176,256]{2,1,0:T(8,128)(2,1)S(1)}, u32[]{:S(2)}, u32[]{:S(2)}) collective-permute-start(bf16[4,176,256]{2,1,0:T(8,128)(2,1)} %get-tuple-element.82), channel_id=1, source_target_pairs={{0,4},{1,5},{2,6},{3,7},{4,0},{5,1},{6,2},{7,3},{8,12},{9,13},{10,... | collective-permute-start | bytes 1081352 | tf_op jit(solution)/shard_map/ppermute | solution.py:266
  95.2 230.6 %copy-start.40 = (bf16[8,176,256]{2,1,0:T(8,128)(2,1)S(1)}, bf16[8,176,256]{2,1,0:T(8,128)(2,1)}, u32[]{:S(2)}) copy-start(bf16[8,176,256]{2,1,0:T(8,128)(2,1)} %get-tuple-element.55) | copy-start | bytes 2162692
  95.2 85.3 %collective-permute-start.33 = (bf16[4,176,256]{2,1,0:T(8,128)(2,1)S(1)}, bf16[4,176,256]{2,1,0:T(8,128)(2,1)S(1)}, u32[]{:S(2)}, u32[]{:S(2)}) collective-permute-start(bf16[4,176,256]{2,1,0:T(8,128)(2,1)S(1)} %copy-done.41), channel_id=1, source_target_pairs={{0,3},{1,4},{2,5},{3,6},{4,7},{5,0},{6,1},{7,2},{8,11},{9,12},{10,... | collective-permute-start | bytes 1081352 | tf_op jit(solution)/shard_map/ppermute | solution.py:266
  108.4 199.9 %copy-start.30 = (bf16[3,176,256]{2,1,0:T(8,128)(2,1)}, bf16[3,176,256]{2,1,0:T(8,128)(2,1)S(1)}, u32[]{:S(2)}) copy-start(bf16[3,176,256]{2,1,0:T(8,128)(2,1)S(1)} %collective-permute-done.26.refs_14_) | copy-start | bytes 811012
  108.4 44.6 %collective-permute-start.24 = (bf16[3,176,256]{2,1,0:T(8,128)(2,1)}, bf16[3,176,256]{2,1,0:T(8,128)(2,1)S(1)}, u32[]{:S(2)}, u32[]{:S(2)}) collective-permute-start(bf16[3,176,256]{2,1,0:T(8,128)(2,1)} %lead.1), channel_id=1, source_target_pairs={{0,4},{1,5},{2,6},{3,7},{4,0},{5,1},{6,2},{7,3},{8,12},{9,13},{10,... | collective-permute-start | bytes 811016 | tf_op jit(solution)/shard_map/ppermute | solution.py:266
  127.4 180.9 %copy-start.31 = (bf16[3,176,256]{2,1,0:T(8,128)(2,1)}, bf16[3,176,256]{2,1,0:T(8,128)(2,1)S(1)}, u32[]{:S(2)}) copy-start(bf16[3,176,256]{2,1,0:T(8,128)(2,1)S(1)} %collective-permute-done.27.refs_15_) | copy-start | bytes 811012
  127.4 62.0 %collective-permute-start.15 = (bf16[5,176,256]{2,1,0:T(8,128)(2,1)}, bf16[5,176,256]{2,1,0:T(8,128)(2,1)S(1)}, u32[]{:S(2)}, u32[]{:S(2)}) collective-permute-start(bf16[5,176,256]{2,1,0:T(8,128)(2,1)} %get-tuple-element.64), channel_id=1, source_target_pairs={{0,2},{1,3},{2,4},{3,5},{4,6},{5,7},{6,0},{7,1},{8,10},{9,11},{10,... | collective-permute-start | bytes 1351688 | tf_op jit(solution)/shard_map/ppermute | solution.py:266
  153.0 44.3 %collective-permute-start.16 = (bf16[5,176,256]{2,1,0:T(8,128)(2,1)}, bf16[5,176,256]{2,1,0:T(8,128)(2,1)S(1)}, u32[]{:S(2)}, u32[]{:S(2)}) collective-permute-start(bf16[5,176,256]{2,1,0:T(8,128)(2,1)} %get-tuple-element.65), channel_id=1, source_target_pairs={{0,3},{1,4},{2,5},{3,6},{4,7},{5,0},{6,1},{7,2},{8,11},{9,12},{10,... | collective-permute-start | bytes 1351688 | tf_op jit(solution)/shard_map/ppermute | solution.py:266
  155.5 152.2 %copy-start.24 = (bf16[4,176,256]{2,1,0:T(8,128)(2,1)}, bf16[4,176,256]{2,1,0:T(8,128)(2,1)S(1)}, u32[]{:S(2)}) copy-start(bf16[4,176,256]{2,1,0:T(8,128)(2,1)S(1)} %collective-permute-done.32.refs_9_) | copy-start | bytes 1081348
  155.5 41.8 %collective-permute-start.17 = (bf16[5,176,256]{2,1,0:T(8,128)(2,1)}, bf16[5,176,256]{2,1,0:T(8,128)(2,1)S(1)}, u32[]{:S(2)}, u32[]{:S(2)}) collective-permute-start(bf16[5,176,256]{2,1,0:T(8,128)(2,1)} %get-tuple-element.66), channel_id=1, source_target_pairs={{0,4},{1,5},{2,6},{3,7},{4,0},{5,1},{6,2},{7,3},{8,12},{9,13},{10,... | collective-permute-start | bytes 1351688 | tf_op jit(solution)/shard_map/ppermute | solution.py:266
  180.5 127.2 %copy-start.25 = (bf16[4,176,256]{2,1,0:T(8,128)(2,1)}, bf16[4,176,256]{2,1,0:T(8,128)(2,1)S(1)}, u32[]{:S(2)}) copy-start(bf16[4,176,256]{2,1,0:T(8,128)(2,1)S(1)} %collective-permute-done.33.refs_10_) | copy-start | bytes 1081348
  180.5 76.1 %collective-permute-start.18 = (bf16[5,176,256]{2,1,0:T(8,128)(2,1)}, bf16[5,176,256]{2,1,0:T(8,128)(2,1)S(1)}, u32[]{:S(2)}, u32[]{:S(2)}) collective-permute-start(bf16[5,176,256]{2,1,0:T(8,128)(2,1)} %get-tuple-element.67), channel_id=1, source_target_pairs={{0,5},{1,6},{2,7},{3,0},{4,1},{5,2},{6,3},{7,4},{8,13},{9,14},{10,... | collective-permute-start | bytes 1351688 | tf_op jit(solution)/shard_map/ppermute | solution.py:266
  188.5 119.2 %copy-start.17 = (bf16[5,176,256]{2,1,0:T(8,128)(2,1)}, bf16[5,176,256]{2,1,0:T(8,128)(2,1)S(1)}, u32[]{:S(2)}) copy-start(bf16[5,176,256]{2,1,0:T(8,128)(2,1)S(1)} %collective-permute-done.14.refs_9_) | copy-start | bytes 1351684
  188.5 93.2 %collective-permute-start.19 = (bf16[5,176,256]{2,1,0:T(8,128)(2,1)}, bf16[5,176,256]{2,1,0:T(8,128)(2,1)S(1)}, u32[]{:S(2)}, u32[]{:S(2)}) collective-permute-start(bf16[5,176,256]{2,1,0:T(8,128)(2,1)} %get-tuple-element.68), channel_id=1, source_target_pairs={{0,6},{1,7},{2,0},{3,1},{4,2},{5,3},{6,4},{7,5},{8,14},{9,15},{10,... | collective-permute-start | bytes 1351688 | tf_op jit(solution)/shard_map/ppermute | solution.py:266
  190.2 118.1 %collective-permute-start.10 = (bf16[8,176,256]{2,1,0:T(8,128)(2,1)}, bf16[8,176,256]{2,1,0:T(8,128)(2,1)S(1)}, u32[]{:S(2)}, u32[]{:S(2)}) collective-permute-start(bf16[8,176,256]{2,1,0:T(8,128)(2,1)} %get-tuple-element.58), channel_id=1, source_target_pairs={{0,4},{1,5},{2,6},{3,7},{4,0},{5,1},{6,2},{7,3},{8,12},{9,13},{10,... | collective-permute-start | bytes 2162696 | tf_op jit(solution)/shard_map/ppermute | solution.py:266
  197.3 110.4 %collective-permute-start.20 = (bf16[5,176,256]{2,1,0:T(8,128)(2,1)}, bf16[5,176,256]{2,1,0:T(8,128)(2,1)S(1)}, u32[]{:S(2)}, u32[]{:S(2)}) collective-permute-start(bf16[5,176,256]{2,1,0:T(8,128)(2,1)} %get-tuple-element.69), channel_id=1, source_target_pairs={{0,7},{1,0},{2,1},{3,2},{4,3},{5,4},{6,5},{7,6},{8,15},{9,8},{10,9... | collective-permute-start | bytes 1351688 | tf_op jit(solution)/shard_map/ppermute | solution.py:266
  198.8 126.9 %collective-permute-start.11 = (bf16[8,176,256]{2,1,0:T(8,128)(2,1)}, bf16[8,176,256]{2,1,0:T(8,128)(2,1)S(1)}, u32[]{:S(2)}, u32[]{:S(2)}) collective-permute-start(bf16[8,176,256]{2,1,0:T(8,128)(2,1)} %get-tuple-element.59), channel_id=1, source_target_pairs={{0,5},{1,6},{2,7},{3,0},{4,1},{5,2},{6,3},{7,4},{8,13},{9,14},{10,... | collective-permute-start | bytes 2162696 | tf_op jit(solution)/shard_map/ppermute | solution.py:266
  257.3 101.3 %collective-permute-start.12 = (bf16[8,176,256]{2,1,0:T(8,128)(2,1)}, bf16[8,176,256]{2,1,0:T(8,128)(2,1)S(1)}, u32[]{:S(2)}, u32[]{:S(2)}) collective-permute-start(bf16[8,176,256]{2,1,0:T(8,128)(2,1)} %get-tuple-element.60), channel_id=1, source_target_pairs={{0,6},{1,7},{2,0},{3,1},{4,2},{5,3},{6,4},{7,5},{8,14},{9,15},{10,... | collective-permute-start | bytes 2162696 | tf_op jit(solution)/shard_map/ppermute | solution.py:266
  282.4 79.3 %collective-permute-start.13 = (bf16[8,176,256]{2,1,0:T(8,128)(2,1)}, bf16[8,176,256]{2,1,0:T(8,128)(2,1)S(1)}, u32[]{:S(2)}, u32[]{:S(2)}) collective-permute-start(bf16[8,176,256]{2,1,0:T(8,128)(2,1)} %get-tuple-element.61), channel_id=1, source_target_pairs={{0,7},{1,0},{2,1},{3,2},{4,3},{5,4},{6,5},{7,6},{8,15},{9,8},{10,9... | collective-permute-start | bytes 2162696 | tf_op jit(solution)/shard_map/ppermute | solution.py:266
  307.7 147.3 %collective-permute-start.35 = (bf16[12,176,256]{2,1,0:T(8,128)(2,1)}, bf16[12,176,256]{2,1,0:T(8,128)(2,1)S(1)}, u32[]{:S(2)}, u32[]{:S(2)}) collective-permute-start(bf16[12,176,256]{2,1,0:T(8,128)(2,1)} %get-tuple-element.86), channel_id=1, source_target_pairs={{0,1},{1,2},{2,3},{3,4},{4,5},{5,6},{6,7},{7,0},{8,9},{9,10},{10,1... | collective-permute-start | bytes 3244040 | tf_op jit(solution)/shard_map/ppermute | solution.py:266
  308.4 164.7 %copy-start.10 = (bf16[8,176,256]{2,1,0:T(8,128)(2,1)}, bf16[8,176,256]{2,1,0:T(8,128)(2,1)S(1)}, u32[]{:S(2)}) copy-start(bf16[8,176,256]{2,1,0:T(8,128)(2,1)S(1)} %collective-permute-done.10.refs_12_) | copy-start | bytes 2162692
  308.4 164.7 %collective-permute-start.36 = (bf16[12,176,256]{2,1,0:T(8,128)(2,1)}, bf16[12,176,256]{2,1,0:T(8,128)(2,1)S(1)}, u32[]{:S(2)}, u32[]{:S(2)}) collective-permute-start(bf16[12,176,256]{2,1,0:T(8,128)(2,1)} %get-tuple-element.87), channel_id=1, source_target_pairs={{0,2},{1,3},{2,4},{3,5},{4,6},{5,7},{6,0},{7,1},{8,10},{9,11},{10,... | collective-permute-start | bytes 3244040 | tf_op jit(solution)/shard_map/ppermute | solution.py:266
  325.8 147.3 %copy-start.11 = (bf16[8,176,256]{2,1,0:T(8,128)(2,1)}, bf16[8,176,256]{2,1,0:T(8,128)(2,1)S(1)}, u32[]{:S(2)}) copy-start(bf16[8,176,256]{2,1,0:T(8,128)(2,1)S(1)} %collective-permute-done.11.refs_13_) | copy-start | bytes 2162692
  325.8 66.9 %collective-permute-start.7 = (bf16[8,176,256]{2,1,0:T(8,128)(2,1)S(1)}, bf16[8,176,256]{2,1,0:T(8,128)(2,1)S(1)}, u32[]{:S(2)}, u32[]{:S(2)}) collective-permute-start(bf16[8,176,256]{2,1,0:T(8,128)(2,1)S(1)} %copy-done.40), channel_id=1, source_target_pairs={{0,1},{1,2},{2,3},{3,4},{4,5},{5,6},{6,7},{7,0},{8,9},{9,10},{10,1... | collective-permute-start | bytes 2162696 | tf_op jit(solution)/shard_map/ppermute | solution.py:266
  358.6 114.6 %copy-start.12 = (bf16[8,176,256]{2,1,0:T(8,128)(2,1)}, bf16[8,176,256]{2,1,0:T(8,128)(2,1)S(1)}, u32[]{:S(2)}) copy-start(bf16[8,176,256]{2,1,0:T(8,128)(2,1)S(1)} %collective-permute-done.12.refs_14_) | copy-start | bytes 2162692
  358.6 34.2 %collective-permute-start.8 = (bf16[8,176,256]{2,1,0:T(8,128)(2,1)}, bf16[8,176,256]{2,1,0:T(8,128)(2,1)S(1)}, u32[]{:S(2)}, u32[]{:S(2)}) collective-permute-start(bf16[8,176,256]{2,1,0:T(8,128)(2,1)} %get-tuple-element.56), channel_id=1, source_target_pairs={{0,2},{1,3},{2,4},{3,5},{4,6},{5,7},{6,0},{7,1},{8,10},{9,11},{10,... | collective-permute-start | bytes 2162696 | tf_op jit(solution)/shard_map/ppermute | solution.py:266
  361.7 93.3 %collective-permute-start.9 = (bf16[8,176,256]{2,1,0:T(8,128)(2,1)}, bf16[8,176,256]{2,1,0:T(8,128)(2,1)S(1)}, u32[]{:S(2)}, u32[]{:S(2)}) collective-permute-start(bf16[8,176,256]{2,1,0:T(8,128)(2,1)} %get-tuple-element.57), channel_id=1, source_target_pairs={{0,3},{1,4},{2,5},{3,6},{4,7},{5,0},{6,1},{7,2},{8,11},{9,12},{10,... | collective-permute-start | bytes 2162696 | tf_op jit(solution)/shard_map/ppermute | solution.py:266
  392.7 85.6 %collective-permute-start.37 = (bf16[12,176,256]{2,1,0:T(8,128)(2,1)}, bf16[12,176,256]{2,1,0:T(8,128)(2,1)S(1)}, u32[]{:S(2)}, u32[]{:S(2)}) collective-permute-start(bf16[12,176,256]{2,1,0:T(8,128)(2,1)} %get-tuple-element.88), channel_id=1, source_target_pairs={{0,3},{1,4},{2,5},{3,6},{4,7},{5,0},{6,1},{7,2},{8,11},{9,12},{10,... | collective-permute-start | bytes 3244040 | tf_op jit(solution)/shard_map/ppermute | solution.py:266
  392.8 85.5 %collective-permute-start.38 = (bf16[12,176,256]{2,1,0:T(8,128)(2,1)}, bf16[12,176,256]{2,1,0:T(8,128)(2,1)}, u32[]{:S(2)}, u32[]{:S(2)}) collective-permute-start(bf16[12,176,256]{2,1,0:T(8,128)(2,1)} %get-tuple-element.89), channel_id=1, source_target_pairs={{0,4},{1,5},{2,6},{3,7},{4,0},{5,1},{6,2},{7,3},{8,12},{9,13},{10,... | collective-permute-start | bytes 3244040 | tf_op jit(solution)/shard_map/ppermute | solution.py:266
  455.0 85.8 %collective-permute-start.39 = (bf16[12,176,256]{2,1,0:T(8,128)(2,1)}, bf16[12,176,256]{2,1,0:T(8,128)(2,1)}, u32[]{:S(2)}, u32[]{:S(2)}) collective-permute-start(bf16[12,176,256]{2,1,0:T(8,128)(2,1)} %get-tuple-element.90), channel_id=1, source_target_pairs={{0,5},{1,6},{2,7},{3,0},{4,1},{5,2},{6,3},{7,4},{8,13},{9,14},{10,... | collective-permute-start | bytes 3244040 | tf_op jit(solution)/shard_map/ppermute | solution.py:266
  455.0 136.3 %copy-start.7 = (bf16[12,176,256]{2,1,0:T(8,128)(2,1)}, bf16[12,176,256]{2,1,0:T(8,128)(2,1)S(1)}, u32[]{:S(2)}) copy-start(bf16[12,176,256]{2,1,0:T(8,128)(2,1)S(1)} %collective-permute-done.35.refs_9_) | copy-start | bytes 3244036
  455.0 88.6 %collective-permute-start.40 = (bf16[12,176,256]{2,1,0:T(8,128)(2,1)}, bf16[12,176,256]{2,1,0:T(8,128)(2,1)}, u32[]{:S(2)}, u32[]{:S(2)}) collective-permute-start(bf16[12,176,256]{2,1,0:T(8,128)(2,1)} %get-tuple-element.91), channel_id=1, source_target_pairs={{0,6},{1,7},{2,0},{3,1},{4,2},{5,3},{6,4},{7,5},{8,14},{9,15},{10,... | collective-permute-start | bytes 3244040 | tf_op jit(solution)/shard_map/ppermute | solution.py:266
  473.1 118.2 %copy-start.8 = (bf16[12,176,256]{2,1,0:T(8,128)(2,1)}, bf16[12,176,256]{2,1,0:T(8,128)(2,1)S(1)}, u32[]{:S(2)}) copy-start(bf16[12,176,256]{2,1,0:T(8,128)(2,1)S(1)} %collective-permute-done.36.refs_10_) | copy-start | bytes 3244036
  473.1 103.0 %collective-permute-start.41 = (bf16[12,176,256]{2,1,0:T(8,128)(2,1)}, bf16[12,176,256]{2,1,0:T(8,128)(2,1)}, u32[]{:S(2)}, u32[]{:S(2)}) collective-permute-start(bf16[12,176,256]{2,1,0:T(8,128)(2,1)} %get-tuple-element.92), channel_id=1, source_target_pairs={{0,7},{1,0},{2,1},{3,2},{4,3},{5,4},{6,5},{7,6},{8,15},{9,8},{10,9... | collective-permute-start | bytes 3244040 | tf_op jit(solution)/shard_map/ppermute | solution.py:266
  478.3 145.7 %collective-permute-start.34 = (bf16[4,176,256]{2,1,0:T(8,128)(2,1)}, bf16[4,176,256]{2,1,0:T(8,128)(2,1)}, u32[]{:S(2)}, u32[]{:S(2)}) collective-permute-start(bf16[4,176,256]{2,1,0:T(8,128)(2,1)} %get-tuple-element.84), channel_id=1, source_target_pairs={{0,5},{1,6},{2,7},{3,0},{4,1},{5,2},{6,3},{7,4},{8,13},{9,14},{10,... | collective-permute-start | bytes 1081352 | tf_op jit(solution)/shard_map/ppermute | solution.py:266
  478.3 149.2 %collective-permute-start.28 = (bf16[4,176,256]{2,1,0:T(8,128)(2,1)}, bf16[4,176,256]{2,1,0:T(8,128)(2,1)}, u32[]{:S(2)}, u32[]{:S(2)}) collective-permute-start(bf16[4,176,256]{2,1,0:T(8,128)(2,1)} %get-tuple-element.77), channel_id=1, source_target_pairs={{0,2},{1,3},{2,4},{3,5},{4,6},{5,7},{6,0},{7,1},{8,10},{9,11},{10,... | collective-permute-start | bytes 1081352 | tf_op jit(solution)/shard_map/ppermute | solution.py:266
  540.8 86.7 %collective-permute-start.29 = (bf16[4,176,256]{2,1,0:T(8,128)(2,1)}, bf16[4,176,256]{2,1,0:T(8,128)(2,1)}, u32[]{:S(2)}, u32[]{:S(2)}) collective-permute-start(bf16[4,176,256]{2,1,0:T(8,128)(2,1)} %get-tuple-element.78), channel_id=1, source_target_pairs={{0,6},{1,7},{2,0},{3,1},{4,2},{5,3},{6,4},{7,5},{8,14},{9,15},{10,... | collective-permute-start | bytes 1081352 | tf_op jit(solution)/shard_map/ppermute | solution.py:266
  543.7 83.9 %collective-permute-start.30 = (bf16[4,176,256]{2,1,0:T(8,128)(2,1)}, bf16[4,176,256]{2,1,0:T(8,128)(2,1)}, u32[]{:S(2)}, u32[]{:S(2)}) collective-permute-start(bf16[4,176,256]{2,1,0:T(8,128)(2,1)} %get-tuple-element.79), channel_id=1, source_target_pairs={{0,1},{1,2},{2,3},{3,4},{4,5},{5,6},{6,7},{7,0},{8,9},{9,10},{10,1... | collective-permute-start | bytes 1081352 | tf_op jit(solution)/shard_map/ppermute | solution.py:266
  576.1 51.5 %collective-permute-start.31 = (bf16[4,176,256]{2,1,0:T(8,128)(2,1)}, bf16[4,176,256]{2,1,0:T(8,128)(2,1)}, u32[]{:S(2)}, u32[]{:S(2)}) collective-permute-start(bf16[4,176,256]{2,1,0:T(8,128)(2,1)} %get-tuple-element.80), channel_id=1, source_target_pairs={{0,7},{1,0},{2,1},{3,2},{4,3},{5,4},{6,5},{7,6},{8,15},{9,8},{10,9... | collective-permute-start | bytes 1081352 | tf_op jit(solution)/shard_map/ppermute | solution.py:266
  (28 other events, 675.2 us)
